TPU v7x, 32 devices: a whole 2x2x4 slice. The times are simulated.
32 devices in a mesh: section: 4 (over y, x), pix: 8 (over z, core).
Axes of the slice: x: 2, y: 2, z: 4, core: 2. Of those that a mesh axis runs over, the one named last changes fastest.
Arguments:
- slc: float32 [2, 200, 2048], P(None, 'section', 'pix'), may hold values from -6 to 6
- neighbours: int32 [15, 2048], P(None, 'pix'), may hold values from 0 to 2047, as said below
- reference_pixel: int32 [1], replicated, may hold values from 0 to 2047
Outputs:
- phases: float32 [2, 200, 2048], P(None, 'section', 'pix')
- compressed: float32 [2, 4, 2048], P(None, 'section', 'pix')
Inputs may be any that keep to these rules, and one draw needn't show every extreme that they name: neighbours[0, p] = p; every entry lies within 256 of its column's pixel p, and that distance is reached.
All inputs are finite; a program needn't handle non-finite values.
Results may differ from a plain program's by a relative error of at most 0.0003.
Values sent between devices are 32-bit elements; how exact they have to be, the bound alone decides.
No kernel may reach another device: no remote copies, remote signals or barrier semaphores. Data moves between devices by JAX's collectives and lax.ppermute only.
A program may use at most 64 MiB of HBM per device.

v0:
```python
import math

import jax
import jax.numpy as jnp
from jax import lax
from jax.sharding import PartitionSpec as P

ITERS = 16


FLOOR = 0.05
REACH_LIMIT = 256


def extended_2(block, sides, width):
    for axis, dim in sides:
        count = lax.axis_size(axis)
        forward = [(i, i + 1) for i in range(count - 1)]
        backward = [(target, source) for source, target in forward]
        low = lax.ppermute(
            lax.slice_in_dim(block, block.shape[dim] - width, None, axis=dim), axis, forward
        )
        high = lax.ppermute(lax.slice_in_dim(block, 0, width, axis=dim), axis, backward)
        block = jnp.concatenate([low, block, high], axis=dim)
    return block


def spread(array, axis, root):
    mine = lax.axis_index(axis) == root
    return lax.psum(jnp.where(mine, array, jnp.zeros_like(array)), axis)


def unit(real, imag):
    scale = 1.0 / jnp.maximum(jnp.sqrt(real * real + imag * imag), FLOOR)
    return (real * scale, imag * scale)


def solve_block(ext_re, ext_im, index, own_re, own_im, iters):
    near_re = ext_re[:, index]
    near_im = ext_im[:, index]
    power = jnp.sum(near_re * near_re + near_im * near_im, axis=1)
    scale = 1.0 / jnp.sqrt(jnp.maximum(power, 1.0))
    z_re = near_re * scale[:, None, :]
    z_im = near_im * scale[:, None, :]
    count = own_re.shape[0]
    start_re = jnp.full(own_re.shape, 1.0 / math.sqrt(count), jnp.float32)
    start_im = jnp.zeros(own_re.shape, jnp.float32)

    def turn(step, carry):
        vec_re, vec_im = carry
        c_re = jnp.sum(z_re * vec_re[:, None, :] + z_im * vec_im[:, None, :], axis=0)
        c_im = jnp.sum(z_re * vec_im[:, None, :] - z_im * vec_re[:, None, :], axis=0)
        u_re = vec_re + jnp.sum(z_re * c_re[None] - z_im * c_im[None], axis=1)
        u_im = vec_im + jnp.sum(z_re * c_im[None] + z_im * c_re[None], axis=1)
        norm = jnp.sqrt(jnp.sum(u_re * u_re + u_im * u_im, axis=0))
        return (u_re / norm, u_im / norm)

    vec_re, vec_im = lax.fori_loop(0, iters, turn, (start_re, start_im))
    comp_re = jnp.sum(vec_re * own_re + vec_im * own_im, axis=0)
    comp_im = jnp.sum(vec_re * own_im - vec_im * own_re, axis=0)
    return (vec_re, vec_im, comp_re, comp_im)


def solve_section(extended, stack, local_index):
    vec_re, vec_im, comp_re, comp_im = solve_block(
        extended[0], extended[1], local_index, stack[0], stack[1], ITERS
    )
    return (jnp.stack([vec_re, vec_im]), jnp.stack([comp_re, comp_im]))


def on_device(slc, neighbours, reference_pixel):
    dates = slc.shape[1]
    pixels = slc.shape[2]
    reach = min(pixels, REACH_LIMIT)
    sections = lax.axis_size("section")
    me_section = lax.axis_index("section")
    me_pix = lax.axis_index("pix")
    local_index = neighbours - (me_pix * pixels - reach)
    quarter = pixels // sections
    begin = me_section * quarter
    whole = lax.all_gather(slc, "section", axis=1, tiled=True)
    dates_all = extended_2(whole, (("pix", 2),), reach)
    own_all = lax.dynamic_slice_in_dim(whole, begin, quarter, 2)
    quarter_index = lax.dynamic_slice_in_dim(local_index, begin, quarter, 1)
    virtual_part = jnp.zeros((2, quarter), jnp.float32)
    vectors = []
    comps = []
    for rnd in range(sections):
        if rnd == 0:
            virtual_ext = jnp.zeros((2, pixels + 2 * reach), jnp.float32)
        else:
            block_virtual = lax.all_gather(virtual_part, "section", axis=1, tiled=True)
            virtual_ext = extended_2(block_virtual, (("pix", 1),), reach)
        extended = jnp.concatenate(
            [virtual_ext[:, None, :], dates_all[:, rnd * dates : (rnd + 1) * dates]], axis=1
        )
        stack = jnp.concatenate(
            [virtual_part[:, None, :], own_all[:, rnd * dates : (rnd + 1) * dates]], axis=1
        )
        vec_part, virtual_part = solve_section(extended, stack, quarter_index)
        vectors.append(vec_part)
        comps.append(virtual_part)
    datum_re = jnp.ones((quarter,), jnp.float32)
    datum_im = jnp.zeros((quarter,), jnp.float32)
    pieces = [None] * sections
    for rnd in range(sections - 1, -1, -1):
        vec_part = vectors[rnd]
        p_re = vec_part[0, 1:] * datum_re - vec_part[1, 1:] * datum_im
        p_im = vec_part[0, 1:] * datum_im + vec_part[1, 1:] * datum_re
        pieces[rnd] = jnp.stack([p_re, p_im])
        g_re, g_im = unit(vec_part[0, 0], vec_part[1, 0])
        datum_re, datum_im = (datum_re * g_re - datum_im * g_im, datum_re * g_im + datum_im * g_re)
    series_part = jnp.concatenate(pieces, axis=1)
    comp_part = jnp.stack(comps, axis=1)
    moved_series, moved_comp = (
        lax.all_to_all(series_part, "section", split_axis=1, concat_axis=2, tiled=True),
        lax.all_to_all(comp_part, "section", split_axis=1, concat_axis=2, tiled=True),
    )
    s_re = moved_series[0]
    s_im = moved_series[1]
    root = reference_pixel[0] // pixels
    column = reference_pixel[0] - root * pixels
    mine = jnp.stack(
        [
            lax.dynamic_index_in_dim(s_re, column, 1, False),
            lax.dynamic_index_in_dim(s_im, column, 1, False),
        ]
    )
    ref_series = spread(mine, "pix", root)
    u_re, u_im = unit(ref_series[0], ref_series[1])
    gain = math.sqrt(dates + 1)
    out_re = gain * (s_re * u_re[:, None] + s_im * u_im[:, None])
    out_im = gain * (s_im * u_re[:, None] - s_re * u_im[:, None])
    return (jnp.stack([out_re, out_im]), moved_comp)


def solution(mesh):
    return jax.shard_map(
        on_device,
        mesh=mesh,
        in_specs=(P(None, "section", "pix"), P(None, "pix"), P()),
        out_specs=(P(None, "section", "pix"), P(None, "section", "pix")),
        check_vma=False,
    )
```

profile of v0, /device:TPU:0, one launch (start us, length us, event | category | flops | bytes accessed | tf_op | source)
XLA Modules:
  0.0 171.6 jit_solution(18223872976591722680)
XLA Ops:
  0.6 11.5 %all_gather.12 = f32[2,200,256]{2,0,1:T(2,128)S(1)} all-gather(f32[2,50,256]{2,0,1:T(2,128)} %param.11), channel_id=1, replica_groups=mesh['section'=4,'pix'=8] {'section'}, dimensions={1}, use_global_device_ids=true | all-gather | bytes 512000 | tf_op jit(solution)/shard_map/all_gather | solution.py:81
  12.3 1.3 collective-permute-start
  13.7 1.3 collective-permute-start.1
  15.0 0.8 compare_select_fusion
  15.9 0.9 constant_dynamic-slice_fusion.3
  16.8 0.7 pad_slice_fusion.14
  17.5 1.8 %collective-permute-done.1 = f32[2,200,256]{1,2,0:T(8,128)S(1)} collective-permute-done((f32[2,200,256]{1,2,0:T(8,128)S(1)}, f32[2,200,256]{1,2,0:T(8,128)S(1)}, u32[]{:S(2)}, u32[]{:S(2)}) %collective-permute-start.1) | collective-permute-done | bytes 409632 | tf_op jit(solution)/shard_map/ppermute | solution.py:23
  19.3 1.5 fusion.52
  21.1 2.9 %gather_fusion = f32[960,51]{1,0:T(8,128)S(1)} fusion(f32[51,768]{0,1:T(8,128)S(1)} %get-tuple-element.315, s32[1024]{0:T(1024)S(1)} %pad_clamp_fusion), kind=kCustom, calls=%fused_computation | custom fusion | bytes 395520 | tf_op jit(solution)/shard_map/gather | solution.py:39
  24.3 4.0 %gather_fusion.1 = f32[960,51]{1,0:T(8,128)} fusion(f32[51,768]{0,1:T(8,128)S(1)} %get-tuple-element.314, s32[1024]{0:T(1024)S(1)} %pad_clamp_fusion), kind=kCustom, calls=%fused_computation.1 | custom fusion | bytes 395520 | tf_op jit(solution)/shard_map/gather | solution.py:40
  28.3 1.3 copy.195
  29.9 8.8 %while.52 = (s32[]{:T(128)}, f32[51,64]{1,0:T(8,128)S(1)}, f32[51,64]{1,0:T(8,128)S(1)}, f32[51,15,64]{2,1,0:T(8,128)S(1)}, f32[51,15,64]{2,1,0:T(8,128)S(1)}, /*index=5*/s32[]{:T(128)}, s32[]{:T(128)}) while((s32[]{:T(128)}, f32[51,64]{1,0:T(8,128)S(1)}, f32[51,64]{1,0:T(8,128)S(1)}, f32[51,15,64]{2,1,0:T(8,128)S(1)}, ...), condition=%wide.region_7.0_spmd.clone, body=%wide.region_1.0_spmd.clone.sunk | while | flops 807491 | bytes 1034839 | solution.py:58
  30.1 0.3 add_reduce_fusion.25
  30.6 0.3 add_reduce_fusion.25
  31.2 0.3 add_reduce_fusion.25
  31.7 0.3 add_reduce_fusion.25
  32.3 0.3 add_reduce_fusion.25
  32.9 0.3 add_reduce_fusion.25
  33.4 0.3 add_reduce_fusion.25
  34.0 0.3 add_reduce_fusion.25
  34.5 0.3 add_reduce_fusion.25
  35.1 0.3 add_reduce_fusion.25
  35.6 0.3 add_reduce_fusion.25
  38.8 7.8 %all-gather = f32[4,64,2]{1,2,0:T(2,128)S(1)} all-gather(f32[1,64,2]{1,2,0:T(2,128)S(1)} %get-tuple-element.353), channel_id=1, replica_groups=mesh['section'=4,'pix'=8] {'section'}, dimensions={0}, use_global_device_ids=true | all-gather | bytes 2560 | tf_op jit(solution)/shard_map/all_gather | solution.py:92
  46.7 7.1 %collective-permute-start.2 = (f32[2,256]{1,0:T(2,128)S(1)}, f32[2,256]{1,0:T(2,128)S(1)}, u32[]{:S(2)}, u32[]{:S(2)}) collective-permute-start(f32[2,256]{1,0:T(2,128)S(1)} %bitcast.309), channel_id=1, source_target_pairs={{0,1},{1,2},{2,3},{3,4},{4,5},{5,6},{6,7},{8,9},{9,10},{10,11},{11... | collective-permute-start | bytes 6152 | tf_op jit(solution)/shard_map/ppermute | solution.py:20
  53.8 1.3 collective-permute-start.3
  55.2 0.6 stack.105
  55.8 0.6 stack.121
  56.4 1.8 %collective-permute-done.3 = f32[2,256]{1,0:T(2,128)S(1)} collective-permute-done((f32[2,256]{1,0:T(2,128)S(1)}, f32[2,256]{1,0:T(2,128)S(1)}, u32[]{:S(2)}, u32[]{:S(2)}) %collective-permute-start.3) | collective-permute-done | bytes 2080 | tf_op jit(solution)/shard_map/ppermute | solution.py:23
  58.2 1.2 copy.198
  59.5 1.4 fusion.18
  60.8 2.9 %gather_fusion.2 = f32[960,51]{1,0:T(8,128)S(1)} fusion(f32[51,768]{0,1:T(8,128)S(1)} %get-tuple-element.313, s32[1024]{0:T(1024)S(1)} %pad_clamp_fusion), kind=kCustom, calls=%fused_computation.2 | custom fusion | bytes 395520 | tf_op jit(solution)/shard_map/gather | solution.py:39
  64.0 2.9 %gather_fusion.3 = f32[960,51]{1,0:T(8,128)S(1)} fusion(f32[51,768]{0,1:T(8,128)S(1)} %get-tuple-element.312, s32[1024]{0:T(1024)S(1)} %pad_clamp_fusion), kind=kCustom, calls=%fused_computation.3 | custom fusion | bytes 395520 | tf_op jit(solution)/shard_map/gather | solution.py:40
  67.4 8.8 %while.53 = (s32[]{:T(128)}, f32[51,64]{1,0:T(8,128)S(1)}, f32[51,64]{1,0:T(8,128)S(1)}, f32[51,15,64]{2,1,0:T(8,128)S(1)}, f32[51,15,64]{2,1,0:T(8,128)S(1)}, /*index=5*/s32[]{:T(128)}, s32[]{:T(128)}) while((s32[]{:T(128)}, f32[51,64]{1,0:T(8,128)S(1)}, f32[51,64]{1,0:T(8,128)S(1)}, f32[51,15,64]{2,1,0:T(8,128)S(1)}, ...), condition=%wide.region_17.0_spmd.clone, body=%wide.region_11.0_spmd.clone.sunk | while | flops 807491 | bytes 1034839 | solution.py:58
  76.3 7.5 %all-gather.1 = f32[4,64,2]{1,2,0:T(2,128)S(1)} all-gather(f32[1,64,2]{1,2,0:T(2,128)S(1)} %get-tuple-element.351), channel_id=1, replica_groups=mesh['section'=4,'pix'=8] {'section'}, dimensions={0}, use_global_device_ids=true | all-gather | bytes 2560 | tf_op jit(solution)/shard_map/all_gather | solution.py:92
  83.8 2.2 %collective-permute-start.4 = (f32[2,256]{1,0:T(2,128)S(1)}, f32[2,256]{1,0:T(2,128)S(1)}, u32[]{:S(2)}, u32[]{:S(2)}) collective-permute-start(f32[2,256]{1,0:T(2,128)S(1)} %bitcast.312), channel_id=1, source_target_pairs={{0,1},{1,2},{2,3},{3,4},{4,5},{5,6},{6,7},{8,9},{9,10},{10,11},{11... | collective-permute-start | bytes 6152 | tf_op jit(solution)/shard_map/ppermute | solution.py:20
  86.1 1.3 collective-permute-start.5
  87.5 3.2 %collective-permute-done.5 = f32[2,256]{1,0:T(2,128)S(1)} collective-permute-done((f32[2,256]{1,0:T(2,128)S(1)}, f32[2,256]{1,0:T(2,128)S(1)}, u32[]{:S(2)}, u32[]{:S(2)}) %collective-permute-start.5) | collective-permute-done | bytes 2080 | tf_op jit(solution)/shard_map/ppermute | solution.py:23
  90.7 0.3 copy.203
  91.0 0.3 fusion.17
  91.3 2.9 %gather_fusion.4 = f32[960,51]{1,0:T(8,128)S(1)} fusion(f32[51,768]{0,1:T(8,128)S(1)} %get-tuple-element.311, s32[1024]{0:T(1024)S(1)} %pad_clamp_fusion), kind=kCustom, calls=%fused_computation.4 | custom fusion | bytes 395520 | tf_op jit(solution)/shard_map/gather | solution.py:39
  94.5 2.9 %gather_fusion.5 = f32[960,51]{1,0:T(8,128)S(1)} fusion(f32[51,768]{0,1:T(8,128)S(1)} %get-tuple-element.310, s32[1024]{0:T(1024)S(1)} %pad_clamp_fusion), kind=kCustom, calls=%fused_computation.5 | custom fusion | bytes 395520 | tf_op jit(solution)/shard_map/gather | solution.py:40
  97.9 8.8 %while.54 = (s32[]{:T(128)}, f32[51,64]{1,0:T(8,128)S(1)}, f32[51,64]{1,0:T(8,128)S(1)}, f32[51,15,64]{2,1,0:T(8,128)S(1)}, f32[51,15,64]{2,1,0:T(8,128)S(1)}, /*index=5*/s32[]{:T(128)}, s32[]{:T(128)}) while((s32[]{:T(128)}, f32[51,64]{1,0:T(8,128)S(1)}, f32[51,64]{1,0:T(8,128)S(1)}, f32[51,15,64]{2,1,0:T(8,128)S(1)}, ...), condition=%wide.region_27.0_spmd.clone, body=%wide.region_21.0_spmd.clone.sunk | while | flops 807491 | bytes 1034839 | solution.py:58
  106.8 7.7 %all-gather.2 = f32[4,64,2]{1,2,0:T(2,128)S(1)} all-gather(f32[1,64,2]{1,2,0:T(2,128)S(1)} %get-tuple-element.349), channel_id=1, replica_groups=mesh['section'=4,'pix'=8] {'section'}, dimensions={0}, use_global_device_ids=true | all-gather | bytes 2560 | tf_op jit(solution)/shard_map/all_gather | solution.py:92
  114.6 2.2 %collective-permute-start.6 = (f32[2,256]{1,0:T(2,128)S(1)}, f32[2,256]{1,0:T(2,128)S(1)}, u32[]{:S(2)}, u32[]{:S(2)}) collective-permute-start(f32[2,256]{1,0:T(2,128)S(1)} %bitcast.306), channel_id=1, source_target_pairs={{0,1},{1,2},{2,3},{3,4},{4,5},{5,6},{6,7},{8,9},{9,10},{10,11},{11... | collective-permute-start | bytes 6152 | tf_op jit(solution)/shard_map/ppermute | solution.py:20
  116.8 1.3 collective-permute-start.7
  118.3 3.2 %collective-permute-done.7 = f32[2,256]{1,0:T(2,128)S(1)} collective-permute-done((f32[2,256]{1,0:T(2,128)S(1)}, f32[2,256]{1,0:T(2,128)S(1)}, u32[]{:S(2)}, u32[]{:S(2)}) %collective-permute-start.7) | collective-permute-done | bytes 2080 | tf_op jit(solution)/shard_map/ppermute | solution.py:23
  121.5 0.3 copy.208
  121.8 0.3 fusion.16
  122.0 2.9 %gather_fusion.6 = f32[960,51]{1,0:T(8,128)S(1)} fusion(f32[51,768]{0,1:T(8,128)S(1)} %get-tuple-element.305, s32[1024]{0:T(1024)S(1)} %pad_clamp_fusion), kind=kCustom, calls=%fused_computation.6 | custom fusion | bytes 395520 | tf_op jit(solution)/shard_map/gather | solution.py:39
  125.2 2.9 %gather_fusion.7 = f32[960,51]{1,0:T(8,128)S(1)} fusion(f32[51,768]{0,1:T(8,128)S(1)} %get-tuple-element.304, s32[1024]{0:T(1024)S(1)} %pad_clamp_fusion), kind=kCustom, calls=%fused_computation.7 | custom fusion | bytes 395520 | tf_op jit(solution)/shard_map/gather | solution.py:40
  128.6 8.5 %while.55 = (s32[]{:T(128)}, f32[51,64]{1,0:T(8,128)S(1)}, f32[51,64]{1,0:T(8,128)S(1)}, f32[51,15,64]{2,1,0:T(8,128)S(1)}, f32[51,15,64]{2,1,0:T(8,128)S(1)}, /*index=5*/s32[]{:T(128)}, s32[]{:T(128)}) while((s32[]{:T(128)}, f32[51,64]{1,0:T(8,128)S(1)}, f32[51,64]{1,0:T(8,128)S(1)}, f32[51,15,64]{2,1,0:T(8,128)S(1)}, ...), condition=%wide.region_37.0_spmd.clone, body=%wide.region_31.0_spmd.clone.sunk | while | flops 807491 | bytes 1034839 | solution.py:58
  137.3 0.7 reshape.547
  138.0 3.2 %all-to-all-start.1 = ((f32[4,1,128]{2,1,0:T(1,128)}), f32[4,1,128]{2,1,0:T(1,128)S(1)}, u32[]{:S(2)}, u32[]{:S(2)}) async-start(f32[4,1,128]{2,1,0:T(1,128)} %reshape.547), calls=%async_computation.1 | async-start | bytes 4096 | tf_op jit(solution)/shard_map/all_to_all | solution.py:117
  141.7 0.9 reshape.545
  142.5 3.2 %all-to-all-done.1 = f32[4,1,128]{2,1,0:T(1,128)S(1)} async-done(((f32[4,1,128]{2,1,0:T(1,128)}), f32[4,1,128]{2,1,0:T(1,128)S(1)}, u32[]{:S(2)}, u32[]{:S(2)}) %all-to-all-start.1) | async-done | bytes 2080 | tf_op jit(solution)/shard_map/all_to_all | solution.py:117
  145.8 3.3 %all-to-all-start = ((f32[4,1,6400]{2,1,0:T(1,128)}), f32[4,1,6400]{2,1,0:T(1,128)S(1)}, u32[]{:S(2)}, u32[]{:S(2)}) async-start(f32[4,1,6400]{2,1,0:T(1,128)} %reshape.545), calls=%async_computation | async-start | bytes 204800 | tf_op jit(solution)/shard_map/all_to_all | solution.py:116
  149.8 0.6 broadcast.415
  150.3 0.7 reduce.5
  151.1 0.7 all_to_all.25
  151.8 2.2 %all-to-all-done = f32[4,1,6400]{2,1,0:T(1,128)S(1)} async-done(((f32[4,1,6400]{2,1,0:T(1,128)}), f32[4,1,6400]{2,1,0:T(1,128)S(1)}, u32[]{:S(2)}, u32[]{:S(2)}) %all-to-all-start) | async-done | bytes 102432 | tf_op jit(solution)/shard_map/all_to_all | solution.py:116
  154.0 0.9 reduce.4
  156.5 13.9 %psum.7 = f32[2,50]{1,0:T(2,128)S(1)} all-reduce(f32[2,50]{1,0:T(2,128)S(1)} %maximum_select_fusion), channel_id=1, replica_groups=mesh['section'=4,'pix'=8] {'pix'}, use_global_device_ids=true, to_apply=%region_38.0 | all-reduce | flops 100 | bytes 800 | tf_op jit(solution)/shard_map/psum | solution.py:30
  170.9 0.7 pad_maximum_fusion.4
  (476 shorter events, 36.5 us)
Async XLA Ops:
  12.3 5.2 %collective-permute-start = (f32[2,200,256]{1,2,0:T(8,128)S(1)}, f32[2,200,256]{1,2,0:T(8,128)S(1)}, u32[]{:S(2)}, u32[]{:S(2)}) collective-permute-start(f32[2,200,256]{1,2,0:T(8,128)S(1)} %copy.191), channel_id=1, source_target_pairs={{0,1},{1,2},{2,3},{3,4},{4,5},{5,6},{6,7},{8,9},{9,10},{10,11},{11... | collective-permute-start | bytes 1228808 | tf_op jit(solution)/shard_map/ppermute | solution.py:20
  13.7 5.6 %collective-permute-start.1 = (f32[2,200,256]{1,2,0:T(8,128)S(1)}, f32[2,200,256]{1,2,0:T(8,128)S(1)}, u32[]{:S(2)}, u32[]{:S(2)}) collective-permute-start(f32[2,200,256]{1,2,0:T(8,128)S(1)} %copy.191), channel_id=1, source_target_pairs={{1,0},{2,1},{3,2},{4,3},{5,4},{6,5},{7,6},{9,8},{10,9},{11,10},{12... | collective-permute-start | bytes 1228808 | tf_op jit(solution)/shard_map/ppermute | solution.py:23
  29.8 8.9 %copy-start.4 = (f32[1,51,64]{2,0,1:T(1,128)S(1)}, f32[1,51,64]{2,0,1:T(1,128)}, u32[]{:S(2)}) copy-start(f32[1,51,64]{2,0,1:T(1,128)} %get-tuple-element.338) | copy-start | bytes 39172
  29.9 8.9 %copy-start.5 = (f32[1,51,64]{2,0,1:T(1,128)S(1)}, f32[1,51,64]{2,0,1:T(1,128)}, u32[]{:S(2)}) copy-start(f32[1,51,64]{2,0,1:T(1,128)} %get-tuple-element.339) | copy-start | bytes 39172
  29.9 25.2 %copy-start.3 = (f32[2,50,64]{2,0,1:T(2,128)S(1)}, f32[2,50,64]{2,0,1:T(2,128)}, u32[]{:S(2)}) copy-start(f32[2,50,64]{2,0,1:T(2,128)} %get-tuple-element.318) | copy-start | bytes 76804
  38.7 20.7 %copy-start = (f32[2,50,768]{1,2,0:T(8,128)S(1)}, f32[2,50,768]{1,2,0:T(8,128)}, u32[]{:S(2)}) copy-start(f32[2,50,768]{1,2,0:T(8,128)} %get-tuple-element.308) | copy-start | bytes 921604
  46.7 9.7 %collective-permute-start.2 = (f32[2,256]{1,0:T(2,128)S(1)}, f32[2,256]{1,0:T(2,128)S(1)}, u32[]{:S(2)}, u32[]{:S(2)}) collective-permute-start(f32[2,256]{1,0:T(2,128)S(1)} %bitcast.309), channel_id=1, source_target_pairs={{0,1},{1,2},{2,3},{3,4},{4,5},{5,6},{6,7},{8,9},{9,10},{10,11},{11... | collective-permute-start | bytes 6152 | tf_op jit(solution)/shard_map/ppermute | solution.py:20
  53.8 4.4 %collective-permute-start.3 = (f32[2,256]{1,0:T(2,128)S(1)}, f32[2,256]{1,0:T(2,128)S(1)}, u32[]{:S(2)}, u32[]{:S(2)}) collective-permute-start(f32[2,256]{1,0:T(2,128)S(1)} %bitcast.310), channel_id=1, source_target_pairs={{1,0},{2,1},{3,2},{4,3},{5,4},{6,5},{7,6},{9,8},{10,9},{11,10},{12... | collective-permute-start | bytes 6152 | tf_op jit(solution)/shard_map/ppermute | solution.py:23
  67.4 20.0 %copy-start.2 = (f32[2,50,64]{2,0,1:T(2,128)S(1)}, f32[2,50,64]{2,0,1:T(2,128)}, u32[]{:S(2)}) copy-start(f32[2,50,64]{2,0,1:T(2,128)} %get-tuple-element.317) | copy-start | bytes 76804
  83.8 3.6 %collective-permute-start.4 = (f32[2,256]{1,0:T(2,128)S(1)}, f32[2,256]{1,0:T(2,128)S(1)}, u32[]{:S(2)}, u32[]{:S(2)}) collective-permute-start(f32[2,256]{1,0:T(2,128)S(1)} %bitcast.312), channel_id=1, source_target_pairs={{0,1},{1,2},{2,3},{3,4},{4,5},{5,6},{6,7},{8,9},{9,10},{10,11},{11... | collective-permute-start | bytes 6152 | tf_op jit(solution)/shard_map/ppermute | solution.py:20
  86.1 4.7 %collective-permute-start.5 = (f32[2,256]{1,0:T(2,128)S(1)}, f32[2,256]{1,0:T(2,128)S(1)}, u32[]{:S(2)}, u32[]{:S(2)}) collective-permute-start(f32[2,256]{1,0:T(2,128)S(1)} %bitcast.313), channel_id=1, source_target_pairs={{1,0},{2,1},{3,2},{4,3},{5,4},{6,5},{7,6},{9,8},{10,9},{11,10},{12... | collective-permute-start | bytes 6152 | tf_op jit(solution)/shard_map/ppermute | solution.py:23
  97.9 20.2 %copy-start.1 = (f32[2,50,64]{2,0,1:T(2,128)S(1)}, f32[2,50,64]{2,0,1:T(2,128)}, u32[]{:S(2)}) copy-start(f32[2,50,64]{2,0,1:T(2,128)} %get-tuple-element.316) | copy-start | bytes 76804
  114.6 3.6 %collective-permute-start.6 = (f32[2,256]{1,0:T(2,128)S(1)}, f32[2,256]{1,0:T(2,128)S(1)}, u32[]{:S(2)}, u32[]{:S(2)}) collective-permute-start(f32[2,256]{1,0:T(2,128)S(1)} %bitcast.306), channel_id=1, source_target_pairs={{0,1},{1,2},{2,3},{3,4},{4,5},{5,6},{6,7},{8,9},{9,10},{10,11},{11... | collective-permute-start | bytes 6152 | tf_op jit(solution)/shard_map/ppermute | solution.py:20
  116.8 4.6 %collective-permute-start.7 = (f32[2,256]{1,0:T(2,128)S(1)}, f32[2,256]{1,0:T(2,128)S(1)}, u32[]{:S(2)}, u32[]{:S(2)}) collective-permute-start(f32[2,256]{1,0:T(2,128)S(1)} %bitcast.307), channel_id=1, source_target_pairs={{1,0},{2,1},{3,2},{4,3},{5,4},{6,5},{7,6},{9,8},{10,9},{11,10},{12... | collective-permute-start | bytes 6152 | tf_op jit(solution)/shard_map/ppermute | solution.py:23
  128.6 12.7 %copy-start.6 = (f32[1,51,64]{2,0,1:T(1,128)S(1)}, f32[1,51,64]{2,0,1:T(1,128)}, u32[]{:S(2)}) copy-start(f32[1,51,64]{2,0,1:T(1,128)} %stack.105) | copy-start | bytes 39172
  128.6 12.7 %copy-start.7 = (f32[1,51,64]{2,0,1:T(1,128)S(1)}, f32[1,51,64]{2,0,1:T(1,128)}, u32[]{:S(2)}) copy-start(f32[1,51,64]{2,0,1:T(1,128)} %stack.121) | copy-start | bytes 39172
  138.0 7.8 %all-to-all-start.1 = ((f32[4,1,128]{2,1,0:T(1,128)}), f32[4,1,128]{2,1,0:T(1,128)S(1)}, u32[]{:S(2)}, u32[]{:S(2)}) async-start(f32[4,1,128]{2,1,0:T(1,128)} %reshape.547), calls=%async_computation.1 | async-start | bytes 4096 | tf_op jit(solution)/shard_map/all_to_all | solution.py:117
  145.8 8.3 %all-to-all-start = ((f32[4,1,6400]{2,1,0:T(1,128)}), f32[4,1,6400]{2,1,0:T(1,128)S(1)}, u32[]{:S(2)}, u32[]{:S(2)}) async-start(f32[4,1,6400]{2,1,0:T(1,128)} %reshape.545), calls=%async_computation | async-start | bytes 204800 | tf_op jit(solution)/shard_map/all_to_all | solution.py:116
where the time goes:
time: 172 us
  blocking collectives  48.4 us (28%)
  local copies, waits for them, and re-layouts  39.5 us (23%)
  other arithmetic  39.4 us (23%)
  starting transfers between devices  24.5 us (14%)
  waiting for transfers between devices  15.5 us (9%)
  loops' own time  2.34 us (1%)
  between operations  2 us (1%)
    all_gather x3, blocking collectives, on_device(): block_virtual = lax.all_gather(virtual_part, 'section', axis=1, tiled=True)  23 us
    reduce_sum x64, other arithmetic, turn(): u_im = vec_im + jnp.sum(z_re * c_im[None] + z_im * c_re[None], axis=1)  17.2 us
    gather x8, local copies, waits for them, and re-layouts, solve_block(): near_im = ext_im[:, index]  14.7 us
    psum x1, blocking collectives, spread(): return lax.psum(jnp.where(mine, array, jnp.zeros_like(array)), axis)  13.9 us
    ppermute x4, starting transfers between devices, extended_2(): lax.ppermute(lax.slice_in_dim(block, block.shape[dim] - width, None, axis...  12.8 us
    gather x8, local copies, waits for them, and re-layouts, solve_block(): near_re = ext_re[:, index]  12.6 us
    reduce_sum x64, other arithmetic, turn(): jnp.sum(z_re * vec_re[:, None, :] + z_im * vec_im[:, None, :], axis=0)  11.5 us
    all_gather x1, blocking collectives, on_device(): whole = lax.all_gather(slc, 'section', axis=1, tiled=True)  11.5 us
  transfers between devices with their start and end apart: 10, of which 6 were waited for; matrix products, arithmetic and copies ran while one was open for 4% of the time, Pallas kernels for 0%

commit v1 on v0

v1 whole, which is shorter than its diff:
```python
import functools
import math

import jax
import jax.numpy as jnp
from jax import lax
from jax.experimental import pallas as pl
from jax.experimental.pallas import tpu as pltpu
from jax.sharding import PartitionSpec as P

ITERS = 16
FLOOR = 0.05
REACH_LIMIT = 256
LANES = 128
SUB = 8
KP = 16
SHRINK = 2.0**-35

SMEM = pl.BlockSpec(memory_space=pltpu.SMEM)
VMEM = pl.BlockSpec(memory_space=pltpu.VMEM)


def f32(*shape):
    return jax.ShapeDtypeStruct(shape, jnp.float32)


def params():
    return pltpu.CompilerParams(vmem_limit_bytes=20 * 1024 * 1024)


def up(n, m):
    return -(-n // m) * m


def colsum(x):
    return jnp.sum(x, axis=0, keepdims=True)


def unit(real, imag):
    scale = 1.0 / jnp.maximum(jnp.sqrt(real * real + imag * imag), FLOOR)
    return (real * scale, imag * scale)


def half(h):
    return pl.ds(h * LANES, LANES)


def gather(base, idx_ref, pieces, xs_ref, hl_ref, zr_ref, zi_ref):
    count, rows, pixels = zr_ref.shape
    dates = pieces[0].shape[1]
    xs_ref[...] = jnp.zeros_like(xs_ref)
    at = 0
    for piece in pieces:
        width = piece.shape[2]
        for c in range(2):
            xs_ref[pl.ds(c * rows, dates), pl.ds(at, width)] = piece[c]
        at += width
    high = xs_ref[...].astype(jnp.bfloat16)
    hl_ref[0 : 2 * rows] = high
    hl_ref[2 * rows : 4 * rows] = (xs_ref[...] - high.astype(jnp.float32)).astype(jnp.bfloat16)
    window = xs_ref.shape[1]
    place = lax.broadcasted_iota(jnp.int32, (window, pixels), 0)
    for k in range(count):
        near = idx_ref[k : k + 1, :] - base
        hot = jnp.where(place == near, 1.0, 0.0).astype(jnp.bfloat16)
        got = jnp.dot(hl_ref[...], hot, preferred_element_type=jnp.float32)
        zr_ref[k] = got[0:rows] + got[2 * rows : 3 * rows]
        zi_ref[k] = got[rows : 2 * rows] + got[3 * rows : 4 * rows]


def scale_dates(zr_ref, zi_ref):
    count, rows, pixels = zr_ref.shape
    for h in range(pixels // LANES):
        for r in range(0, rows, SUB):
            power = None
            for k in range(count):
                a = zr_ref[k, pl.ds(r, SUB), half(h)]
                b = zi_ref[k, pl.ds(r, SUB), half(h)]
                power = a * a + b * b if power is None else power + (a * a + b * b)
            scale = lax.rsqrt(jnp.maximum(power, 1.0))
            for k in range(count):
                zr_ref[k, pl.ds(r, SUB), half(h)] *= scale
                zi_ref[k, pl.ds(r, SUB), half(h)] *= scale


def merge_rows(parts):
    row = lax.broadcasted_iota(jnp.int32, (SUB, LANES), 0)
    for step in (4, 2, 1):
        low = jnp.bitwise_and(row, step) == 0
        n = len(parts) // 2
        out = []
        for i in range(n):
            a, b = parts[i], parts[i + n]
            far = jnp.where(low, pltpu.roll(a, SUB - step, 0), pltpu.roll(b, step, 0))
            out.append(jnp.where(low, a, b) + far)
        parts = out
    return parts[0]


def gram(pair_ref, zr_ref, zi_ref, xs_ref, own_at, gr_ref, gi_ref, sum_ref, block=3):
    count, rows, pixels = zr_ref.shape
    zero = jnp.zeros((SUB, LANES), jnp.float32)
    for h in range(pixels // LANES):
        here = pl.ds(own_at + h * LANES, LANES)

        def load(k, r):
            if k == count:
                return (xs_ref[pl.ds(r, SUB), here], xs_ref[pl.ds(rows + r, SUB), here])
            return (zr_ref[k, pl.ds(r, SUB), half(h)], zi_ref[k, pl.ds(r, SUB), half(h)])

        for k0 in range(0, count, block):
            for l0 in range(k0, count + 1, block):
                pairs = [
                    (k, l)
                    for k in range(k0, min(k0 + block, count))
                    for l in range(l0, min(l0 + block, count + 1))
                    if l >= k
                ]
                acc = {}
                for r in range(0, rows, SUB):
                    val = {n: load(n, r) for n in sorted({n for p in pairs for n in p})}
                    for k, l in pairs:
                        ar, ai = val[k]
                        br, bi = val[l]
                        re = ar * br + ai * bi
                        im = None if k == l else ar * bi - ai * br
                        if r:
                            re = acc[k, l][0] + re
                            im = None if k == l else acc[k, l][1] + im
                        acc[k, l] = (re, im)
                for k, l in pairs:
                    pair_ref[0, l, k] = acc[k, l][0]
                    pair_ref[1, l, k] = zero if k == l else acc[k, l][1]
        for c, g_ref in ((0, gr_ref), (1, gi_ref)):
            for l in range(count + 1):
                for kt in range(KP // SUB):
                    ks = range(kt * SUB, kt * SUB + SUB)
                    if min(ks) > min(l, count - 1):
                        continue
                    parts = [pair_ref[c, l, k] if k <= min(l, count - 1) else zero for k in ks]
                    g_ref[l, h, pl.ds(kt * SUB, SUB), :] = merge_rows(parts)
        row = lax.broadcasted_iota(jnp.int32, (SUB, LANES), 0)
        for c, g_ref in ((0, gr_ref), (1, gi_ref)):
            for l in range(count):
                for kt in range(KP // SUB):
                    ks = list(range(kt * SUB, kt * SUB + SUB))
                    if max(ks) <= l:
                        continue
                    other = jnp.concatenate(
                        [g_ref[k, h, pl.ds(l, 1), :] if l < k < count else zero[0:1] for k in ks], axis=0
                    )
                    if c:
                        other = -other
                    if min(ks) <= l:
                        other = jnp.where(row + ks[0] <= l, g_ref[l, h, pl.ds(kt * SUB, SUB), :], other)
                    g_ref[l, h, pl.ds(kt * SUB, SUB), :] = other
        for c in range(2):
            tiles = []
            for k in range(KP):
                total = None
                if k <= count:
                    for r in range(0, rows, SUB):
                        v = load(k, r)[c]
                        total = v if total is None else total + v
                tiles.append(zero if total is None else total)
            for kt in range(KP // SUB):
                sum_ref[c, h, pl.ds(kt * SUB, SUB), :] = merge_rows(tiles[kt * SUB : kt * SUB + SUB])


def turns(gr_ref, gi_ref, g0, count):
    halves = gr_ref.shape[1]

    def product(b, g):
        acc = [list(x) for x in g]
        for l in range(count):
            for h in range(halves):
                br = jnp.broadcast_to(b[h][0][l : l + 1], (KP, LANES))
                bi = jnp.broadcast_to(b[h][1][l : l + 1], (KP, LANES))
                gr = gr_ref[l, h]
                gi = gi_ref[l, h]
                acc[h][0] = acc[h][0] + (gr * br - gi * bi)
                acc[h][1] = acc[h][1] + (gr * bi + gi * br)
        return acc

    def step(_, carry):
        b, g = carry
        t = product(b, g)
        return tuple((b[h][0] + t[h][0], b[h][1] + t[h][1]) for h in range(halves)), g

    g = tuple(g0)
    b = g
    b, g = lax.fori_loop(0, ITERS // 2 - 1, step, (b, g))
    b = tuple((x * SHRINK, y * SHRINK) for x, y in b)
    g = tuple((x * SHRINK, y * SHRINK) for x, y in g)
    b, g = lax.fori_loop(0, ITERS - ITERS // 2, step, (b, g))
    return b, g, product(b, g)


def solve(virtual, gr_ref, gi_ref, hr, hi, sum_ref, stack, beta_ref, state_ref):
    halves = gr_ref.shape[1]
    count = gr_ref.shape[0]
    first = 1.0 / math.sqrt(stack)
    g0 = []
    for h in range(halves):
        zr, zi = sum_ref[0, h], sum_ref[1, h]
        row = lax.broadcasted_iota(jnp.int32, (KP, LANES), 0)
        zr = jnp.where(row < count, zr, 0.0)
        zi = jnp.where(row < count, zi, 0.0)
        if virtual is not None:
            zr = zr + virtual[h][1][0]
            zi = zi + virtual[h][1][1]
        g0.append((zr * first, zi * -first))
    b, g, t = turns(gr_ref, gi_ref, g0, count)
    for h in range(halves):
        norm = colsum(b[h][0] * (g[h][0] + t[h][0]) + b[h][1] * (g[h][1] + t[h][1]))
        inv = lax.rsqrt(SHRINK * SHRINK + norm)
        br, bi = b[h][0] * inv, b[h][1] * inv
        a = inv * (SHRINK * first)
        xr, xi = hr[h], hi[h]
        sr, si = sum_ref[0, h][count : count + 1], sum_ref[1, h][count : count + 1]
        fr, fi = a, jnp.zeros_like(a)
        if virtual is not None:
            (wr, wi), (zr, zi) = virtual[h]
            xr, xi = xr + (zr * wr + zi * wi), xi + (zr * wi - zi * wr)
            sr, si = sr + wr, si + wi
            fr = a + colsum(zr * br - zi * bi)
            fi = colsum(zr * bi + zi * br)
        beta_ref[0, h] = br
        beta_ref[1, h] = bi
        fr, fi = unit(fr, fi)
        state_ref[0:1, half(h)] = a * sr + colsum(br * xr + bi * xi)
        state_ref[1:2, half(h)] = a * si + colsum(br * xi - bi * xr)
        state_ref[2:3, half(h)] = fr
        state_ref[3:4, half(h)] = fi
        state_ref[4:5, half(h)] = a
        state_ref[5:8, half(h)] = jnp.zeros((3, LANES), jnp.float32)


def prepare_kernel(
    stack, base_ref, idx_ref, low_ref, own_ref, high_ref,
    zr_ref, zi_ref, gr_ref, gi_ref, sum_ref, beta_ref, state_ref, comp_ref,
    xs_ref, hl_ref, pair_ref,
):
    gather(base_ref[0], idx_ref, (low_ref, own_ref, high_ref), xs_ref, hl_ref, zr_ref, zi_ref)
    scale_dates(zr_ref, zi_ref)
    gram(pair_ref, zr_ref, zi_ref, xs_ref, low_ref.shape[2], gr_ref, gi_ref, sum_ref)
    count = zr_ref.shape[0]
    halves = gr_ref.shape[1]
    hr = [gr_ref[count, h] for h in range(halves)]
    hi = [gi_ref[count, h] for h in range(halves)]
    solve(None, gr_ref.at[0:count], gi_ref.at[0:count], hr, hi, sum_ref, stack, beta_ref, state_ref)
    comp_ref[...] = state_ref[0:2]


def lane_take(x, i):
    return jnp.take_along_axis(x, i, axis=1, mode="promise_in_bounds")


def round_kernel(
    rnd, stack, where_ref, idx_ref, low_ref, own_ref, high_ref,
    gr_ref, gi_ref, sum_ref, beta0_ref, state0_ref,
    beta_ref, state_ref, comp_ref, fr_ref, fi_ref,
):
    count = gr_ref.shape[0] - 1
    halves = gr_ref.shape[1]
    reach = low_ref.shape[1]
    beta_ref[...] = beta0_ref[...]
    state_ref[...] = state0_ref[...]

    @pl.when(where_ref[1] == rnd)
    def _():
        tiles = []
        for ref in (low_ref, own_ref, high_ref):
            for t in range(ref.shape[1] // LANES):
                tiles.append([ref[c : c + 1, half(t)] for c in range(2)])
        virtual = []
        for h in range(halves):
            parts = []
            for kt in range(KP // SUB):
                rows = min(SUB, count - kt * SUB)
                raw = idx_ref[pl.ds(kt * SUB, rows), half(h)] - where_ref[0]
                if rows < SUB:
                    raw = jnp.concatenate([raw, jnp.full((SUB - rows, LANES), -1, jnp.int32)], axis=0)
                lane = jnp.bitwise_and(raw, LANES - 1)
                tile = jnp.right_shift(raw, 7)
                both = []
                for c in range(2):
                    out = jnp.zeros((SUB, LANES), jnp.float32)
                    for n in range(h, h + 2 * reach // LANES + 1):
                        got = lane_take(jnp.broadcast_to(tiles[n][c], (SUB, LANES)), lane)
                        out = jnp.where(tile == n, got, out)
                    both.append(out)
                parts.append(both)
            zr = jnp.concatenate([p[0] for p in parts], axis=0)
            zi = jnp.concatenate([p[1] for p in parts], axis=0)
            scale = lax.rsqrt(jnp.maximum(colsum(zr * zr + zi * zi), 1.0))
            zr, zi = zr * scale, zi * scale
            own = tiles[reach // LANES + h]
            virtual.append((own, (zr, zi)))
            for l in range(count):
                br = jnp.broadcast_to(zr[l : l + 1], (KP, LANES))
                bi = jnp.broadcast_to(zi[l : l + 1], (KP, LANES))
                fr_ref[l, h] = gr_ref[l, h] + (zr * br + zi * bi)
                fi_ref[l, h] = gi_ref[l, h] + (zr * bi - zi * br)
        hr = [gr_ref[count, h] for h in range(halves)]
        hi = [gi_ref[count, h] for h in range(halves)]
        solve(virtual, fr_ref, fi_ref, hr, hi, sum_ref, stack, beta_ref, state_ref)

    comp_ref[...] = state_ref[0:2]


def vector_kernel(at_ref, zr_ref, zi_ref, beta_ref, state_ref, vec_ref, slot_ref, turned_ref):
    count, rows, pixels = zr_ref.shape
    dates = vec_ref.shape[1]
    local = at_ref[2]
    for h in range(pixels // LANES):
        a = state_ref[4:5, half(h)]
        acc_r = [jnp.broadcast_to(a, (SUB, LANES)) for _ in range(0, rows, SUB)]
        acc_i = [jnp.zeros((SUB, LANES), jnp.float32) for _ in range(0, rows, SUB)]
        for k in range(count):
            br = jnp.broadcast_to(beta_ref[0, h, k : k + 1, :], (SUB, LANES))
            bi = jnp.broadcast_to(beta_ref[1, h, k : k + 1, :], (SUB, LANES))
            for n, r in enumerate(range(0, rows, SUB)):
                zr = zr_ref[k, pl.ds(r, SUB), half(h)]
                zi = zi_ref[k, pl.ds(r, SUB), half(h)]
                acc_r[n] = acc_r[n] + (zr * br - zi * bi)
                acc_i[n] = acc_i[n] + (zr * bi + zi * br)
        for c, acc in ((0, acc_r), (1, acc_i)):
            whole = jnp.concatenate(acc, axis=0)
            vec_ref[c, :, half(h)] = whole[0:dates]
            wide = jnp.concatenate([whole, jnp.zeros((up(rows, LANES) - rows, LANES), jnp.float32)], axis=0)
            turned_ref[c, half(h)] = jnp.transpose(wide)
    slot_ref[...] = jnp.zeros_like(slot_ref)
    lane = lax.broadcasted_iota(jnp.int32, (1, LANES), 1)
    halves = pixels // LANES
    for c in range(2):
        for h in range(halves):
            slot_ref[c * halves + h : c * halves + h + 1] = state_ref[2 + c : 3 + c, half(h)]
        slot_ref[2 * halves + c : 2 * halves + c + 1] = turned_ref[c, pl.ds(local, 1), :]
        picked = jnp.zeros((1, LANES), jnp.float32)
        for h in range(halves):
            picked = picked + jnp.where(lane == local - h * LANES, state_ref[2 + c : 3 + c, half(h)], 0.0)
        slot_ref[2 * halves + 2 + c : 2 * halves + 3 + c] = jnp.broadcast_to(
            jnp.sum(picked, axis=1, keepdims=True), (1, LANES)
        )


def finish_kernel(sections, at_ref, vec_ref, got_ref, out_ref):
    dates, pixels = vec_ref.shape[1:]
    section, mine, root, blocks = at_ref[1], at_ref[3], at_ref[4], at_ref[5]
    halves = pixels // LANES
    one = jnp.ones((1, LANES), jnp.float32)
    datum = [(one, 0.0 * one) for _ in range(halves)]
    at_root = (one, 0.0 * one)
    for s in range(sections - 1, 0, -1):
        later = section < s
        own = got_ref[s * blocks + mine]
        ref = got_ref[s * blocks + root]

        def times(d, fr, fi):
            fr = jnp.where(later, fr, 1.0)
            fi = jnp.where(later, fi, 0.0)
            return (d[0] * fr - d[1] * fi, d[0] * fi + d[1] * fr)

        for h in range(halves):
            datum[h] = times(datum[h], own[h : h + 1], own[halves + h : halves + h + 1])
        at_root = times(at_root, ref[2 * halves + 2 : 2 * halves + 3], ref[2 * halves + 3 : 2 * halves + 4])
    ref = got_ref[section * blocks + root]
    vr, vi = ref[2 * halves : 2 * halves + 1], ref[2 * halves + 1 : 2 * halves + 2]
    ur, ui = unit(vr * at_root[0] - vi * at_root[1], vr * at_root[1] + vi * at_root[0])
    gain = math.sqrt(dates + 1)
    ur = jnp.transpose(jnp.broadcast_to(ur * gain, (LANES, LANES)))[0:dates]
    ui = jnp.transpose(jnp.broadcast_to(ui * gain, (LANES, LANES)))[0:dates]
    for h in range(halves):
        wr = ur * datum[h][0] + ui * datum[h][1]
        wi = ur * datum[h][1] - ui * datum[h][0]
        vr = vec_ref[0, :, half(h)]
        vi = vec_ref[1, :, half(h)]
        out_ref[0, :, half(h)] = vr * wr - vi * wi
        out_ref[1, :, half(h)] = vr * wi + vi * wr


def on_device(slc, neighbours, reference_pixel):
    dates, pixels = slc.shape[1:]
    count = neighbours.shape[0]
    reach = min(pixels, REACH_LIMIT)
    sections = lax.axis_size("section")
    blocks = lax.axis_size("pix")
    section = lax.axis_index("section")
    block = lax.axis_index("pix")
    stack = dates + 1
    halves = pixels // LANES
    rows = up(dates, SUB)
    window = pixels + 2 * reach
    base = block * pixels - reach

    forward = [(i, i + 1) for i in range(blocks - 1)]
    backward = [(i + 1, i) for i in range(blocks - 1)]
    low = lax.ppermute(slc[:, :, pixels - reach :], "pix", forward)
    high = lax.ppermute(slc[:, :, :reach], "pix", backward)

    root = reference_pixel[0] // pixels
    local = reference_pixel[0] - root * pixels
    at = jnp.stack([base, section, local, block, root, jnp.int32(blocks)]).astype(jnp.int32)

    zr, zi, gr, gi, sums, beta, state, comp = pl.pallas_call(
        functools.partial(prepare_kernel, stack),
        out_shape=[
            f32(count, rows, pixels), f32(count, rows, pixels),
            f32(count + 1, halves, KP, LANES), f32(count + 1, halves, KP, LANES),
            f32(2, halves, KP, LANES), f32(2, halves, KP, LANES), f32(SUB, pixels), f32(2, pixels),
        ],
        in_specs=[SMEM] + [VMEM] * 4,
        out_specs=[VMEM] * 8,
        scratch_shapes=[
            pltpu.VMEM((2 * rows, window), jnp.float32),
            pltpu.VMEM((4 * rows, window), jnp.bfloat16),
            pltpu.VMEM((2, count + 1, count, SUB, LANES), jnp.float32),
        ],
        compiler_params=params(),
        name="prepare",
    )(at, neighbours, low, slc, high)

    for rnd in range(1, sections):
        def hop(shift):
            pairs = [
                ((rnd - 1) * blocks + q, rnd * blocks + q + shift)
                for q in range(blocks)
                if 0 <= q + shift < blocks
            ]
            return lax.ppermute(comp, ("section", "pix"), pairs)

        beta, state, comp = pl.pallas_call(
            functools.partial(round_kernel, rnd, stack),
            out_shape=[f32(2, halves, KP, LANES), f32(SUB, pixels), f32(2, pixels)],
            in_specs=[SMEM] + [VMEM] * 9,
            out_specs=[VMEM] * 3,
            scratch_shapes=[pltpu.VMEM((count, halves, KP, LANES), jnp.float32)] * 2,
            compiler_params=params(),
            name=f"round{rnd}",
        )(at, neighbours, hop(1)[:, pixels - reach :], hop(0), hop(-1)[:, :reach], gr, gi, sums, beta, state)

    slot_rows = up(2 * halves + 4, SUB)
    vec, slot = pl.pallas_call(
        vector_kernel,
        out_shape=[f32(2, dates, pixels), f32(slot_rows, LANES)],
        in_specs=[SMEM] + [VMEM] * 4,
        out_specs=[VMEM] * 2,
        scratch_shapes=[pltpu.VMEM((2, pixels, LANES), jnp.float32)],
        compiler_params=params(),
        name="vectors",
    )(at, zr, zi, beta, state)
    devices = sections * blocks
    sent = jnp.broadcast_to(slot[None], (devices, slot_rows, LANES))
    got = lax.all_to_all(sent, ("section", "pix"), 0, 0, tiled=True)
    out = pl.pallas_call(
        functools.partial(finish_kernel, sections),
        out_shape=f32(2, dates, pixels),
        in_specs=[SMEM] + [VMEM] * 2,
        out_specs=VMEM,
        compiler_params=params(),
        name="finish",
    )(at, vec, got)
    return (out, comp[:, None, :])


def solution(mesh):
    return jax.shard_map(
        on_device,
        mesh=mesh,
        in_specs=(P(None, "section", "pix"), P(None, "pix"), P()),
        out_specs=(P(None, "section", "pix"), P(None, "section", "pix")),
        check_vma=False,
    )
```

time: 172 us -> 61.2 us (0.36)
  blocking collectives: 48.4 us -> 0 us
  other arithmetic: 39.4 us -> 0 us
  local copies, waits for them, and re-layouts: 39.5 us -> 3.4 us
  starting transfers between devices: 24.5 us -> 37.3 us
  Pallas kernels: 0 us -> 9.53 us
  waiting for transfers between devices: 15.5 us -> 9.04 us
  loops' own time: 2.34 us -> 0 us
    all_gather x4 -> x0, blocking collectives: 34.5 us -> none  [the longest x3 23 us: on_device(): block_virtual = lax.all_gather(virtual_part, 'section', axis=1, tiled=True)]
    reduce_sum x200 -> x0, other arithmetic: 31.4 us -> none  [the longest x64 17.2 us: turn(): u_im = vec_im + jnp.sum(z_re * c_im[None] + z_im * c_re[None], axis=1)]
    gather x16 -> x0, local copies, waits for them, and re-layouts: 27.3 us -> none  [the longest x8 14.7 us: solve_block(): near_im = ext_im[:, index]]
    psum x1 -> x0, blocking collectives: 13.9 us -> none  [spread(): return lax.psum(jnp.where(mine, array, jnp.zeros_like(array)), axis)]
    all_to_all x2 -> x1, starting transfers between devices: 6.53 us -> 20.4 us  [on_device(): got = lax.all_to_all(sent, ('section', 'pix'), 0, 0, tiled=True)]
    pallas_call x0 -> x6, Pallas kernels: none -> 9.53 us  [the longest x1 6.3 us: on_device(): pl.pallas_call(functools.partial(prepare_kernel, stack), out_shape=[f32(c...]
    ppermute x8 -> x11, waiting for transfers between devices: 10 us -> 1.46 us  [the longest x9 1.29 us: hop(): return lax.ppermute(comp, ('section', 'pix'), pairs)]
    slice x8 -> x0, local copies, waits for them, and re-layouts: 3.65 us -> none  [the longest x1 1.53 us: on_device(): dates_all[:, rnd * dates:(rnd + 1) * dates]]
  transfers between devices with their start and end apart: 10 -> 12, of which waited for: 6 -> 3; matrix products, arithmetic and copies ran while one was open for 4% -> 1% of each run, Pallas kernels for 0% -> 0%
where the time goes in v1:
time: 61.2 us; the launch traced here: 60.8 us
  starting transfers between devices  37.3 us (61%)
  Pallas kernels  9.53 us (16%)
  waiting for transfers between devices  9.04 us (15%)
  local copies, waits for them, and re-layouts  3.4 us (6%)
  between operations  1.51 us (2%)
    all_to_all x1, starting transfers between devices, on_device(): got = lax.all_to_all(sent, ('section', 'pix'), 0, 0, tiled=True)  20.4 us
    ppermute x9, starting transfers between devices, hop(): return lax.ppermute(comp, ('section', 'pix'), pairs)  12.6 us
    all_to_all x1, waiting for transfers between devices, on_device(): got = lax.all_to_all(sent, ('section', 'pix'), 0, 0, tiled=True)  7.58 us
    pallas_call x1, Pallas kernels, on_device(): pl.pallas_call(functools.partial(prepare_kernel, stack), out_shape=[f32(c...  6.3 us
    ppermute x1, starting transfers between devices, on_device(): low = lax.ppermute(slc[:, :, pixels - reach:], 'pix', forward)  3.04 us
    unnamed x5, local copies, waits for them, and re-layouts  2.63 us
    pallas_call x3, Pallas kernels, on_device(): pl.pallas_call(functools.partial(round_kernel, rnd, stack), out_shape=[f3...  1.65 us
    ppermute x1, starting transfers between devices, on_device(): high = lax.ppermute(slc[:, :, :reach], 'pix', backward)  1.29 us
  transfers between devices with their start and end apart: 12, of which 3 were waited for; matrix products, arithmetic and copies ran while one was open for 1% of the time, Pallas kernels for 0%

profile of v1, /device:TPU:0, one launch (start us, length us, event | category | flops | bytes accessed | tf_op | source)
XLA Modules:
  0.0 60.8 jit_solution(15624779762793073154)
XLA Ops:
  0.6 0.9 %copy.5.own_ref = f32[2,50,256]{2,1,0:T(8,128)S(1)} copy(f32[2,50,256]{2,0,1:T(2,128)} %param.3) | data formatting | bytes 204800 | tf_op args[0]
  1.5 1.3 %collective-permute-start.1 = (f32[2,50,256]{2,1,0:T(8,128)S(1)}, f32[2,50,256]{2,1,0:T(8,128)S(1)}, u32[]{:S(2)}, u32[]{:S(2)}) collective-permute-start(f32[2,50,256]{2,1,0:T(8,128)S(1)} %copy.5.own_ref), channel_id=1, source_target_pairs={{1,0},{2,1},{3,2},{4,3},{5,4},{6,5},{7,6},{9,8},{10,9},{11,10},{12... | collective-permute-start | bytes 307208 | tf_op jit(solution)/shard_map/ppermute | solution.py:400
  2.8 3.0 %collective-permute-start = (f32[2,50,256]{2,1,0:T(8,128)S(1)}, f32[2,50,256]{2,1,0:T(8,128)S(1)}, u32[]{:S(2)}, u32[]{:S(2)}) collective-permute-start(f32[2,50,256]{2,1,0:T(8,128)S(1)} %copy.5.own_ref), channel_id=1, source_target_pairs={{0,1},{1,2},{2,3},{3,4},{4,5},{5,6},{6,7},{8,9},{9,10},{10,11},{11... | collective-permute-start | bytes 307208 | tf_op jit(solution)/shard_map/ppermute | solution.py:399
  6.5 0.0 copy-start
  6.6 0.1 stack.23.base_ref.where_ref.at_ref
  6.7 0.0 collective-permute-done.1.high_ref
  6.7 0.2 collective-permute-done.low_ref
  6.8 0.4 copy-done
  7.3 6.3 %prepare.1 = (f32[15,56,256]{2,1,0:T(8,128)S(1)}, f32[15,56,256]{2,1,0:T(8,128)S(1)}, f32[16,2,16,128]{3,2,1,0:T(8,128)S(1)}, f32[16,2,16,128]{3,2,1,0:T(8,128)S...) custom-call(s32[6]{0:T(128)S(1)} %stack.23.base_ref.where_ref.at_ref, ...), custom_call_target="tpu_custom_call" | custom-call | tf_op jit(solution)/shard_map/prepare/pallas_call | solution.py:406
  13.6 0.7 %collective-permute-start.4 = (f32[2,256]{1,0:T(2,128)S(1)}, f32[2,256]{1,0:T(2,128)S(1)}, u32[]{:S(2)}, u32[]{:S(2)}) collective-permute-start(f32[2,256]{1,0:T(2,128)S(1)} %get-tuple-element.23), channel_id=1, source_target_pairs={{1,8},{2,9},{3,10},{4,11},{5,12},{6,13},{7,14}} | collective-permute-start | bytes 6152 | tf_op jit(solution)/shard_map/ppermute | solution.py:431
  14.2 5.5 %collective-permute-start.3 = (f32[2,256]{1,0:T(2,128)S(1)}, f32[2,256]{1,0:T(2,128)S(1)}, u32[]{:S(2)}, u32[]{:S(2)}) collective-permute-start(f32[2,256]{1,0:T(2,128)S(1)} %get-tuple-element.23), channel_id=1, source_target_pairs={{0,8},{1,9},{2,10},{3,11},{4,12},{5,13},{6,14},{7,15}} | collective-permute-start | bytes 6152 | tf_op jit(solution)/shard_map/ppermute | solution.py:431
  19.7 2.5 %collective-permute-start.2 = (f32[2,256]{1,0:T(2,128)S(1)}, f32[2,256]{1,0:T(2,128)S(1)}, u32[]{:S(2)}, u32[]{:S(2)}) collective-permute-start(f32[2,256]{1,0:T(2,128)S(1)} %get-tuple-element.23), channel_id=1, source_target_pairs={{0,9},{1,10},{2,11},{3,12},{4,13},{5,14},{6,15}} | collective-permute-start | bytes 6152 | tf_op jit(solution)/shard_map/ppermute | solution.py:431
  22.2 0.0 collective-permute-done.4.high_ref
  22.2 0.0 collective-permute-done.3.own_ref
  22.2 1.3 %collective-permute-done.2.low_ref = f32[2,256]{1,0:T(2,128)S(1)} collective-permute-done((f32[2,256]{1,0:T(2,128)S(1)}, f32[2,256]{1,0:T(2,128)S(1)}, u32[]{:S(2)}, u32[]{:S(2)}) %collective-permute-start.2) | collective-permute-done | bytes 2080 | tf_op jit(solution)/shard_map/ppermute | solution.py:431
  23.5 0.5 round1.1
  24.1 0.7 %collective-permute-start.7 = (f32[2,256]{1,0:T(2,128)S(1)}, f32[2,256]{1,0:T(2,128)S(1)}, u32[]{:S(2)}, u32[]{:S(2)}) collective-permute-start(f32[2,256]{1,0:T(2,128)S(1)} %get-tuple-element.29), channel_id=1, source_target_pairs={{9,16},{10,17},{11,18},{12,19},{13,20},{14,21},{15,22}} | collective-permute-start | bytes 6152 | tf_op jit(solution)/shard_map/ppermute | solution.py:431
  24.7 0.7 %collective-permute-start.6 = (f32[2,256]{1,0:T(2,128)S(1)}, f32[2,256]{1,0:T(2,128)S(1)}, u32[]{:S(2)}, u32[]{:S(2)}) collective-permute-start(f32[2,256]{1,0:T(2,128)S(1)} %get-tuple-element.29), channel_id=1, source_target_pairs={{8,16},{9,17},{10,18},{11,19},{12,20},{13,21},{14,22},{15,23}} | collective-permute-start | bytes 6152 | tf_op jit(solution)/shard_map/ppermute | solution.py:431
  25.4 0.7 %collective-permute-start.5 = (f32[2,256]{1,0:T(2,128)S(1)}, f32[2,256]{1,0:T(2,128)S(1)}, u32[]{:S(2)}, u32[]{:S(2)}) collective-permute-start(f32[2,256]{1,0:T(2,128)S(1)} %get-tuple-element.29), channel_id=1, source_target_pairs={{8,17},{9,18},{10,19},{11,20},{12,21},{13,22},{14,23}} | collective-permute-start | bytes 6152 | tf_op jit(solution)/shard_map/ppermute | solution.py:431
  26.1 0.0 collective-permute-done.7.high_ref
  26.1 0.0 collective-permute-done.6.own_ref
  26.1 0.0 collective-permute-done.5.low_ref
  26.1 0.6 round2.1
  26.7 0.7 %collective-permute-start.10 = (f32[2,256]{1,0:T(2,128)S(1)}, f32[2,256]{1,0:T(2,128)S(1)}, u32[]{:S(2)}, u32[]{:S(2)}) collective-permute-start(f32[2,256]{1,0:T(2,128)S(1)} %get-tuple-element.32), channel_id=1, source_target_pairs={{17,24},{18,25},{19,26},{20,27},{21,28},{22,29},{23,30}} | collective-permute-start | bytes 6152 | tf_op jit(solution)/shard_map/ppermute | solution.py:431
  27.3 0.7 %collective-permute-start.9 = (f32[2,256]{1,0:T(2,128)S(1)}, f32[2,256]{1,0:T(2,128)S(1)}, u32[]{:S(2)}, u32[]{:S(2)}) collective-permute-start(f32[2,256]{1,0:T(2,128)S(1)} %get-tuple-element.32), channel_id=1, source_target_pairs={{16,24},{17,25},{18,26},{19,27},{20,28},{21,29},{22,30},{23,31}} | collective-permute-start | bytes 6152 | tf_op jit(solution)/shard_map/ppermute | solution.py:431
  28.0 0.7 %collective-permute-start.8 = (f32[2,256]{1,0:T(2,128)S(1)}, f32[2,256]{1,0:T(2,128)S(1)}, u32[]{:S(2)}, u32[]{:S(2)}) collective-permute-start(f32[2,256]{1,0:T(2,128)S(1)} %get-tuple-element.32), channel_id=1, source_target_pairs={{16,25},{17,26},{18,27},{19,28},{20,29},{21,30},{22,31}} | collective-permute-start | bytes 6152 | tf_op jit(solution)/shard_map/ppermute | solution.py:431
  28.7 0.0 collective-permute-done.10.high_ref
  28.7 0.0 collective-permute-done.9.own_ref
  28.7 0.0 collective-permute-done.8.low_ref
  28.7 0.6 round3.1
  29.3 0.9 %vectors.1 = (f32[2,50,256]{2,1,0:T(8,128)S(1)}, f32[8,128]{1,0:T(8,128)S(1)}) custom-call(s32[6]{0:T(128)S(1)} %stack.23.base_ref.where_ref.at_ref, f32[15,56,256]{2,1,0:T(8,128)S(1)} %get-tuple-element.21.zr_ref, f32[15,56,256]{2,1,0:T(8,128)S(1)} %get-tuple-element.22.zi_ref, f32[2,2,16,128]{3,2,1,0:T(8,128)S(1)} %get-tuple-element.35.beta_ref, ...), custom_call_target="tpu_custom_call" | custom-call | tf_op jit(solution)/shard_map/vectors/pallas_call | solution.py:444
  30.2 0.7 %broadcast_in_dim.4 = f32[32,8,128]{2,1,0:T(8,128)} broadcast(f32[8,128]{1,0:T(8,128)S(1)} %get-tuple-element.38), dimensions={1,2} | broadcast | bytes 135168 | tf_op jit(solution)/shard_map/broadcast_in_dim | solution.py:454
  30.9 20.4 %all-to-all-start = ((f32[32,8,128]{2,1,0:T(8,128)}), f32[32,8,128]{2,1,0:T(8,128)S(1)}, u32[]{:S(2)}, u32[]{:S(2)}) async-start(f32[32,8,128]{2,1,0:T(8,128)} %broadcast_in_dim.4), calls=%async_computation | async-start | bytes 262144 | tf_op jit(solution)/shard_map/all_to_all | solution.py:455
  51.3 0.6 copy.9
  51.9 7.6 %all-to-all-done.got_ref = f32[32,8,128]{2,1,0:T(8,128)S(1)} async-done(((f32[32,8,128]{2,1,0:T(8,128)}), f32[32,8,128]{2,1,0:T(8,128)S(1)}, u32[]{:S(2)}, u32[]{:S(2)}) %all-to-all-start) | async-done | bytes 131104 | tf_op jit(solution)/shard_map/all_to_all | solution.py:455
  59.4 0.7 %finish.1 = f32[2,50,256]{2,1,0:T(8,128)S(1)} custom-call(s32[6]{0:T(128)S(1)} %stack.23.base_ref.where_ref.at_ref, f32[2,50,256]{2,1,0:T(8,128)S(1)} %get-tuple-element.37.vec_ref, f32[32,8,128]{2,1,0:T(8,128)S(1)} %all-to-all-done.got_ref), custom_call_target="tpu_custom_call" | custom-call | tf_op jit(solution)/shard_map/finish/pallas_call | solution.py:456
  60.1 0.7 %copy.8 = f32[2,50,256]{2,0,1:T(2,128)} copy(f32[2,50,256]{2,1,0:T(8,128)S(1)} %finish.1) | data formatting | bytes 204800
Async XLA Ops:
  1.5 5.1 %collective-permute-start.1 = (f32[2,50,256]{2,1,0:T(8,128)S(1)}, f32[2,50,256]{2,1,0:T(8,128)S(1)}, u32[]{:S(2)}, u32[]{:S(2)}) collective-permute-start(f32[2,50,256]{2,1,0:T(8,128)S(1)} %copy.5.own_ref), channel_id=1, source_target_pairs={{1,0},{2,1},{3,2},{4,3},{5,4},{6,5},{7,6},{9,8},{10,9},{11,10},{12... | collective-permute-start | bytes 307208 | tf_op jit(solution)/shard_map/ppermute | solution.py:400
  2.8 4.0 %collective-permute-start = (f32[2,50,256]{2,1,0:T(8,128)S(1)}, f32[2,50,256]{2,1,0:T(8,128)S(1)}, u32[]{:S(2)}, u32[]{:S(2)}) collective-permute-start(f32[2,50,256]{2,1,0:T(8,128)S(1)} %copy.5.own_ref), channel_id=1, source_target_pairs={{0,1},{1,2},{2,3},{3,4},{4,5},{5,6},{6,7},{8,9},{9,10},{10,11},{11... | collective-permute-start | bytes 307208 | tf_op jit(solution)/shard_map/ppermute | solution.py:399
  6.5 0.7 %copy-start = (s32[15,256]{1,0:T(8,128)S(1)}, s32[15,256]{1,0:T(8,128)}, u32[]{:S(2)}) copy-start(s32[15,256]{1,0:T(8,128)} %idx_ref.7) | copy-start | bytes 46084
  13.6 8.7 %collective-permute-start.4 = (f32[2,256]{1,0:T(2,128)S(1)}, f32[2,256]{1,0:T(2,128)S(1)}, u32[]{:S(2)}, u32[]{:S(2)}) collective-permute-start(f32[2,256]{1,0:T(2,128)S(1)} %get-tuple-element.23), channel_id=1, source_target_pairs={{1,8},{2,9},{3,10},{4,11},{5,12},{6,13},{7,14}} | collective-permute-start | bytes 6152 | tf_op jit(solution)/shard_map/ppermute | solution.py:431
  14.2 8.0 %collective-permute-start.3 = (f32[2,256]{1,0:T(2,128)S(1)}, f32[2,256]{1,0:T(2,128)S(1)}, u32[]{:S(2)}, u32[]{:S(2)}) collective-permute-start(f32[2,256]{1,0:T(2,128)S(1)} %get-tuple-element.23), channel_id=1, source_target_pairs={{0,8},{1,9},{2,10},{3,11},{4,12},{5,13},{6,14},{7,15}} | collective-permute-start | bytes 6152 | tf_op jit(solution)/shard_map/ppermute | solution.py:431
  19.7 3.8 %collective-permute-start.2 = (f32[2,256]{1,0:T(2,128)S(1)}, f32[2,256]{1,0:T(2,128)S(1)}, u32[]{:S(2)}, u32[]{:S(2)}) collective-permute-start(f32[2,256]{1,0:T(2,128)S(1)} %get-tuple-element.23), channel_id=1, source_target_pairs={{0,9},{1,10},{2,11},{3,12},{4,13},{5,14},{6,15}} | collective-permute-start | bytes 6152 | tf_op jit(solution)/shard_map/ppermute | solution.py:431
  24.1 2.0 %collective-permute-start.7 = (f32[2,256]{1,0:T(2,128)S(1)}, f32[2,256]{1,0:T(2,128)S(1)}, u32[]{:S(2)}, u32[]{:S(2)}) collective-permute-start(f32[2,256]{1,0:T(2,128)S(1)} %get-tuple-element.29), channel_id=1, source_target_pairs={{9,16},{10,17},{11,18},{12,19},{13,20},{14,21},{15,22}} | collective-permute-start | bytes 6152 | tf_op jit(solution)/shard_map/ppermute | solution.py:431
  24.7 1.4 %collective-permute-start.6 = (f32[2,256]{1,0:T(2,128)S(1)}, f32[2,256]{1,0:T(2,128)S(1)}, u32[]{:S(2)}, u32[]{:S(2)}) collective-permute-start(f32[2,256]{1,0:T(2,128)S(1)} %get-tuple-element.29), channel_id=1, source_target_pairs={{8,16},{9,17},{10,18},{11,19},{12,20},{13,21},{14,22},{15,23}} | collective-permute-start | bytes 6152 | tf_op jit(solution)/shard_map/ppermute | solution.py:431
  25.4 0.7 %collective-permute-start.5 = (f32[2,256]{1,0:T(2,128)S(1)}, f32[2,256]{1,0:T(2,128)S(1)}, u32[]{:S(2)}, u32[]{:S(2)}) collective-permute-start(f32[2,256]{1,0:T(2,128)S(1)} %get-tuple-element.29), channel_id=1, source_target_pairs={{8,17},{9,18},{10,19},{11,20},{12,21},{13,22},{14,23}} | collective-permute-start | bytes 6152 | tf_op jit(solution)/shard_map/ppermute | solution.py:431
  26.7 2.0 %collective-permute-start.10 = (f32[2,256]{1,0:T(2,128)S(1)}, f32[2,256]{1,0:T(2,128)S(1)}, u32[]{:S(2)}, u32[]{:S(2)}) collective-permute-start(f32[2,256]{1,0:T(2,128)S(1)} %get-tuple-element.32), channel_id=1, source_target_pairs={{17,24},{18,25},{19,26},{20,27},{21,28},{22,29},{23,30}} | collective-permute-start | bytes 6152 | tf_op jit(solution)/shard_map/ppermute | solution.py:431
  27.3 1.4 %collective-permute-start.9 = (f32[2,256]{1,0:T(2,128)S(1)}, f32[2,256]{1,0:T(2,128)S(1)}, u32[]{:S(2)}, u32[]{:S(2)}) collective-permute-start(f32[2,256]{1,0:T(2,128)S(1)} %get-tuple-element.32), channel_id=1, source_target_pairs={{16,24},{17,25},{18,26},{19,27},{20,28},{21,29},{22,30},{23,31}} | collective-permute-start | bytes 6152 | tf_op jit(solution)/shard_map/ppermute | solution.py:431
  28.0 0.7 %collective-permute-start.8 = (f32[2,256]{1,0:T(2,128)S(1)}, f32[2,256]{1,0:T(2,128)S(1)}, u32[]{:S(2)}, u32[]{:S(2)}) collective-permute-start(f32[2,256]{1,0:T(2,128)S(1)} %get-tuple-element.32), channel_id=1, source_target_pairs={{16,25},{17,26},{18,27},{19,28},{20,29},{21,30},{22,31}} | collective-permute-start | bytes 6152 | tf_op jit(solution)/shard_map/ppermute | solution.py:431
  30.9 28.6 %all-to-all-start = ((f32[32,8,128]{2,1,0:T(8,128)}), f32[32,8,128]{2,1,0:T(8,128)S(1)}, u32[]{:S(2)}, u32[]{:S(2)}) async-start(f32[32,8,128]{2,1,0:T(8,128)} %broadcast_in_dim.4), calls=%async_computation | async-start | bytes 262144 | tf_op jit(solution)/shard_map/all_to_all | solution.py:455

commit v2 on v1

--- a/solution.py
+++ b/solution.py
@@ -28,6 +28,10 @@
     return pltpu.CompilerParams(vmem_limit_bytes=20 * 1024 * 1024)
 
 
+def cost(flops):
+    return pl.CostEstimate(flops=flops, bytes_accessed=0, transcendentals=0)
+
+
 def up(n, m):
     return -(-n // m) * m
 
@@ -45,27 +49,29 @@
     return pl.ds(h * LANES, LANES)
 
 
-def gather(base, idx_ref, pieces, xs_ref, hl_ref, zr_ref, zi_ref):
+def gather(start, idx_ref, pieces, xs_ref, hl_ref, zr_ref, zi_ref, add):
     count, rows, pixels = zr_ref.shape
-    dates = pieces[0].shape[1]
     xs_ref[...] = jnp.zeros_like(xs_ref)
     at = 0
-    for piece in pieces:
-        width = piece.shape[2]
+    place = []
+    for piece, first in pieces:
+        dates, _, width = piece.shape
         for c in range(2):
-            xs_ref[pl.ds(c * rows, dates), pl.ds(at, width)] = piece[c]
+            xs_ref[pl.ds(c * rows, dates), pl.ds(at, width)] = piece[:, c]
+        place.append(lax.broadcasted_iota(jnp.int32, (width, pixels), 0) + first)
         at += width
+    place = jnp.concatenate(place, axis=0)
     high = xs_ref[...].astype(jnp.bfloat16)
     hl_ref[0 : 2 * rows] = high
     hl_ref[2 * rows : 4 * rows] = (xs_ref[...] - high.astype(jnp.float32)).astype(jnp.bfloat16)
-    window = xs_ref.shape[1]
-    place = lax.broadcasted_iota(jnp.int32, (window, pixels), 0)
     for k in range(count):
-        near = idx_ref[k : k + 1, :] - base
+        near = idx_ref[k : k + 1, :] - start
         hot = jnp.where(place == near, 1.0, 0.0).astype(jnp.bfloat16)
         got = jnp.dot(hl_ref[...], hot, preferred_element_type=jnp.float32)
-        zr_ref[k] = got[0:rows] + got[2 * rows : 3 * rows]
-        zi_ref[k] = got[rows : 2 * rows] + got[3 * rows : 4 * rows]
+        zr = got[0:rows] + got[2 * rows : 3 * rows]
+        zi = got[rows : 2 * rows] + got[3 * rows : 4 * rows]
+        zr_ref[k] = zr_ref[k] + zr if add else zr
+        zi_ref[k] = zi_ref[k] + zi if add else zi
 
 
 def scale_dates(zr_ref, zi_ref):
@@ -87,25 +93,24 @@
     row = lax.broadcasted_iota(jnp.int32, (SUB, LANES), 0)
     for step in (4, 2, 1):
         low = jnp.bitwise_and(row, step) == 0
+        other = jnp.bitwise_xor(row, step)
         n = len(parts) // 2
         out = []
         for i in range(n):
             a, b = parts[i], parts[i + n]
-            far = jnp.where(low, pltpu.roll(a, SUB - step, 0), pltpu.roll(b, step, 0))
+            far = jnp.take_along_axis(jnp.where(low, b, a), other, axis=0, mode="promise_in_bounds")
             out.append(jnp.where(low, a, b) + far)
         parts = out
     return parts[0]
 
 
-def gram(pair_ref, zr_ref, zi_ref, xs_ref, own_at, gr_ref, gi_ref, sum_ref, block=3):
+def gram(pair_ref, zr_ref, zi_ref, own_ref, gr_ref, gi_ref, sum_ref, block=3):
     count, rows, pixels = zr_ref.shape
     zero = jnp.zeros((SUB, LANES), jnp.float32)
     for h in range(pixels // LANES):
-        here = pl.ds(own_at + h * LANES, LANES)
-
         def load(k, r):
             if k == count:
-                return (xs_ref[pl.ds(r, SUB), here], xs_ref[pl.ds(rows + r, SUB), here])
+                return (own_ref[pl.ds(r, SUB), half(h)], own_ref[pl.ds(rows + r, SUB), half(h)])
             return (zr_ref[k, pl.ds(r, SUB), half(h)], zi_ref[k, pl.ds(r, SUB), half(h)])
 
         for k0 in range(0, count, block):
@@ -119,18 +124,16 @@
                 acc = {}
                 for r in range(0, rows, SUB):
                     val = {n: load(n, r) for n in sorted({n for p in pairs for n in p})}
+                    minus = {k: val[k][0] - val[k][1] for k in {k for k, l in pairs if k != l}}
+                    plus = {l: val[l][0] + val[l][1] for l in {l for k, l in pairs if k != l}}
                     for k, l in pairs:
-                        ar, ai = val[k]
-                        br, bi = val[l]
-                        re = ar * br + ai * bi
-                        im = None if k == l else ar * bi - ai * br
-                        if r:
-                            re = acc[k, l][0] + re
-                            im = None if k == l else acc[k, l][1] + im
-                        acc[k, l] = (re, im)
+                        new = [val[k][0] * val[l][0], val[k][1] * val[l][1]]
+                        if k != l:
+                            new.append(minus[k] * plus[l])
+                        acc[k, l] = [x + y for x, y in zip(acc[k, l], new)] if r else new
                 for k, l in pairs:
-                    pair_ref[0, l, k] = acc[k, l][0]
-                    pair_ref[1, l, k] = zero if k == l else acc[k, l][1]
+                    pair_ref[0, l, k] = acc[k, l][0] + acc[k, l][1]
+                    pair_ref[1, l, k] = zero if k == l else acc[k, l][2] - (acc[k, l][0] - acc[k, l][1])
         for c, g_ref in ((0, gr_ref), (1, gi_ref)):
             for l in range(count + 1):
                 for kt in range(KP // SUB):
@@ -236,20 +239,28 @@
         state_ref[5:8, half(h)] = jnp.zeros((3, LANES), jnp.float32)
 
 
-def prepare_kernel(
-    stack, base_ref, idx_ref, low_ref, own_ref, high_ref,
-    zr_ref, zi_ref, gr_ref, gi_ref, sum_ref, beta_ref, state_ref, comp_ref,
-    xs_ref, hl_ref, pair_ref,
-):
-    gather(base_ref[0], idx_ref, (low_ref, own_ref, high_ref), xs_ref, hl_ref, zr_ref, zi_ref)
-    scale_dates(zr_ref, zi_ref)
-    gram(pair_ref, zr_ref, zi_ref, xs_ref, low_ref.shape[2], gr_ref, gi_ref, sum_ref)
-    count = zr_ref.shape[0]
-    halves = gr_ref.shape[1]
-    hr = [gr_ref[count, h] for h in range(halves)]
-    hi = [gi_ref[count, h] for h in range(halves)]
-    solve(None, gr_ref.at[0:count], gi_ref.at[0:count], hr, hi, sum_ref, stack, beta_ref, state_ref)
-    comp_ref[...] = state_ref[0:2]
+def own_kernel(at_ref, idx_ref, slc_ref, zr_ref, zi_ref, own_ref, hl_ref):
+    gather(at_ref[6], idx_ref, ((slc_ref, 0),), own_ref, hl_ref, zr_ref, zi_ref, False)
+
+
+def prepare_kernel(stack, first, at_ref, idx_ref, low_ref, high_ref, own_ref, *refs):
+    refs = refs[2 if first else 7 :]
+    zr_ref, zi_ref, gr_ref, gi_ref, sum_ref, beta_ref, state_ref = refs[:7]
+    xs_ref, hl_ref, pair_ref = refs[-3:]
+
+    @pl.when(at_ref[1] == 0 if first else at_ref[1] != 0)
+    def _():
+        count, _, pixels = zr_ref.shape
+        pieces = ((low_ref, -low_ref.shape[2]), (high_ref, pixels))
+        gather(at_ref[6], idx_ref, pieces, xs_ref, hl_ref, zr_ref, zi_ref, True)
+        scale_dates(zr_ref, zi_ref)
+        gram(pair_ref, zr_ref, zi_ref, own_ref, gr_ref, gi_ref, sum_ref)
+        if first:
+            halves = gr_ref.shape[1]
+            hr = [gr_ref[count, h] for h in range(halves)]
+            hi = [gi_ref[count, h] for h in range(halves)]
+            solve(None, gr_ref.at[0:count], gi_ref.at[0:count], hr, hi, sum_ref, stack, beta_ref, state_ref)
+            refs[7][...] = state_ref[0:2]
 
 
 def lane_take(x, i):
@@ -330,22 +341,24 @@
             vec_ref[c, :, half(h)] = whole[0:dates]
             wide = jnp.concatenate([whole, jnp.zeros((up(rows, LANES) - rows, LANES), jnp.float32)], axis=0)
             turned_ref[c, half(h)] = jnp.transpose(wide)
-    slot_ref[...] = jnp.zeros_like(slot_ref)
+    slot = [jnp.zeros((1, LANES), jnp.float32)] * slot_ref.shape[1]
     lane = lax.broadcasted_iota(jnp.int32, (1, LANES), 1)
     halves = pixels // LANES
     for c in range(2):
         for h in range(halves):
-            slot_ref[c * halves + h : c * halves + h + 1] = state_ref[2 + c : 3 + c, half(h)]
-        slot_ref[2 * halves + c : 2 * halves + c + 1] = turned_ref[c, pl.ds(local, 1), :]
+            slot[c * halves + h] = state_ref[2 + c : 3 + c, half(h)]
+        slot[2 * halves + c] = turned_ref[c, pl.ds(local, 1), :]
         picked = jnp.zeros((1, LANES), jnp.float32)
         for h in range(halves):
             picked = picked + jnp.where(lane == local - h * LANES, state_ref[2 + c : 3 + c, half(h)], 0.0)
-        slot_ref[2 * halves + 2 + c : 2 * halves + 3 + c] = jnp.broadcast_to(
-            jnp.sum(picked, axis=1, keepdims=True), (1, LANES)
-        )
-
-
-def finish_kernel(sections, at_ref, vec_ref, got_ref, out_ref):
+        slot[2 * halves + 2 + c] = jnp.broadcast_to(jnp.sum(picked, axis=1, keepdims=True), (1, LANES))
+    slot = jnp.concatenate(slot, axis=0)
+    for n in range(slot_ref.shape[0]):
+        slot_ref[n] = slot
+
+
+def finish_kernel(sections, at_ref, vec_ref, got_ref, comp_ref, out_ref, small_ref):
+    small_ref[:, 0] = comp_ref[...]
     dates, pixels = vec_ref.shape[1:]
     section, mine, root, blocks = at_ref[1], at_ref[3], at_ref[4], at_ref[5]
     halves = pixels // LANES
@@ -376,12 +389,13 @@
         wi = ur * datum[h][1] - ui * datum[h][0]
         vr = vec_ref[0, :, half(h)]
         vi = vec_ref[1, :, half(h)]
-        out_ref[0, :, half(h)] = vr * wr - vi * wi
-        out_ref[1, :, half(h)] = vr * wi + vi * wr
+        out_ref[:, 0, half(h)] = vr * wr - vi * wi
+        out_ref[:, 1, half(h)] = vr * wi + vi * wr
 
 
 def on_device(slc, neighbours, reference_pixel):
     dates, pixels = slc.shape[1:]
+    slc = jnp.transpose(slc, (1, 0, 2))
     count = neighbours.shape[0]
     reach = min(pixels, REACH_LIMIT)
     sections = lax.axis_size("section")
@@ -391,7 +405,6 @@
     stack = dates + 1
     halves = pixels // LANES
     rows = up(dates, SUB)
-    window = pixels + 2 * reach
     base = block * pixels - reach
 
     forward = [(i, i + 1) for i in range(blocks - 1)]
@@ -401,25 +414,43 @@
 
     root = reference_pixel[0] // pixels
     local = reference_pixel[0] - root * pixels
-    at = jnp.stack([base, section, local, block, root, jnp.int32(blocks)]).astype(jnp.int32)
-
-    zr, zi, gr, gi, sums, beta, state, comp = pl.pallas_call(
-        functools.partial(prepare_kernel, stack),
-        out_shape=[
-            f32(count, rows, pixels), f32(count, rows, pixels),
-            f32(count + 1, halves, KP, LANES), f32(count + 1, halves, KP, LANES),
-            f32(2, halves, KP, LANES), f32(2, halves, KP, LANES), f32(SUB, pixels), f32(2, pixels),
-        ],
-        in_specs=[SMEM] + [VMEM] * 4,
-        out_specs=[VMEM] * 8,
-        scratch_shapes=[
-            pltpu.VMEM((2 * rows, window), jnp.float32),
-            pltpu.VMEM((4 * rows, window), jnp.bfloat16),
-            pltpu.VMEM((2, count + 1, count, SUB, LANES), jnp.float32),
-        ],
+    at = jnp.stack([base, section, local, block, root, jnp.int32(blocks), block * pixels]).astype(jnp.int32)
+
+    made = [
+        f32(count, rows, pixels), f32(count, rows, pixels),
+        f32(count + 1, halves, KP, LANES), f32(count + 1, halves, KP, LANES),
+        f32(2, halves, KP, LANES), f32(2, halves, KP, LANES), f32(SUB, pixels), f32(2, pixels),
+    ]
+    zr, zi, own = pl.pallas_call(
+        own_kernel,
+        out_shape=made[:2] + [f32(2 * rows, pixels)],
+        in_specs=[SMEM, VMEM, VMEM],
+        out_specs=[VMEM] * 3,
+        scratch_shapes=[pltpu.VMEM((4 * rows, pixels), jnp.bfloat16)],
         compiler_params=params(),
-        name="prepare",
-    )(at, neighbours, low, slc, high)
+        cost_estimate=cost(2 * 4 * rows * pixels * pixels * count),
+        name="own",
+    )(at, neighbours, slc)
+
+    def prepare(first, carried):
+        return pl.pallas_call(
+            functools.partial(prepare_kernel, stack, first),
+            out_shape=made[: 8 if first else 7],
+            in_specs=[SMEM] + [VMEM] * (4 + len(carried)),
+            out_specs=[VMEM] * (8 if first else 7),
+            scratch_shapes=[
+                pltpu.VMEM((2 * rows, 2 * reach), jnp.float32),
+                pltpu.VMEM((4 * rows, 2 * reach), jnp.bfloat16),
+                pltpu.VMEM((2, count + 1, count, SUB, LANES), jnp.float32),
+            ],
+            input_output_aliases={5 + n: n for n in range(len(carried))},
+            compiler_params=params(),
+            cost_estimate=cost(50 * 12 * rows * reach * pixels * count),
+            name="prepare" + ("0" if first else "n"),
+        )(at, neighbours, low, high, own, *carried)
+
+    *made_0, comp = prepare(True, (zr, zi))
+    zr, zi, gr, gi, sums, beta, state = prepare(False, made_0)
 
     for rnd in range(1, sections):
         def hop(shift):
@@ -440,28 +471,27 @@
             name=f"round{rnd}",
         )(at, neighbours, hop(1)[:, pixels - reach :], hop(0), hop(-1)[:, :reach], gr, gi, sums, beta, state)
 
+    devices = sections * blocks
     slot_rows = up(2 * halves + 4, SUB)
-    vec, slot = pl.pallas_call(
+    vec, sent = pl.pallas_call(
         vector_kernel,
-        out_shape=[f32(2, dates, pixels), f32(slot_rows, LANES)],
+        out_shape=[f32(2, dates, pixels), f32(devices, slot_rows, LANES)],
         in_specs=[SMEM] + [VMEM] * 4,
         out_specs=[VMEM] * 2,
         scratch_shapes=[pltpu.VMEM((2, pixels, LANES), jnp.float32)],
         compiler_params=params(),
         name="vectors",
     )(at, zr, zi, beta, state)
-    devices = sections * blocks
-    sent = jnp.broadcast_to(slot[None], (devices, slot_rows, LANES))
     got = lax.all_to_all(sent, ("section", "pix"), 0, 0, tiled=True)
-    out = pl.pallas_call(
+    out, small = pl.pallas_call(
         functools.partial(finish_kernel, sections),
-        out_shape=f32(2, dates, pixels),
-        in_specs=[SMEM] + [VMEM] * 2,
-        out_specs=VMEM,
+        out_shape=[f32(dates, 2, pixels), f32(2, 1, pixels)],
+        in_specs=[SMEM] + [VMEM] * 3,
+        out_specs=[VMEM] * 2,
         compiler_params=params(),
         name="finish",
-    )(at, vec, got)
-    return (out, comp[:, None, :])
+    )(at, vec, got, comp)
+    return (jnp.transpose(out, (1, 0, 2)), small)
 
 
 def solution(mesh):

time: 61.2 us -> 56.7 us (0.926)
  blocking collectives: 0 us -> 29.4 us
  starting transfers between devices: 37.3 us -> 11.5 us
  waiting for transfers between devices: 9.04 us -> 0.73 us
  Pallas kernels: 9.53 us -> 11.5 us
  local copies, waits for them, and re-layouts: 3.4 us -> 1.59 us
    all_to_all x0 -> x1, blocking collectives: none -> 29.4 us  [on_device(): got = lax.all_to_all(sent, ('section', 'pix'), 0, 0, tiled=True)]
    all_to_all x1 -> x0, starting transfers between devices: 20.4 us -> none  [on_device(): got = lax.all_to_all(sent, ('section', 'pix'), 0, 0, tiled=True)]
    all_to_all x1 -> x0, waiting for transfers between devices: 7.58 us -> none  [on_device(): got = lax.all_to_all(sent, ('section', 'pix'), 0, 0, tiled=True)]
    ppermute x9, starting transfers between devices: 12.6 us -> 7.21 us  [hop(): return lax.ppermute(comp, ('section', 'pix'), pairs)]
    pallas_call x3 -> x5, Pallas kernels: 7.88 us -> 9.86 us  [the longest x2 6.35 us: prepare(): pl.pallas_call(functools.partial(prepare_kernel, stack, first), out_shape...]
    unnamed x5 -> x4, local copies, waits for them, and re-layouts: 2.63 us -> 1.51 us
    broadcast_in_dim x1 -> x0, local copies, waits for them, and re-layouts: 0.69 us -> none  [on_device(): sent = jnp.broadcast_to(slot[None], (devices, slot_rows, LANES))]
  transfers between devices with their start and end apart: 12 -> 11, of which waited for: 3 -> 1; matrix products, arithmetic and copies ran while one was open for 1% -> 0% of each run, Pallas kernels for 0% -> 3%
where the time goes in v2:
time: 56.7 us; the launch traced here: 56.3 us
  blocking collectives  29.4 us (52%)
  starting transfers between devices  11.5 us (20%)
  Pallas kernels  11.5 us (20%)
  local copies, waits for them, and re-layouts  1.59 us (3%)
  between operations  1.53 us (3%)
  waiting for transfers between devices  0.73 us (1%)
    all_to_all x1, blocking collectives, on_device(): got = lax.all_to_all(sent, ('section', 'pix'), 0, 0, tiled=True)  29.4 us
    ppermute x9, starting transfers between devices, hop(): return lax.ppermute(comp, ('section', 'pix'), pairs)  7.21 us
    pallas_call x2, Pallas kernels, prepare(): pl.pallas_call(functools.partial(prepare_kernel, stack, first), out_shape...  6.35 us
    ppermute x1, starting transfers between devices, on_device(): low = lax.ppermute(slc[:, :, pixels - reach:], 'pix', forward)  3.04 us
    pallas_call x3, Pallas kernels, on_device(): pl.pallas_call(functools.partial(round_kernel, rnd, stack), out_shape=[f3...  1.65 us
    unnamed x4, local copies, waits for them, and re-layouts  1.51 us
    pallas_call x1, Pallas kernels, on_device(): pl.pallas_call(functools.partial(finish_kernel, sections), out_shape=[f32...  1.37 us
    ppermute x1, starting transfers between devices, on_device(): high = lax.ppermute(slc[:, :, :reach], 'pix', backward)  1.29 us
  transfers between devices with their start and end apart: 11, of which 1 were waited for; matrix products, arithmetic and copies ran while one was open for 0% of the time, Pallas kernels for 3%

profile of v2, /device:TPU:0, one launch (start us, length us, event | category | flops | bytes accessed | tf_op | source)
XLA Modules:
  0.0 56.3 jit_solution(7250480745758899950)
XLA Ops:
  0.6 1.3 %collective-permute-start.1 = (f32[50,2,256]{2,1,0:T(2,128)}, f32[50,2,256]{2,1,0:T(2,128)S(1)}, u32[]{:S(2)}, u32[]{:S(2)}) collective-permute-start(f32[50,2,256]{2,1,0:T(2,128)} %bitcast.14), channel_id=1, source_target_pairs={{1,0},{2,1},{3,2},{4,3},{5,4},{6,5},{7,6},{9,8},{10,9},{11,10},{12... | collective-permute-start | bytes 307208 | tf_op jit(solution)/shard_map/ppermute | solution.py:413
  1.9 3.0 %collective-permute-start = (f32[50,2,256]{2,1,0:T(2,128)}, f32[50,2,256]{2,1,0:T(2,128)S(1)}, u32[]{:S(2)}, u32[]{:S(2)}) collective-permute-start(f32[50,2,256]{2,1,0:T(2,128)} %bitcast.15), channel_id=1, source_target_pairs={{0,1},{1,2},{2,3},{3,4},{4,5},{5,6},{6,7},{8,9},{9,10},{10,11},{11... | collective-permute-start | bytes 307208 | tf_op jit(solution)/shard_map/ppermute | solution.py:412
  5.6 0.0 copy-start
  5.7 0.1 stack.27.at_ref.where_ref
  5.7 0.6 %copy-done = s32[15,256]{1,0:T(8,128)S(1)} copy-done((s32[15,256]{1,0:T(8,128)S(1)}, s32[15,256]{1,0:T(8,128)}, u32[]{:S(2)}) %copy-start) | copy-done | bytes 15384
  6.4 0.0 copy-start.1
  6.4 0.9 %copy-done.1 = f32[2,50,256]{2,0,1:T(2,128)S(1)} copy-done((f32[2,50,256]{2,0,1:T(2,128)S(1)}, f32[2,50,256]{2,0,1:T(2,128)}, u32[]{:S(2)}) %copy-start.1) | copy-done | bytes 102424
  7.3 1.2 %own.1 = (f32[15,56,256]{2,1,0:T(8,128)S(1)}, f32[15,56,256]{2,1,0:T(8,128)S(1)}, f32[112,256]{1,0:T(8,128)S(1)}) custom-call(s32[7]{0:T(128)S(1)} %stack.27.at_ref.where_ref, s32[15,256]{1,0:T(8,128)S(1)} %copy-done, f32[50,2,256]{2,1,0:T(2,128)S(1)} %bitcast.16), custom_call_target="tpu_custom_call" | custom-call | flops 440401920 | tf_op jit(solution)/shard_map/own/pallas_call | solution.py:424
  8.5 0.0 collective-permute-done.1.high_ref
  8.5 0.0 collective-permute-done.low_ref
  8.5 5.8 %prepare0.1 = (f32[15,56,256]{2,1,0:T(8,128)S(1)}, f32[15,56,256]{2,1,0:T(8,128)S(1)}, f32[16,2,16,128]{3,2,1,0:T(8,128)S(1)}, f32[16,2,16,128]{3,2,1,0:T(8,128)...) custom-call(s32[7]{0:T(128)S(1)} %stack.27.at_ref.where_ref, ...), custom_call_target="tpu_custom_call", output_to_operand_aliasing={{0}: (5, {}), {1}: (6, {})} | custom-call | flops 33030144000 | tf_op jit(solution)/shard_map/prepare0/pallas_call | solution.py:436
  14.3 0.7 %collective-permute-start.4 = (f32[2,256]{1,0:T(2,128)S(1)}, f32[2,256]{1,0:T(2,128)S(1)}, u32[]{:S(2)}, u32[]{:S(2)}) collective-permute-start(f32[2,256]{1,0:T(2,128)S(1)} %get-tuple-element.45), channel_id=1, source_target_pairs={{1,8},{2,9},{3,10},{4,11},{5,12},{6,13},{7,14}} | collective-permute-start | bytes 6152 | tf_op jit(solution)/shard_map/ppermute | solution.py:462
  14.9 1.3 %collective-permute-start.3 = (f32[2,256]{1,0:T(2,128)S(1)}, f32[2,256]{1,0:T(2,128)S(1)}, u32[]{:S(2)}, u32[]{:S(2)}) collective-permute-start(f32[2,256]{1,0:T(2,128)S(1)} %get-tuple-element.45), channel_id=1, source_target_pairs={{0,8},{1,9},{2,10},{3,11},{4,12},{5,13},{6,14},{7,15}} | collective-permute-start | bytes 6152 | tf_op jit(solution)/shard_map/ppermute | solution.py:462
  16.2 1.3 %collective-permute-start.2 = (f32[2,256]{1,0:T(2,128)S(1)}, f32[2,256]{1,0:T(2,128)S(1)}, u32[]{:S(2)}, u32[]{:S(2)}) collective-permute-start(f32[2,256]{1,0:T(2,128)S(1)} %get-tuple-element.45), channel_id=1, source_target_pairs={{0,9},{1,10},{2,11},{3,12},{4,13},{5,14},{6,15}} | collective-permute-start | bytes 6152 | tf_op jit(solution)/shard_map/ppermute | solution.py:462
  17.5 0.6 preparen.1
  18.1 0.0 collective-permute-done.4.high_ref
  18.1 0.0 collective-permute-done.3.own_ref
  18.1 0.7 %collective-permute-done.2.low_ref = f32[2,256]{1,0:T(2,128)S(1)} collective-permute-done((f32[2,256]{1,0:T(2,128)S(1)}, f32[2,256]{1,0:T(2,128)S(1)}, u32[]{:S(2)}, u32[]{:S(2)}) %collective-permute-start.2) | collective-permute-done | bytes 2080 | tf_op jit(solution)/shard_map/ppermute | solution.py:462
  18.8 0.5 round1.1
  19.4 0.7 %collective-permute-start.7 = (f32[2,256]{1,0:T(2,128)S(1)}, f32[2,256]{1,0:T(2,128)S(1)}, u32[]{:S(2)}, u32[]{:S(2)}) collective-permute-start(f32[2,256]{1,0:T(2,128)S(1)} %get-tuple-element.51), channel_id=1, source_target_pairs={{9,16},{10,17},{11,18},{12,19},{13,20},{14,21},{15,22}} | collective-permute-start | bytes 6152 | tf_op jit(solution)/shard_map/ppermute | solution.py:462
  20.1 0.7 %collective-permute-start.6 = (f32[2,256]{1,0:T(2,128)S(1)}, f32[2,256]{1,0:T(2,128)S(1)}, u32[]{:S(2)}, u32[]{:S(2)}) collective-permute-start(f32[2,256]{1,0:T(2,128)S(1)} %get-tuple-element.51), channel_id=1, source_target_pairs={{8,16},{9,17},{10,18},{11,19},{12,20},{13,21},{14,22},{15,23}} | collective-permute-start | bytes 6152 | tf_op jit(solution)/shard_map/ppermute | solution.py:462
  20.7 0.7 %collective-permute-start.5 = (f32[2,256]{1,0:T(2,128)S(1)}, f32[2,256]{1,0:T(2,128)S(1)}, u32[]{:S(2)}, u32[]{:S(2)}) collective-permute-start(f32[2,256]{1,0:T(2,128)S(1)} %get-tuple-element.51), channel_id=1, source_target_pairs={{8,17},{9,18},{10,19},{11,20},{12,21},{13,22},{14,23}} | collective-permute-start | bytes 6152 | tf_op jit(solution)/shard_map/ppermute | solution.py:462
  21.4 0.0 collective-permute-done.7.high_ref
  21.4 0.0 collective-permute-done.6.own_ref
  21.4 0.0 collective-permute-done.5.low_ref
  21.4 0.6 round2.1
  22.0 0.7 %collective-permute-start.10 = (f32[2,256]{1,0:T(2,128)S(1)}, f32[2,256]{1,0:T(2,128)S(1)}, u32[]{:S(2)}, u32[]{:S(2)}) collective-permute-start(f32[2,256]{1,0:T(2,128)S(1)} %get-tuple-element.54), channel_id=1, source_target_pairs={{17,24},{18,25},{19,26},{20,27},{21,28},{22,29},{23,30}} | collective-permute-start | bytes 6152 | tf_op jit(solution)/shard_map/ppermute | solution.py:462
  22.7 0.7 %collective-permute-start.9 = (f32[2,256]{1,0:T(2,128)S(1)}, f32[2,256]{1,0:T(2,128)S(1)}, u32[]{:S(2)}, u32[]{:S(2)}) collective-permute-start(f32[2,256]{1,0:T(2,128)S(1)} %get-tuple-element.54), channel_id=1, source_target_pairs={{16,24},{17,25},{18,26},{19,27},{20,28},{21,29},{22,30},{23,31}} | collective-permute-start | bytes 6152 | tf_op jit(solution)/shard_map/ppermute | solution.py:462
  23.3 0.7 %collective-permute-start.8 = (f32[2,256]{1,0:T(2,128)S(1)}, f32[2,256]{1,0:T(2,128)S(1)}, u32[]{:S(2)}, u32[]{:S(2)}) collective-permute-start(f32[2,256]{1,0:T(2,128)S(1)} %get-tuple-element.54), channel_id=1, source_target_pairs={{16,25},{17,26},{18,27},{19,28},{20,29},{21,30},{22,31}} | collective-permute-start | bytes 6152 | tf_op jit(solution)/shard_map/ppermute | solution.py:462
  24.0 0.0 collective-permute-done.10.high_ref
  24.0 0.0 collective-permute-done.9.own_ref
  24.0 0.0 collective-permute-done.8.low_ref
  24.0 0.6 round3.1
  24.6 1.0 %vectors.1 = (f32[2,50,256]{2,1,0:T(8,128)S(1)}, f32[32,8,128]{2,1,0:T(8,128)S(1)}) custom-call(s32[7]{0:T(128)S(1)} %stack.27.at_ref.where_ref, f32[15,56,256]{2,1,0:T(8,128)S(1)} %get-tuple-element.43.zr_ref, f32[15,56,256]{2,1,0:T(8,128)S(1)} %get-tuple-element.44.zi_ref, f32[2,2,16,128]{3,2,1,0:T(8,128)S(1)} %get-tuple-element.57.beta_ref, ...), custom_call_target="tpu_custom_call" | custom-call | tf_op jit(solution)/shard_map/vectors/pallas_call | solution.py:476
  25.5 29.4 %all_to_all.5.got_ref = f32[32,8,128]{2,1,0:T(8,128)S(1)} all-to-all(f32[32,8,128]{2,1,0:T(8,128)S(1)} %get-tuple-element.60), channel_id=1, replica_groups=mesh['section'=4,'pix'=8] {'section','pix'}, dimensions={0} | all-to-all | bytes 262144 | tf_op jit(solution)/shard_map/all_to_all | solution.py:485
  54.9 1.4 %finish.1 = (f32[50,2,256]{2,1,0:T(2,128)}, f32[2,1,256]{2,1,0:T(1,128)}) custom-call(s32[7]{0:T(128)S(1)} %stack.27.at_ref.where_ref, f32[2,50,256]{2,1,0:T(8,128)S(1)} %get-tuple-element.59.vec_ref, f32[32,8,128]{2,1,0:T(8,128)S(1)} %all_to_all.5.got_ref, f32[2,256]{1,0:T(2,128)S(1)} %get-tuple-element.61.comp_ref), custom_call_target="tpu_custom_call" | custom-call | tf_op jit(solution)/shard_map/finish/pallas_call | solution.py:486
Async XLA Ops:
  0.6 7.8 %collective-permute-start.1 = (f32[50,2,256]{2,1,0:T(2,128)}, f32[50,2,256]{2,1,0:T(2,128)S(1)}, u32[]{:S(2)}, u32[]{:S(2)}) collective-permute-start(f32[50,2,256]{2,1,0:T(2,128)} %bitcast.14), channel_id=1, source_target_pairs={{1,0},{2,1},{3,2},{4,3},{5,4},{6,5},{7,6},{9,8},{10,9},{11,10},{12... | collective-permute-start | bytes 307208 | tf_op jit(solution)/shard_map/ppermute | solution.py:413
  1.9 6.5 %collective-permute-start = (f32[50,2,256]{2,1,0:T(2,128)}, f32[50,2,256]{2,1,0:T(2,128)S(1)}, u32[]{:S(2)}, u32[]{:S(2)}) collective-permute-start(f32[50,2,256]{2,1,0:T(2,128)} %bitcast.15), channel_id=1, source_target_pairs={{0,1},{1,2},{2,3},{3,4},{4,5},{5,6},{6,7},{8,9},{9,10},{10,11},{11... | collective-permute-start | bytes 307208 | tf_op jit(solution)/shard_map/ppermute | solution.py:412
  5.6 0.7 %copy-start = (s32[15,256]{1,0:T(8,128)S(1)}, s32[15,256]{1,0:T(8,128)}, u32[]{:S(2)}) copy-start(s32[15,256]{1,0:T(8,128)} %idx_ref.11) | copy-start | bytes 46084
  6.4 0.9 %copy-start.1 = (f32[2,50,256]{2,0,1:T(2,128)S(1)}, f32[2,50,256]{2,0,1:T(2,128)}, u32[]{:S(2)}) copy-start(f32[2,50,256]{2,0,1:T(2,128)} %param.3) | copy-start | bytes 307204
  14.3 3.8 %collective-permute-start.4 = (f32[2,256]{1,0:T(2,128)S(1)}, f32[2,256]{1,0:T(2,128)S(1)}, u32[]{:S(2)}, u32[]{:S(2)}) collective-permute-start(f32[2,256]{1,0:T(2,128)S(1)} %get-tuple-element.45), channel_id=1, source_target_pairs={{1,8},{2,9},{3,10},{4,11},{5,12},{6,13},{7,14}} | collective-permute-start | bytes 6152 | tf_op jit(solution)/shard_map/ppermute | solution.py:462
  14.9 3.2 %collective-permute-start.3 = (f32[2,256]{1,0:T(2,128)S(1)}, f32[2,256]{1,0:T(2,128)S(1)}, u32[]{:S(2)}, u32[]{:S(2)}) collective-permute-start(f32[2,256]{1,0:T(2,128)S(1)} %get-tuple-element.45), channel_id=1, source_target_pairs={{0,8},{1,9},{2,10},{3,11},{4,12},{5,13},{6,14},{7,15}} | collective-permute-start | bytes 6152 | tf_op jit(solution)/shard_map/ppermute | solution.py:462
  16.2 2.6 %collective-permute-start.2 = (f32[2,256]{1,0:T(2,128)S(1)}, f32[2,256]{1,0:T(2,128)S(1)}, u32[]{:S(2)}, u32[]{:S(2)}) collective-permute-start(f32[2,256]{1,0:T(2,128)S(1)} %get-tuple-element.45), channel_id=1, source_target_pairs={{0,9},{1,10},{2,11},{3,12},{4,13},{5,14},{6,15}} | collective-permute-start | bytes 6152 | tf_op jit(solution)/shard_map/ppermute | solution.py:462
  19.4 2.0 %collective-permute-start.7 = (f32[2,256]{1,0:T(2,128)S(1)}, f32[2,256]{1,0:T(2,128)S(1)}, u32[]{:S(2)}, u32[]{:S(2)}) collective-permute-start(f32[2,256]{1,0:T(2,128)S(1)} %get-tuple-element.51), channel_id=1, source_target_pairs={{9,16},{10,17},{11,18},{12,19},{13,20},{14,21},{15,22}} | collective-permute-start | bytes 6152 | tf_op jit(solution)/shard_map/ppermute | solution.py:462
  20.1 1.4 %collective-permute-start.6 = (f32[2,256]{1,0:T(2,128)S(1)}, f32[2,256]{1,0:T(2,128)S(1)}, u32[]{:S(2)}, u32[]{:S(2)}) collective-permute-start(f32[2,256]{1,0:T(2,128)S(1)} %get-tuple-element.51), channel_id=1, source_target_pairs={{8,16},{9,17},{10,18},{11,19},{12,20},{13,21},{14,22},{15,23}} | collective-permute-start | bytes 6152 | tf_op jit(solution)/shard_map/ppermute | solution.py:462
  20.7 0.7 %collective-permute-start.5 = (f32[2,256]{1,0:T(2,128)S(1)}, f32[2,256]{1,0:T(2,128)S(1)}, u32[]{:S(2)}, u32[]{:S(2)}) collective-permute-start(f32[2,256]{1,0:T(2,128)S(1)} %get-tuple-element.51), channel_id=1, source_target_pairs={{8,17},{9,18},{10,19},{11,20},{12,21},{13,22},{14,23}} | collective-permute-start | bytes 6152 | tf_op jit(solution)/shard_map/ppermute | solution.py:462
  22.0 2.0 %collective-permute-start.10 = (f32[2,256]{1,0:T(2,128)S(1)}, f32[2,256]{1,0:T(2,128)S(1)}, u32[]{:S(2)}, u32[]{:S(2)}) collective-permute-start(f32[2,256]{1,0:T(2,128)S(1)} %get-tuple-element.54), channel_id=1, source_target_pairs={{17,24},{18,25},{19,26},{20,27},{21,28},{22,29},{23,30}} | collective-permute-start | bytes 6152 | tf_op jit(solution)/shard_map/ppermute | solution.py:462
  22.7 1.4 %collective-permute-start.9 = (f32[2,256]{1,0:T(2,128)S(1)}, f32[2,256]{1,0:T(2,128)S(1)}, u32[]{:S(2)}, u32[]{:S(2)}) collective-permute-start(f32[2,256]{1,0:T(2,128)S(1)} %get-tuple-element.54), channel_id=1, source_target_pairs={{16,24},{17,25},{18,26},{19,27},{20,28},{21,29},{22,30},{23,31}} | collective-permute-start | bytes 6152 | tf_op jit(solution)/shard_map/ppermute | solution.py:462
  23.3 0.7 %collective-permute-start.8 = (f32[2,256]{1,0:T(2,128)S(1)}, f32[2,256]{1,0:T(2,128)S(1)}, u32[]{:S(2)}, u32[]{:S(2)}) collective-permute-start(f32[2,256]{1,0:T(2,128)S(1)} %get-tuple-element.54), channel_id=1, source_target_pairs={{16,25},{17,26},{18,27},{19,28},{20,29},{21,30},{22,31}} | collective-permute-start | bytes 6152 | tf_op jit(solution)/shard_map/ppermute | solution.py:462

commit v3 on v2

--- a/solution.py
+++ b/solution.py
@@ -18,6 +18,7 @@
 
 SMEM = pl.BlockSpec(memory_space=pltpu.SMEM)
 VMEM = pl.BlockSpec(memory_space=pltpu.VMEM)
+HBM = pl.BlockSpec(memory_space=pltpu.HBM)
 
 
 def f32(*shape):
@@ -239,8 +240,16 @@
         state_ref[5:8, half(h)] = jnp.zeros((3, LANES), jnp.float32)
 
 
-def own_kernel(at_ref, idx_ref, slc_ref, zr_ref, zi_ref, own_ref, hl_ref):
-    gather(at_ref[6], idx_ref, ((slc_ref, 0),), own_ref, hl_ref, zr_ref, zi_ref, False)
+def own_kernel(at_ref, idx_hbm, slc_hbm, zr_ref, zi_ref, own_ref, idx_ref, slc_ref, hl_ref, sems):
+    copies = [
+        pltpu.make_async_copy(slc_hbm, slc_ref, sems.at[0]),
+        pltpu.make_async_copy(idx_hbm, idx_ref, sems.at[1]),
+    ]
+    for copy in copies:
+        copy.start()
+    for copy in copies:
+        copy.wait()
+    gather(at_ref[2], idx_ref, ((slc_ref, 0),), own_ref, hl_ref, zr_ref, zi_ref, False)
 
 
 def prepare_kernel(stack, first, at_ref, idx_ref, low_ref, high_ref, own_ref, *refs):
@@ -252,7 +261,7 @@
     def _():
         count, _, pixels = zr_ref.shape
         pieces = ((low_ref, -low_ref.shape[2]), (high_ref, pixels))
-        gather(at_ref[6], idx_ref, pieces, xs_ref, hl_ref, zr_ref, zi_ref, True)
+        gather(at_ref[2], idx_ref, pieces, xs_ref, hl_ref, zr_ref, zi_ref, True)
         scale_dates(zr_ref, zi_ref)
         gram(pair_ref, zr_ref, zi_ref, own_ref, gr_ref, gi_ref, sum_ref)
         if first:
@@ -269,9 +278,14 @@
 
 def round_kernel(
     rnd, stack, where_ref, idx_ref, low_ref, own_ref, high_ref,
-    gr_ref, gi_ref, sum_ref, beta0_ref, state0_ref,
-    beta_ref, state_ref, comp_ref, fr_ref, fi_ref,
+    gr_ref, gi_ref, sum_ref, beta0_ref, state0_ref, *refs,
 ):
+    last = len(refs) > 5
+    if last:
+        late, (comp_ref, *made), refs = refs[:3], refs[3:6], refs[6:]
+        fr_ref, fi_ref, beta_ref, state_ref, turned_ref = refs
+    else:
+        beta_ref, state_ref, comp_ref, fr_ref, fi_ref = refs
     count = gr_ref.shape[0] - 1
     halves = gr_ref.shape[1]
     reach = low_ref.shape[1]
@@ -318,12 +332,14 @@
         solve(virtual, fr_ref, fi_ref, hr, hi, sum_ref, stack, beta_ref, state_ref)
 
     comp_ref[...] = state_ref[0:2]
-
-
-def vector_kernel(at_ref, zr_ref, zi_ref, beta_ref, state_ref, vec_ref, slot_ref, turned_ref):
+    if last:
+        vectors(*late, beta_ref, state_ref, *made, turned_ref)
+
+
+def vectors(at_ref, zr_ref, zi_ref, beta_ref, state_ref, vec_ref, slot_ref, turned_ref):
     count, rows, pixels = zr_ref.shape
     dates = vec_ref.shape[1]
-    local = at_ref[2]
+    local = at_ref[0]
     for h in range(pixels // LANES):
         a = state_ref[4:5, half(h)]
         acc_r = [jnp.broadcast_to(a, (SUB, LANES)) for _ in range(0, rows, SUB)]
@@ -357,10 +373,10 @@
         slot_ref[n] = slot
 
 
-def finish_kernel(sections, at_ref, vec_ref, got_ref, comp_ref, out_ref, small_ref):
+def finish_kernel(sections, where_ref, at_ref, vec_ref, got_ref, comp_ref, out_ref, small_ref):
     small_ref[:, 0] = comp_ref[...]
     dates, pixels = vec_ref.shape[1:]
-    section, mine, root, blocks = at_ref[1], at_ref[3], at_ref[4], at_ref[5]
+    section, mine, blocks, root = where_ref[1], where_ref[3], where_ref[4], at_ref[1]
     halves = pixels // LANES
     one = jnp.ones((1, LANES), jnp.float32)
     datum = [(one, 0.0 * one) for _ in range(halves)]
@@ -412,21 +428,23 @@
     low = lax.ppermute(slc[:, :, pixels - reach :], "pix", forward)
     high = lax.ppermute(slc[:, :, :reach], "pix", backward)
 
-    root = reference_pixel[0] // pixels
-    local = reference_pixel[0] - root * pixels
-    at = jnp.stack([base, section, local, block, root, jnp.int32(blocks), block * pixels]).astype(jnp.int32)
+    at = jnp.stack([base, section, block * pixels, block, jnp.int32(blocks)]).astype(jnp.int32)
 
     made = [
         f32(count, rows, pixels), f32(count, rows, pixels),
         f32(count + 1, halves, KP, LANES), f32(count + 1, halves, KP, LANES),
         f32(2, halves, KP, LANES), f32(2, halves, KP, LANES), f32(SUB, pixels), f32(2, pixels),
     ]
-    zr, zi, own = pl.pallas_call(
+    zr, zi, own, neighbours = pl.pallas_call(
         own_kernel,
-        out_shape=made[:2] + [f32(2 * rows, pixels)],
-        in_specs=[SMEM, VMEM, VMEM],
-        out_specs=[VMEM] * 3,
-        scratch_shapes=[pltpu.VMEM((4 * rows, pixels), jnp.bfloat16)],
+        out_shape=made[:2] + [f32(2 * rows, pixels), jax.ShapeDtypeStruct(neighbours.shape, jnp.int32)],
+        in_specs=[SMEM, HBM, HBM],
+        out_specs=[VMEM] * 4,
+        scratch_shapes=[
+            pltpu.VMEM((dates, 2, pixels), jnp.float32),
+            pltpu.VMEM((4 * rows, pixels), jnp.bfloat16),
+            pltpu.SemaphoreType.DMA((2,)),
+        ],
         compiler_params=params(),
         cost_estimate=cost(2 * 4 * rows * pixels * pixels * count),
         name="own",
@@ -461,36 +479,40 @@
             ]
             return lax.ppermute(comp, ("section", "pix"), pairs)
 
-        beta, state, comp = pl.pallas_call(
+        last = rnd == sections - 1
+        late, specs = (), []
+        scratch = [pltpu.VMEM((count, halves, KP, LANES), jnp.float32)] * 2
+        outs = [f32(2, halves, KP, LANES), f32(SUB, pixels), f32(2, pixels)]
+        if last:
+            late, specs = (ref_at, zr, zi), [SMEM, VMEM, VMEM]
+            scratch += [pltpu.VMEM(o.shape, o.dtype) for o in outs[:2]] + [pltpu.VMEM((2, pixels, LANES), jnp.float32)]
+            outs = outs[2:] + [f32(2, dates, pixels), f32(sections * blocks, up(2 * halves + 4, SUB), LANES)]
+        made = pl.pallas_call(
             functools.partial(round_kernel, rnd, stack),
-            out_shape=[f32(2, halves, KP, LANES), f32(SUB, pixels), f32(2, pixels)],
-            in_specs=[SMEM] + [VMEM] * 9,
+            out_shape=outs,
+            in_specs=[SMEM] + [VMEM] * 9 + specs,
             out_specs=[VMEM] * 3,
-            scratch_shapes=[pltpu.VMEM((count, halves, KP, LANES), jnp.float32)] * 2,
+            scratch_shapes=scratch,
             compiler_params=params(),
             name=f"round{rnd}",
-        )(at, neighbours, hop(1)[:, pixels - reach :], hop(0), hop(-1)[:, :reach], gr, gi, sums, beta, state)
-
-    devices = sections * blocks
-    slot_rows = up(2 * halves + 4, SUB)
-    vec, sent = pl.pallas_call(
-        vector_kernel,
-        out_shape=[f32(2, dates, pixels), f32(devices, slot_rows, LANES)],
-        in_specs=[SMEM] + [VMEM] * 4,
-        out_specs=[VMEM] * 2,
-        scratch_shapes=[pltpu.VMEM((2, pixels, LANES), jnp.float32)],
-        compiler_params=params(),
-        name="vectors",
-    )(at, zr, zi, beta, state)
+        )(at, neighbours, hop(1)[:, pixels - reach :], hop(0), hop(-1)[:, :reach], gr, gi, sums, beta, state, *late)
+        if last:
+            comp, vec, sent = made
+        else:
+            beta, state, comp = made
+        if rnd == 1:
+            pixel = lax.optimization_barrier((reference_pixel, comp))[0][0]
+            ref_at = jnp.stack([pixel % pixels, pixel // pixels]).astype(jnp.int32)
+
     got = lax.all_to_all(sent, ("section", "pix"), 0, 0, tiled=True)
     out, small = pl.pallas_call(
         functools.partial(finish_kernel, sections),
         out_shape=[f32(dates, 2, pixels), f32(2, 1, pixels)],
-        in_specs=[SMEM] + [VMEM] * 3,
+        in_specs=[SMEM, SMEM] + [VMEM] * 3,
         out_specs=[VMEM] * 2,
         compiler_params=params(),
         name="finish",
-    )(at, vec, got, comp)
+    )(at, ref_at, vec, got, comp)
     return (jnp.transpose(out, (1, 0, 2)), small)
 
 

time: 56.7 us -> 56.1 us (0.989)
  waiting for transfers between devices: 0.73 us -> 1.96 us
  local copies, waits for them, and re-layouts: 1.59 us -> 0.98 us
  starting transfers between devices: 11.5 us -> 10.9 us
    ppermute x1, waiting for transfers between devices: 0.01 us -> 1.89 us  [on_device(): high = lax.ppermute(slc[:, :, :reach], 'pix', backward)]
    ppermute x9, waiting for transfers between devices: 0.72 us -> 0.07 us  [hop(): return lax.ppermute(comp, ('section', 'pix'), pairs)]
    ppermute x1, starting transfers between devices: 3.04 us -> 2.4 us  [on_device(): low = lax.ppermute(slc[:, :, pixels - reach:], 'pix', forward)]
    unnamed x4, local copies, waits for them, and re-layouts: 1.51 us -> 0.9 us
    pallas_call x5 -> x4, Pallas kernels: 3.8 us -> 3.45 us  [the longest x3 2.06 us: on_device(): pl.pallas_call(functools.partial(round_kernel, rnd, stack), out_shape=out...]
where the time goes in v3:
time: 56.1 us; the launch traced here: 55.8 us
  blocking collectives  29.2 us (52%)
  Pallas kernels  11.2 us (20%)
  starting transfers between devices  10.9 us (19%)
  waiting for transfers between devices  1.96 us (3%)
  between operations  1.5 us (3%)
  local copies, waits for them, and re-layouts  0.98 us (2%)
    all_to_all x1, blocking collectives, on_device(): got = lax.all_to_all(sent, ('section', 'pix'), 0, 0, tiled=True)  29.2 us
    ppermute x9, starting transfers between devices, hop(): return lax.ppermute(comp, ('section', 'pix'), pairs)  7.21 us
    pallas_call x2, Pallas kernels, prepare(): pl.pallas_call(functools.partial(prepare_kernel, stack, first), out_shape...  6.34 us
    ppermute x1, starting transfers between devices, on_device(): low = lax.ppermute(slc[:, :, pixels - reach:], 'pix', forward)  2.4 us
    pallas_call x3, Pallas kernels, on_device(): pl.pallas_call(functools.partial(round_kernel, rnd, stack), out_shape=out...  2.06 us
    ppermute x1, waiting for transfers between devices, on_device(): high = lax.ppermute(slc[:, :, :reach], 'pix', backward)  1.89 us
    pallas_call x1, Pallas kernels, on_device(): pl.pallas_call(own_kernel, out_shape=made[:2] + [f32(2 * rows, pixels), j...  1.39 us
    pallas_call x1, Pallas kernels, on_device(): pl.pallas_call(functools.partial(finish_kernel, sections), out_shape=[f32...  1.37 us
  transfers between devices with their start and end apart: 11, of which 1 were waited for; matrix products, arithmetic and copies ran while one was open for 0% of the time, Pallas kernels for 3%

profile of v3, /device:TPU:0, one launch (start us, length us, event | category | flops | bytes accessed | tf_op | source)
XLA Modules:
  0.0 55.8 jit_solution(6649392236528203917)
XLA Ops:
  0.6 0.0 copy-start.1
  0.6 2.4 %collective-permute-start = (f32[50,2,256]{2,1,0:T(2,128)}, f32[50,2,256]{2,1,0:T(2,128)S(1)}, u32[]{:S(2)}, u32[]{:S(2)}) collective-permute-start(f32[50,2,256]{2,1,0:T(2,128)} %bitcast.13), channel_id=1, source_target_pairs={{0,1},{1,2},{2,3},{3,4},{4,5},{5,6},{6,7},{8,9},{9,10},{10,11},{11... | collective-permute-start | bytes 307208 | tf_op jit(solution)/shard_map/ppermute | solution.py:428
  3.1 1.3 %collective-permute-start.1 = (f32[50,2,256]{2,1,0:T(2,128)}, f32[50,2,256]{2,1,0:T(2,128)S(1)}, u32[]{:S(2)}, u32[]{:S(2)}) collective-permute-start(f32[50,2,256]{2,1,0:T(2,128)} %bitcast.14), channel_id=1, source_target_pairs={{1,0},{2,1},{3,2},{4,3},{5,4},{6,5},{7,6},{9,8},{10,9},{11,10},{12... | collective-permute-start | bytes 307208 | tf_op jit(solution)/shard_map/ppermute | solution.py:429
  4.4 0.1 stack.28.at_ref.where_ref
  4.4 0.0 copy-done.1
  4.4 0.0 copy-start
  4.4 0.9 %copy-done = f32[2,50,256]{2,0,1:T(2,128)S(1)} copy-done((f32[2,50,256]{2,0,1:T(2,128)S(1)}, f32[2,50,256]{2,0,1:T(2,128)}, u32[]{:S(2)}) %copy-start) | copy-done | bytes 102424
  5.3 1.4 %own.1 = (f32[15,56,256]{2,1,0:T(8,128)S(1)}, f32[15,56,256]{2,1,0:T(8,128)S(1)}, f32[112,256]{1,0:T(8,128)S(1)}, s32[15,256]{1,0:T(8,128)S(1)}) custom-call(s32[5]{0:T(128)S(1)} %stack.28.at_ref.where_ref, s32[15,256]{1,0:T(8,128)S(1)} %copy-done.1, f32[50,2,256]{2,1,0:T(2,128)S(1)} %bitcast.15), custom_call_target="tpu_custom_call" | custom-call | flops 440401920 | tf_op jit(solution)/shard_map/own/pallas_call | solution.py:438
  6.7 0.0 collective-permute-done.low_ref
  6.7 1.9 %collective-permute-done.1.high_ref = f32[50,2,256]{2,1,0:T(2,128)S(1)} collective-permute-done((f32[50,2,256]{2,1,0:T(2,128)}, f32[50,2,256]{2,1,0:T(2,128)S(1)}, u32[]{:S(2)}, u32[]{:S(2)}) %collective-permute-start.1) | collective-permute-done | bytes 102432 | tf_op jit(solution)/shard_map/ppermute | solution.py:429
  8.6 5.8 %prepare0.1 = (f32[15,56,256]{2,1,0:T(8,128)S(1)}, f32[15,56,256]{2,1,0:T(8,128)S(1)}, f32[16,2,16,128]{3,2,1,0:T(8,128)S(1)}, f32[16,2,16,128]{3,2,1,0:T(8,128)...) custom-call(s32[5]{0:T(128)S(1)} %stack.28.at_ref.where_ref, ...), custom_call_target="tpu_custom_call", output_to_operand_aliasing={{0}: (5, {}), {1}: (6, {})} | custom-call | flops 33030144000 | tf_op jit(solution)/shard_map/prepare0/pallas_call | solution.py:454
  14.4 1.3 %collective-permute-start.2 = (f32[2,256]{1,0:T(2,128)S(1)}, f32[2,256]{1,0:T(2,128)S(1)}, u32[]{:S(2)}, u32[]{:S(2)}) collective-permute-start(f32[2,256]{1,0:T(2,128)S(1)} %get-tuple-element.37), channel_id=1, source_target_pairs={{0,9},{1,10},{2,11},{3,12},{4,13},{5,14},{6,15}} | collective-permute-start | bytes 6152 | tf_op jit(solution)/shard_map/ppermute | solution.py:480
  15.7 1.3 %collective-permute-start.3 = (f32[2,256]{1,0:T(2,128)S(1)}, f32[2,256]{1,0:T(2,128)S(1)}, u32[]{:S(2)}, u32[]{:S(2)}) collective-permute-start(f32[2,256]{1,0:T(2,128)S(1)} %get-tuple-element.37), channel_id=1, source_target_pairs={{0,8},{1,9},{2,10},{3,11},{4,12},{5,13},{6,14},{7,15}} | collective-permute-start | bytes 6152 | tf_op jit(solution)/shard_map/ppermute | solution.py:480
  17.0 0.7 %collective-permute-start.4 = (f32[2,256]{1,0:T(2,128)S(1)}, f32[2,256]{1,0:T(2,128)S(1)}, u32[]{:S(2)}, u32[]{:S(2)}) collective-permute-start(f32[2,256]{1,0:T(2,128)S(1)} %get-tuple-element.37), channel_id=1, source_target_pairs={{1,8},{2,9},{3,10},{4,11},{5,12},{6,13},{7,14}} | collective-permute-start | bytes 6152 | tf_op jit(solution)/shard_map/ppermute | solution.py:480
  17.7 0.6 %preparen.1 = (f32[15,56,256]{2,1,0:T(8,128)S(1)}, f32[15,56,256]{2,1,0:T(8,128)S(1)}, f32[16,2,16,128]{3,2,1,0:T(8,128)S(1)}, f32[16,2,16,128]{3,2,1,0:T(8,128)...) custom-call(s32[5]{0:T(128)S(1)} %stack.28.at_ref.where_ref, ...), custom_call_target="tpu_custom_call", output_to_operand_aliasing={{0}: (5, {}), {1}: (6, {}), {2}: (7, {}), {3}: (8, {}), {4}... | custom-call | flops 33030144000 | tf_op jit(solution)/shard_map/preparen/pallas_call | solution.py:454
  18.3 0.0 collective-permute-done.2.low_ref
  18.3 0.0 collective-permute-done.3.own_ref
  18.3 0.0 collective-permute-done.4.high_ref
  18.3 0.5 round1.1
  18.9 0.7 %collective-permute-start.5 = (f32[2,256]{1,0:T(2,128)S(1)}, f32[2,256]{1,0:T(2,128)S(1)}, u32[]{:S(2)}, u32[]{:S(2)}) collective-permute-start(f32[2,256]{1,0:T(2,128)S(1)} %get-tuple-element.50), channel_id=1, source_target_pairs={{8,17},{9,18},{10,19},{11,20},{12,21},{13,22},{14,23}} | collective-permute-start | bytes 6152 | tf_op jit(solution)/shard_map/ppermute | solution.py:480
  19.5 0.7 %collective-permute-start.6 = (f32[2,256]{1,0:T(2,128)S(1)}, f32[2,256]{1,0:T(2,128)S(1)}, u32[]{:S(2)}, u32[]{:S(2)}) collective-permute-start(f32[2,256]{1,0:T(2,128)S(1)} %get-tuple-element.50), channel_id=1, source_target_pairs={{8,16},{9,17},{10,18},{11,19},{12,20},{13,21},{14,22},{15,23}} | collective-permute-start | bytes 6152 | tf_op jit(solution)/shard_map/ppermute | solution.py:480
  20.2 0.7 %collective-permute-start.7 = (f32[2,256]{1,0:T(2,128)S(1)}, f32[2,256]{1,0:T(2,128)S(1)}, u32[]{:S(2)}, u32[]{:S(2)}) collective-permute-start(f32[2,256]{1,0:T(2,128)S(1)} %get-tuple-element.50), channel_id=1, source_target_pairs={{9,16},{10,17},{11,18},{12,19},{13,20},{14,21},{15,22}} | collective-permute-start | bytes 6152 | tf_op jit(solution)/shard_map/ppermute | solution.py:480
  21.6 0.0 collective-permute-done.5.low_ref
  21.6 0.0 collective-permute-done.6.own_ref
  21.6 0.0 collective-permute-done.7.high_ref
  21.6 0.6 round2.1
  22.1 0.7 %collective-permute-start.10 = (f32[2,256]{1,0:T(2,128)S(1)}, f32[2,256]{1,0:T(2,128)S(1)}, u32[]{:S(2)}, u32[]{:S(2)}) collective-permute-start(f32[2,256]{1,0:T(2,128)S(1)} %get-tuple-element.54), channel_id=1, source_target_pairs={{17,24},{18,25},{19,26},{20,27},{21,28},{22,29},{23,30}} | collective-permute-start | bytes 6152 | tf_op jit(solution)/shard_map/ppermute | solution.py:480
  22.8 0.7 %collective-permute-start.8 = (f32[2,256]{1,0:T(2,128)S(1)}, f32[2,256]{1,0:T(2,128)S(1)}, u32[]{:S(2)}, u32[]{:S(2)}) collective-permute-start(f32[2,256]{1,0:T(2,128)S(1)} %get-tuple-element.54), channel_id=1, source_target_pairs={{16,25},{17,26},{18,27},{19,28},{20,29},{21,30},{22,31}} | collective-permute-start | bytes 6152 | tf_op jit(solution)/shard_map/ppermute | solution.py:480
  23.5 0.7 %collective-permute-start.9 = (f32[2,256]{1,0:T(2,128)S(1)}, f32[2,256]{1,0:T(2,128)S(1)}, u32[]{:S(2)}, u32[]{:S(2)}) collective-permute-start(f32[2,256]{1,0:T(2,128)S(1)} %get-tuple-element.54), channel_id=1, source_target_pairs={{16,24},{17,25},{18,26},{19,27},{20,28},{21,29},{22,30},{23,31}} | collective-permute-start | bytes 6152 | tf_op jit(solution)/shard_map/ppermute | solution.py:480
  24.2 0.1 pad_add_fusion.refs_0_.at_ref
  24.2 0.0 collective-permute-done.10.high_ref
  24.2 0.0 collective-permute-done.8.low_ref
  24.2 0.0 collective-permute-done.9.own_ref
  24.2 1.0 %round3.1 = (f32[2,256]{1,0:T(2,128)S(1)}, f32[2,50,256]{2,1,0:T(8,128)S(1)}, f32[32,8,128]{2,1,0:T(8,128)S(1)}) custom-call(s32[5]{0:T(128)S(1)} %stack.28.at_ref.where_ref, s32[15,256]{1,0:T(8,128)S(1)} %get-tuple-element.33.idx_ref, f32[2,256]{1,0:T(2,128)S(1)} %collective-permute-done.8.low_ref, f32[2,256]{1,0:T(2,128)S(1)} %collective-permute-done.9.own_ref, ...), custom_call_target="tpu_custom_call" | custom-call | tf_op jit(solution)/shard_map/round3/pallas_call | solution.py:490
  25.2 29.2 %all_to_all.5.got_ref = f32[32,8,128]{2,1,0:T(8,128)S(1)} all-to-all(f32[32,8,128]{2,1,0:T(8,128)S(1)} %get-tuple-element.60), channel_id=1, replica_groups=mesh['section'=4,'pix'=8] {'section','pix'}, dimensions={0} | all-to-all | bytes 262144 | tf_op jit(solution)/shard_map/all_to_all | solution.py:507
  54.4 1.4 %finish.1 = (f32[50,2,256]{2,1,0:T(2,128)}, f32[2,1,256]{2,1,0:T(1,128)}) custom-call(s32[5]{0:T(128)S(1)} %stack.28.at_ref.where_ref, s32[2]{0:T(128)S(1)} %pad_add_fusion.refs_0_.at_ref, f32[2,50,256]{2,1,0:T(8,128)S(1)} %get-tuple-element.59.vec_ref, f32[32,8,128]{2,1,0:T(8,128)S(1)} %all_to_all.5.got_ref, f32[2,256]{1,0:T(2,128)S(1)} %get-tuple-element.61.comp_ref), custom_call_target="tpu_custom_call" | custom-call | tf_op jit(solution)/shard_map/finish/pallas_call | solution.py:508
Async XLA Ops:
  0.6 3.8 %copy-start.1 = (s32[15,256]{1,0:T(8,128)S(1)}, s32[15,256]{1,0:T(8,128)}, u32[]{:S(2)}) copy-start(s32[15,256]{1,0:T(8,128)} %idx_hbm.1) | copy-start | bytes 46084
  0.6 6.1 %collective-permute-start = (f32[50,2,256]{2,1,0:T(2,128)}, f32[50,2,256]{2,1,0:T(2,128)S(1)}, u32[]{:S(2)}, u32[]{:S(2)}) collective-permute-start(f32[50,2,256]{2,1,0:T(2,128)} %bitcast.13), channel_id=1, source_target_pairs={{0,1},{1,2},{2,3},{3,4},{4,5},{5,6},{6,7},{8,9},{9,10},{10,11},{11... | collective-permute-start | bytes 307208 | tf_op jit(solution)/shard_map/ppermute | solution.py:428
  3.1 5.6 %collective-permute-start.1 = (f32[50,2,256]{2,1,0:T(2,128)}, f32[50,2,256]{2,1,0:T(2,128)S(1)}, u32[]{:S(2)}, u32[]{:S(2)}) collective-permute-start(f32[50,2,256]{2,1,0:T(2,128)} %bitcast.14), channel_id=1, source_target_pairs={{1,0},{2,1},{3,2},{4,3},{5,4},{6,5},{7,6},{9,8},{10,9},{11,10},{12... | collective-permute-start | bytes 307208 | tf_op jit(solution)/shard_map/ppermute | solution.py:429
  4.4 0.9 %copy-start = (f32[2,50,256]{2,0,1:T(2,128)S(1)}, f32[2,50,256]{2,0,1:T(2,128)}, u32[]{:S(2)}) copy-start(f32[2,50,256]{2,0,1:T(2,128)} %param.3) | copy-start | bytes 307204
  14.4 3.8 %collective-permute-start.2 = (f32[2,256]{1,0:T(2,128)S(1)}, f32[2,256]{1,0:T(2,128)S(1)}, u32[]{:S(2)}, u32[]{:S(2)}) collective-permute-start(f32[2,256]{1,0:T(2,128)S(1)} %get-tuple-element.37), channel_id=1, source_target_pairs={{0,9},{1,10},{2,11},{3,12},{4,13},{5,14},{6,15}} | collective-permute-start | bytes 6152 | tf_op jit(solution)/shard_map/ppermute | solution.py:480
  15.7 2.6 %collective-permute-start.3 = (f32[2,256]{1,0:T(2,128)S(1)}, f32[2,256]{1,0:T(2,128)S(1)}, u32[]{:S(2)}, u32[]{:S(2)}) collective-permute-start(f32[2,256]{1,0:T(2,128)S(1)} %get-tuple-element.37), channel_id=1, source_target_pairs={{0,8},{1,9},{2,10},{3,11},{4,12},{5,13},{6,14},{7,15}} | collective-permute-start | bytes 6152 | tf_op jit(solution)/shard_map/ppermute | solution.py:480
  17.0 1.3 %collective-permute-start.4 = (f32[2,256]{1,0:T(2,128)S(1)}, f32[2,256]{1,0:T(2,128)S(1)}, u32[]{:S(2)}, u32[]{:S(2)}) collective-permute-start(f32[2,256]{1,0:T(2,128)S(1)} %get-tuple-element.37), channel_id=1, source_target_pairs={{1,8},{2,9},{3,10},{4,11},{5,12},{6,13},{7,14}} | collective-permute-start | bytes 6152 | tf_op jit(solution)/shard_map/ppermute | solution.py:480
  18.9 2.7 %collective-permute-start.5 = (f32[2,256]{1,0:T(2,128)S(1)}, f32[2,256]{1,0:T(2,128)S(1)}, u32[]{:S(2)}, u32[]{:S(2)}) collective-permute-start(f32[2,256]{1,0:T(2,128)S(1)} %get-tuple-element.50), channel_id=1, source_target_pairs={{8,17},{9,18},{10,19},{11,20},{12,21},{13,22},{14,23}} | collective-permute-start | bytes 6152 | tf_op jit(solution)/shard_map/ppermute | solution.py:480
  19.5 2.0 %collective-permute-start.6 = (f32[2,256]{1,0:T(2,128)S(1)}, f32[2,256]{1,0:T(2,128)S(1)}, u32[]{:S(2)}, u32[]{:S(2)}) collective-permute-start(f32[2,256]{1,0:T(2,128)S(1)} %get-tuple-element.50), channel_id=1, source_target_pairs={{8,16},{9,17},{10,18},{11,19},{12,20},{13,21},{14,22},{15,23}} | collective-permute-start | bytes 6152 | tf_op jit(solution)/shard_map/ppermute | solution.py:480
  20.2 1.4 %collective-permute-start.7 = (f32[2,256]{1,0:T(2,128)S(1)}, f32[2,256]{1,0:T(2,128)S(1)}, u32[]{:S(2)}, u32[]{:S(2)}) collective-permute-start(f32[2,256]{1,0:T(2,128)S(1)} %get-tuple-element.50), channel_id=1, source_target_pairs={{9,16},{10,17},{11,18},{12,19},{13,20},{14,21},{15,22}} | collective-permute-start | bytes 6152 | tf_op jit(solution)/shard_map/ppermute | solution.py:480
  22.1 2.1 %collective-permute-start.10 = (f32[2,256]{1,0:T(2,128)S(1)}, f32[2,256]{1,0:T(2,128)S(1)}, u32[]{:S(2)}, u32[]{:S(2)}) collective-permute-start(f32[2,256]{1,0:T(2,128)S(1)} %get-tuple-element.54), channel_id=1, source_target_pairs={{17,24},{18,25},{19,26},{20,27},{21,28},{22,29},{23,30}} | collective-permute-start | bytes 6152 | tf_op jit(solution)/shard_map/ppermute | solution.py:480
  22.8 1.4 %collective-permute-start.8 = (f32[2,256]{1,0:T(2,128)S(1)}, f32[2,256]{1,0:T(2,128)S(1)}, u32[]{:S(2)}, u32[]{:S(2)}) collective-permute-start(f32[2,256]{1,0:T(2,128)S(1)} %get-tuple-element.54), channel_id=1, source_target_pairs={{16,25},{17,26},{18,27},{19,28},{20,29},{21,30},{22,31}} | collective-permute-start | bytes 6152 | tf_op jit(solution)/shard_map/ppermute | solution.py:480
  23.5 0.8 %collective-permute-start.9 = (f32[2,256]{1,0:T(2,128)S(1)}, f32[2,256]{1,0:T(2,128)S(1)}, u32[]{:S(2)}, u32[]{:S(2)}) collective-permute-start(f32[2,256]{1,0:T(2,128)S(1)} %get-tuple-element.54), channel_id=1, source_target_pairs={{16,24},{17,25},{18,26},{19,27},{20,28},{21,29},{22,30},{23,31}} | collective-permute-start | bytes 6152 | tf_op jit(solution)/shard_map/ppermute | solution.py:480

commit v4 on v3

--- a/solution.py
+++ b/solution.py
@@ -7,6 +7,7 @@
 from jax.experimental import pallas as pl
 from jax.experimental.pallas import tpu as pltpu
 from jax.sharding import PartitionSpec as P
+
 
 ITERS = 16
 FLOOR = 0.05
@@ -252,15 +253,15 @@
     gather(at_ref[2], idx_ref, ((slc_ref, 0),), own_ref, hl_ref, zr_ref, zi_ref, False)
 
 
-def prepare_kernel(stack, first, at_ref, idx_ref, low_ref, high_ref, own_ref, *refs):
+def prepare_kernel(stack, first, at_ref, idx_ref, near_ref, far_ref, own_ref, *refs):
     refs = refs[2 if first else 7 :]
     zr_ref, zi_ref, gr_ref, gi_ref, sum_ref, beta_ref, state_ref = refs[:7]
     xs_ref, hl_ref, pair_ref = refs[-3:]
 
     @pl.when(at_ref[1] == 0 if first else at_ref[1] != 0)
     def _():
-        count, _, pixels = zr_ref.shape
-        pieces = ((low_ref, -low_ref.shape[2]), (high_ref, pixels))
+        count = zr_ref.shape[0]
+        pieces = ((near_ref, at_ref[5]), (far_ref, at_ref[6]))
         gather(at_ref[2], idx_ref, pieces, xs_ref, hl_ref, zr_ref, zi_ref, True)
         scale_dates(zr_ref, zi_ref)
         gram(pair_ref, zr_ref, zi_ref, own_ref, gr_ref, gi_ref, sum_ref)
@@ -423,12 +424,20 @@
     rows = up(dates, SUB)
     base = block * pixels - reach
 
-    forward = [(i, i + 1) for i in range(blocks - 1)]
-    backward = [(i + 1, i) for i in range(blocks - 1)]
-    low = lax.ppermute(slc[:, :, pixels - reach :], "pix", forward)
-    high = lax.ppermute(slc[:, :, :reach], "pix", backward)
-
-    at = jnp.stack([base, section, block * pixels, block, jnp.int32(blocks)]).astype(jnp.int32)
+    even = block % 2 == 0
+
+    def swap(first, upper):
+        pairs = [(i, i + 1) for i in range(first, blocks - 1, 2)]
+        pairs += [(j, i) for i, j in pairs]
+        sent = slc
+        if reach < pixels:
+            sent = jnp.where(upper, slc[:, :, pixels - reach :], slc[:, :, :reach])
+        return lax.ppermute(sent, "pix", pairs), jnp.where(upper, pixels, -reach)
+
+    near, near_at = swap(0, even)
+    far, far_at = swap(1, ~even)
+
+    at = jnp.stack([base, section, block * pixels, block, jnp.int32(blocks), near_at, far_at]).astype(jnp.int32)
 
     made = [
         f32(count, rows, pixels), f32(count, rows, pixels),
@@ -464,8 +473,7 @@
             input_output_aliases={5 + n: n for n in range(len(carried))},
             compiler_params=params(),
             cost_estimate=cost(50 * 12 * rows * reach * pixels * count),
-            name="prepare" + ("0" if first else "n"),
-        )(at, neighbours, low, high, own, *carried)
+        )(at, neighbours, near, far, own, *carried)
 
     *made_0, comp = prepare(True, (zr, zi))
     zr, zi, gr, gi, sums, beta, state = prepare(False, made_0)
@@ -494,7 +502,6 @@
             out_specs=[VMEM] * 3,
             scratch_shapes=scratch,
             compiler_params=params(),
-            name=f"round{rnd}",
         )(at, neighbours, hop(1)[:, pixels - reach :], hop(0), hop(-1)[:, :reach], gr, gi, sums, beta, state, *late)
         if last:
             comp, vec, sent = made

time: 56.1 us -> 54.3 us (0.968)
  starting transfers between devices: 10.9 us -> 8.87 us
  waiting for transfers between devices: 1.96 us -> 0.07 us
  blocking collectives: 29.2 us -> 30.6 us
  local copies, waits for them, and re-layouts: 0.98 us -> 1.59 us
    ppermute x2, starting transfers between devices: 3.7 us -> 1.21 us  [swap(): return (lax.ppermute(sent, 'pix', pairs), jnp.where(upper, pixels, -reach))]
    ppermute x2, waiting for transfers between devices: 1.9 us -> 0.01 us  [swap(): return (lax.ppermute(sent, 'pix', pairs), jnp.where(upper, pixels, -reach))]
    all_to_all x1, blocking collectives: 29.2 us -> 30.6 us  [on_device(): got = lax.all_to_all(sent, ('section', 'pix'), 0, 0, tiled=True)]
    unnamed x4, local copies, waits for them, and re-layouts: 0.9 us -> 1.51 us
  transfers between devices with their start and end apart: 11 -> 11, of which waited for: 1 -> 0; matrix products, arithmetic and copies ran while one was open for 0% -> 0% of each run, Pallas kernels for 3% -> 4%
where the time goes in v4:
time: 54.3 us; the launch traced here: 53.9 us
  blocking collectives  30.6 us (56%)
  Pallas kernels  11.2 us (21%)
  starting transfers between devices  8.87 us (16%)
  local copies, waits for them, and re-layouts  1.59 us (3%)
  between operations  1.51 us (3%)
    all_to_all x1, blocking collectives, on_device(): got = lax.all_to_all(sent, ('section', 'pix'), 0, 0, tiled=True)  30.6 us
    ppermute x9, starting transfers between devices, hop(): return lax.ppermute(comp, ('section', 'pix'), pairs)  7.65 us
    pallas_call x2, Pallas kernels, prepare(): pl.pallas_call(functools.partial(prepare_kernel, stack, first), out_shape...  6.35 us
    pallas_call x3, Pallas kernels, on_device(): pl.pallas_call(functools.partial(round_kernel, rnd, stack), out_shape=out...  2.06 us
    unnamed x4, local copies, waits for them, and re-layouts  1.51 us
    pallas_call x1, Pallas kernels, on_device(): pl.pallas_call(own_kernel, out_shape=made[:2] + [f32(2 * rows, pixels), j...  1.39 us
    pallas_call x1, Pallas kernels, on_device(): pl.pallas_call(functools.partial(finish_kernel, sections), out_shape=[f32...  1.37 us
    ppermute x2, starting transfers between devices, swap(): return (lax.ppermute(sent, 'pix', pairs), jnp.where(upper, pixels, -reach))  1.21 us
  transfers between devices with their start and end apart: 11, of which 0 were waited for; matrix products, arithmetic and copies ran while one was open for 0% of the time, Pallas kernels for 4%

profile of v4, /device:TPU:0, one launch (start us, length us, event | category | flops | bytes accessed | tf_op | source)
XLA Modules:
  0.0 53.9 jit_solution(11602841158357704672)
XLA Ops:
  0.6 0.6 %collective-permute-start = (f32[50,2,256]{2,1,0:T(2,128)}, f32[50,2,256]{2,1,0:T(2,128)S(1)}, u32[]{:S(2)}, u32[]{:S(2)}) collective-permute-start(f32[50,2,256]{2,1,0:T(2,128)} %bitcast.15), channel_id=1, source_target_pairs={{0,1},{2,3},{4,5},{6,7},{1,0},{3,2},{5,4},{7,6},{8,9},{10,11},{12,... | collective-permute-start | bytes 307208 | tf_op jit(solution)/shard_map/ppermute | solution.py:435
  1.2 0.7 %collective-permute-start.1 = (f32[50,2,256]{2,1,0:T(2,128)}, f32[50,2,256]{2,1,0:T(2,128)S(1)}, u32[]{:S(2)}, u32[]{:S(2)}) collective-permute-start(f32[50,2,256]{2,1,0:T(2,128)} %bitcast.16), channel_id=1, source_target_pairs={{1,2},{3,4},{5,6},{2,1},{4,3},{6,5},{9,10},{11,12},{13,14},{10,9},... | collective-permute-start | bytes 307208 | tf_op jit(solution)/shard_map/ppermute | solution.py:435
  1.9 0.0 copy-start.1
  1.9 0.1 stack.36.at_ref.where_ref
  2.0 0.6 %copy-done.1 = s32[15,256]{1,0:T(8,128)S(1)} copy-done((s32[15,256]{1,0:T(8,128)S(1)}, s32[15,256]{1,0:T(8,128)}, u32[]{:S(2)}) %copy-start.1) | copy-done | bytes 15384
  2.6 0.0 copy-start
  2.6 0.9 %copy-done = f32[2,50,256]{2,0,1:T(2,128)S(1)} copy-done((f32[2,50,256]{2,0,1:T(2,128)S(1)}, f32[2,50,256]{2,0,1:T(2,128)}, u32[]{:S(2)}) %copy-start) | copy-done | bytes 102424
  3.5 1.4 %own.1 = (f32[15,56,256]{2,1,0:T(8,128)S(1)}, f32[15,56,256]{2,1,0:T(8,128)S(1)}, f32[112,256]{1,0:T(8,128)S(1)}, s32[15,256]{1,0:T(8,128)S(1)}) custom-call(s32[7]{0:T(128)S(1)} %stack.36.at_ref.where_ref, s32[15,256]{1,0:T(8,128)S(1)} %copy-done.1, f32[50,2,256]{2,1,0:T(2,128)S(1)} %bitcast.17), custom_call_target="tpu_custom_call" | custom-call | flops 440401920 | tf_op jit(solution)/shard_map/own/pallas_call | solution.py:447
  4.9 0.0 collective-permute-done.near_ref
  4.9 0.0 collective-permute-done.1.far_ref
  4.9 5.8 %shard_map.50 = (f32[15,56,256]{2,1,0:T(8,128)S(1)}, f32[15,56,256]{2,1,0:T(8,128)S(1)}, f32[16,2,16,128]{3,2,1,0:T(8,128)S(1)}, f32[16,2,16,128]{3,2,1,0:T(8,12...) custom-call(s32[7]{0:T(128)S(1)} %stack.36.at_ref.where_ref, ...), custom_call_target="tpu_custom_call", output_to_operand_aliasing={{0}: (5, {}), {1}: (6, {})} | custom-call | flops 33030144000 | tf_op jit(solution)/shard_map/pallas_call | solution.py:463
  10.7 1.7 %collective-permute-start.2 = (f32[2,256]{1,0:T(2,128)S(1)}, f32[2,256]{1,0:T(2,128)S(1)}, u32[]{:S(2)}, u32[]{:S(2)}) collective-permute-start(f32[2,256]{1,0:T(2,128)S(1)} %get-tuple-element.37), channel_id=1, source_target_pairs={{0,9},{1,10},{2,11},{3,12},{4,13},{5,14},{6,15}} | collective-permute-start | bytes 6152 | tf_op jit(solution)/shard_map/ppermute | solution.py:488
  12.4 1.3 %collective-permute-start.3 = (f32[2,256]{1,0:T(2,128)S(1)}, f32[2,256]{1,0:T(2,128)S(1)}, u32[]{:S(2)}, u32[]{:S(2)}) collective-permute-start(f32[2,256]{1,0:T(2,128)S(1)} %get-tuple-element.37), channel_id=1, source_target_pairs={{0,8},{1,9},{2,10},{3,11},{4,12},{5,13},{6,14},{7,15}} | collective-permute-start | bytes 6152 | tf_op jit(solution)/shard_map/ppermute | solution.py:488
  13.7 0.7 %collective-permute-start.4 = (f32[2,256]{1,0:T(2,128)S(1)}, f32[2,256]{1,0:T(2,128)S(1)}, u32[]{:S(2)}, u32[]{:S(2)}) collective-permute-start(f32[2,256]{1,0:T(2,128)S(1)} %get-tuple-element.37), channel_id=1, source_target_pairs={{1,8},{2,9},{3,10},{4,11},{5,12},{6,13},{7,14}} | collective-permute-start | bytes 6152 | tf_op jit(solution)/shard_map/ppermute | solution.py:488
  14.4 0.6 %shard_map.51 = (f32[15,56,256]{2,1,0:T(8,128)S(1)}, f32[15,56,256]{2,1,0:T(8,128)S(1)}, f32[16,2,16,128]{3,2,1,0:T(8,128)S(1)}, f32[16,2,16,128]{3,2,1,0:T(8,12...) custom-call(s32[7]{0:T(128)S(1)} %stack.36.at_ref.where_ref, ...), custom_call_target="tpu_custom_call", output_to_operand_aliasing={{0}: (5, {}), {1}: (6, {}), {2}: (7, {}), {3}: (8, {}), {4}... | custom-call | flops 33030144000 | tf_op jit(solution)/shard_map/pallas_call | solution.py:463
  15.0 0.0 collective-permute-done.2.low_ref
  15.0 0.0 collective-permute-done.3.own_ref
  15.0 0.0 collective-permute-done.4.high_ref
  15.0 0.5 %shard_map.52 = (f32[2,2,16,128]{3,2,1,0:T(8,128)S(1)}, f32[8,256]{1,0:T(8,128)S(1)}, f32[2,256]{1,0:T(2,128)S(1)}) custom-call(s32[7]{0:T(128)S(1)} %stack.36.at_ref.where_ref, s32[15,256]{1,0:T(8,128)S(1)} %get-tuple-element.33.idx_ref, f32[2,256]{1,0:T(2,128)S(1)} %collective-permute-done.2.low_ref, f32[2,256]{1,0:T(2,128)S(1)} %collective-permute-done.3.own_ref, ...), custom_call_target="tpu_custom_call" | custom-call | tf_op jit(solution)/shard_map/pallas_call | solution.py:498
  15.6 0.7 %collective-permute-start.5 = (f32[2,256]{1,0:T(2,128)S(1)}, f32[2,256]{1,0:T(2,128)S(1)}, u32[]{:S(2)}, u32[]{:S(2)}) collective-permute-start(f32[2,256]{1,0:T(2,128)S(1)} %get-tuple-element.50), channel_id=1, source_target_pairs={{8,17},{9,18},{10,19},{11,20},{12,21},{13,22},{14,23}} | collective-permute-start | bytes 6152 | tf_op jit(solution)/shard_map/ppermute | solution.py:488
  16.2 0.7 %collective-permute-start.6 = (f32[2,256]{1,0:T(2,128)S(1)}, f32[2,256]{1,0:T(2,128)S(1)}, u32[]{:S(2)}, u32[]{:S(2)}) collective-permute-start(f32[2,256]{1,0:T(2,128)S(1)} %get-tuple-element.50), channel_id=1, source_target_pairs={{8,16},{9,17},{10,18},{11,19},{12,20},{13,21},{14,22},{15,23}} | collective-permute-start | bytes 6152 | tf_op jit(solution)/shard_map/ppermute | solution.py:488
  16.9 0.7 %collective-permute-start.7 = (f32[2,256]{1,0:T(2,128)S(1)}, f32[2,256]{1,0:T(2,128)S(1)}, u32[]{:S(2)}, u32[]{:S(2)}) collective-permute-start(f32[2,256]{1,0:T(2,128)S(1)} %get-tuple-element.50), channel_id=1, source_target_pairs={{9,16},{10,17},{11,18},{12,19},{13,20},{14,21},{15,22}} | collective-permute-start | bytes 6152 | tf_op jit(solution)/shard_map/ppermute | solution.py:488
  18.3 0.0 collective-permute-done.5.low_ref
  18.3 0.0 collective-permute-done.6.own_ref
  18.3 0.0 collective-permute-done.7.high_ref
  18.3 0.6 %shard_map.53 = (f32[2,2,16,128]{3,2,1,0:T(8,128)S(1)}, f32[8,256]{1,0:T(8,128)S(1)}, f32[2,256]{1,0:T(2,128)S(1)}) custom-call(s32[7]{0:T(128)S(1)} %stack.36.at_ref.where_ref, s32[15,256]{1,0:T(8,128)S(1)} %get-tuple-element.33.idx_ref, f32[2,256]{1,0:T(2,128)S(1)} %collective-permute-done.5.low_ref, f32[2,256]{1,0:T(2,128)S(1)} %collective-permute-done.6.own_ref, ...), custom_call_target="tpu_custom_call" | custom-call | tf_op jit(solution)/shard_map/pallas_call | solution.py:498
  18.8 0.7 %collective-permute-start.10 = (f32[2,256]{1,0:T(2,128)S(1)}, f32[2,256]{1,0:T(2,128)S(1)}, u32[]{:S(2)}, u32[]{:S(2)}) collective-permute-start(f32[2,256]{1,0:T(2,128)S(1)} %get-tuple-element.54), channel_id=1, source_target_pairs={{17,24},{18,25},{19,26},{20,27},{21,28},{22,29},{23,30}} | collective-permute-start | bytes 6152 | tf_op jit(solution)/shard_map/ppermute | solution.py:488
  19.5 0.7 %collective-permute-start.8 = (f32[2,256]{1,0:T(2,128)S(1)}, f32[2,256]{1,0:T(2,128)S(1)}, u32[]{:S(2)}, u32[]{:S(2)}) collective-permute-start(f32[2,256]{1,0:T(2,128)S(1)} %get-tuple-element.54), channel_id=1, source_target_pairs={{16,25},{17,26},{18,27},{19,28},{20,29},{21,30},{22,31}} | collective-permute-start | bytes 6152 | tf_op jit(solution)/shard_map/ppermute | solution.py:488
  20.2 0.7 %collective-permute-start.9 = (f32[2,256]{1,0:T(2,128)S(1)}, f32[2,256]{1,0:T(2,128)S(1)}, u32[]{:S(2)}, u32[]{:S(2)}) collective-permute-start(f32[2,256]{1,0:T(2,128)S(1)} %get-tuple-element.54), channel_id=1, source_target_pairs={{16,24},{17,25},{18,26},{19,27},{20,28},{21,29},{22,30},{23,31}} | collective-permute-start | bytes 6152 | tf_op jit(solution)/shard_map/ppermute | solution.py:488
  20.9 0.1 pad_add_fusion.refs_0_.at_ref
  20.9 0.0 collective-permute-done.10.high_ref
  20.9 0.0 collective-permute-done.8.low_ref
  20.9 0.0 collective-permute-done.9.own_ref
  20.9 1.0 %shard_map.54 = (f32[2,256]{1,0:T(2,128)S(1)}, f32[2,50,256]{2,1,0:T(8,128)S(1)}, f32[32,8,128]{2,1,0:T(8,128)S(1)}) custom-call(s32[7]{0:T(128)S(1)} %stack.36.at_ref.where_ref, s32[15,256]{1,0:T(8,128)S(1)} %get-tuple-element.33.idx_ref, f32[2,256]{1,0:T(2,128)S(1)} %collective-permute-done.8.low_ref, f32[2,256]{1,0:T(2,128)S(1)} %collective-permute-done.9.own_ref, ...), custom_call_target="tpu_custom_call" | custom-call | tf_op jit(solution)/shard_map/pallas_call | solution.py:498
  21.9 30.6 %all_to_all.5.got_ref = f32[32,8,128]{2,1,0:T(8,128)S(1)} all-to-all(f32[32,8,128]{2,1,0:T(8,128)S(1)} %get-tuple-element.60), channel_id=1, replica_groups=mesh['section'=4,'pix'=8] {'section','pix'}, dimensions={0} | all-to-all | bytes 262144 | tf_op jit(solution)/shard_map/all_to_all | solution.py:514
  52.5 1.4 %finish.1 = (f32[50,2,256]{2,1,0:T(2,128)}, f32[2,1,256]{2,1,0:T(1,128)}) custom-call(s32[7]{0:T(128)S(1)} %stack.36.at_ref.where_ref, s32[2]{0:T(128)S(1)} %pad_add_fusion.refs_0_.at_ref, f32[2,50,256]{2,1,0:T(8,128)S(1)} %get-tuple-element.59.vec_ref, f32[32,8,128]{2,1,0:T(8,128)S(1)} %all_to_all.5.got_ref, f32[2,256]{1,0:T(2,128)S(1)} %get-tuple-element.61.comp_ref), custom_call_target="tpu_custom_call" | custom-call | tf_op jit(solution)/shard_map/finish/pallas_call | solution.py:515
Async XLA Ops:
  0.6 4.2 %collective-permute-start = (f32[50,2,256]{2,1,0:T(2,128)}, f32[50,2,256]{2,1,0:T(2,128)S(1)}, u32[]{:S(2)}, u32[]{:S(2)}) collective-permute-start(f32[50,2,256]{2,1,0:T(2,128)} %bitcast.15), channel_id=1, source_target_pairs={{0,1},{2,3},{4,5},{6,7},{1,0},{3,2},{5,4},{7,6},{8,9},{10,11},{12,... | collective-permute-start | bytes 307208 | tf_op jit(solution)/shard_map/ppermute | solution.py:435
  1.2 3.7 %collective-permute-start.1 = (f32[50,2,256]{2,1,0:T(2,128)}, f32[50,2,256]{2,1,0:T(2,128)S(1)}, u32[]{:S(2)}, u32[]{:S(2)}) collective-permute-start(f32[50,2,256]{2,1,0:T(2,128)} %bitcast.16), channel_id=1, source_target_pairs={{1,2},{3,4},{5,6},{2,1},{4,3},{6,5},{9,10},{11,12},{13,14},{10,9},... | collective-permute-start | bytes 307208 | tf_op jit(solution)/shard_map/ppermute | solution.py:435
  1.9 0.7 %copy-start.1 = (s32[15,256]{1,0:T(8,128)S(1)}, s32[15,256]{1,0:T(8,128)}, u32[]{:S(2)}) copy-start(s32[15,256]{1,0:T(8,128)} %idx_hbm.1) | copy-start | bytes 46084
  2.6 0.9 %copy-start = (f32[2,50,256]{2,0,1:T(2,128)S(1)}, f32[2,50,256]{2,0,1:T(2,128)}, u32[]{:S(2)}) copy-start(f32[2,50,256]{2,0,1:T(2,128)} %param.3) | copy-start | bytes 307204
  10.7 4.3 %collective-permute-start.2 = (f32[2,256]{1,0:T(2,128)S(1)}, f32[2,256]{1,0:T(2,128)S(1)}, u32[]{:S(2)}, u32[]{:S(2)}) collective-permute-start(f32[2,256]{1,0:T(2,128)S(1)} %get-tuple-element.37), channel_id=1, source_target_pairs={{0,9},{1,10},{2,11},{3,12},{4,13},{5,14},{6,15}} | collective-permute-start | bytes 6152 | tf_op jit(solution)/shard_map/ppermute | solution.py:488
  12.4 2.6 %collective-permute-start.3 = (f32[2,256]{1,0:T(2,128)S(1)}, f32[2,256]{1,0:T(2,128)S(1)}, u32[]{:S(2)}, u32[]{:S(2)}) collective-permute-start(f32[2,256]{1,0:T(2,128)S(1)} %get-tuple-element.37), channel_id=1, source_target_pairs={{0,8},{1,9},{2,10},{3,11},{4,12},{5,13},{6,14},{7,15}} | collective-permute-start | bytes 6152 | tf_op jit(solution)/shard_map/ppermute | solution.py:488
  13.7 1.3 %collective-permute-start.4 = (f32[2,256]{1,0:T(2,128)S(1)}, f32[2,256]{1,0:T(2,128)S(1)}, u32[]{:S(2)}, u32[]{:S(2)}) collective-permute-start(f32[2,256]{1,0:T(2,128)S(1)} %get-tuple-element.37), channel_id=1, source_target_pairs={{1,8},{2,9},{3,10},{4,11},{5,12},{6,13},{7,14}} | collective-permute-start | bytes 6152 | tf_op jit(solution)/shard_map/ppermute | solution.py:488
  15.6 2.7 %collective-permute-start.5 = (f32[2,256]{1,0:T(2,128)S(1)}, f32[2,256]{1,0:T(2,128)S(1)}, u32[]{:S(2)}, u32[]{:S(2)}) collective-permute-start(f32[2,256]{1,0:T(2,128)S(1)} %get-tuple-element.50), channel_id=1, source_target_pairs={{8,17},{9,18},{10,19},{11,20},{12,21},{13,22},{14,23}} | collective-permute-start | bytes 6152 | tf_op jit(solution)/shard_map/ppermute | solution.py:488
  16.2 2.0 %collective-permute-start.6 = (f32[2,256]{1,0:T(2,128)S(1)}, f32[2,256]{1,0:T(2,128)S(1)}, u32[]{:S(2)}, u32[]{:S(2)}) collective-permute-start(f32[2,256]{1,0:T(2,128)S(1)} %get-tuple-element.50), channel_id=1, source_target_pairs={{8,16},{9,17},{10,18},{11,19},{12,20},{13,21},{14,22},{15,23}} | collective-permute-start | bytes 6152 | tf_op jit(solution)/shard_map/ppermute | solution.py:488
  16.9 1.4 %collective-permute-start.7 = (f32[2,256]{1,0:T(2,128)S(1)}, f32[2,256]{1,0:T(2,128)S(1)}, u32[]{:S(2)}, u32[]{:S(2)}) collective-permute-start(f32[2,256]{1,0:T(2,128)S(1)} %get-tuple-element.50), channel_id=1, source_target_pairs={{9,16},{10,17},{11,18},{12,19},{13,20},{14,21},{15,22}} | collective-permute-start | bytes 6152 | tf_op jit(solution)/shard_map/ppermute | solution.py:488
  18.8 2.1 %collective-permute-start.10 = (f32[2,256]{1,0:T(2,128)S(1)}, f32[2,256]{1,0:T(2,128)S(1)}, u32[]{:S(2)}, u32[]{:S(2)}) collective-permute-start(f32[2,256]{1,0:T(2,128)S(1)} %get-tuple-element.54), channel_id=1, source_target_pairs={{17,24},{18,25},{19,26},{20,27},{21,28},{22,29},{23,30}} | collective-permute-start | bytes 6152 | tf_op jit(solution)/shard_map/ppermute | solution.py:488
  19.5 1.4 %collective-permute-start.8 = (f32[2,256]{1,0:T(2,128)S(1)}, f32[2,256]{1,0:T(2,128)S(1)}, u32[]{:S(2)}, u32[]{:S(2)}) collective-permute-start(f32[2,256]{1,0:T(2,128)S(1)} %get-tuple-element.54), channel_id=1, source_target_pairs={{16,25},{17,26},{18,27},{19,28},{20,29},{21,30},{22,31}} | collective-permute-start | bytes 6152 | tf_op jit(solution)/shard_map/ppermute | solution.py:488
  20.2 0.8 %collective-permute-start.9 = (f32[2,256]{1,0:T(2,128)S(1)}, f32[2,256]{1,0:T(2,128)S(1)}, u32[]{:S(2)}, u32[]{:S(2)}) collective-permute-start(f32[2,256]{1,0:T(2,128)S(1)} %get-tuple-element.54), channel_id=1, source_target_pairs={{16,24},{17,25},{18,26},{19,27},{20,28},{21,29},{22,30},{23,31}} | collective-permute-start | bytes 6152 | tf_op jit(solution)/shard_map/ppermute | solution.py:488

commit v5 on v4

--- a/solution.py
+++ b/solution.py
@@ -45,6 +45,15 @@
 def unit(real, imag):
     scale = 1.0 / jnp.maximum(jnp.sqrt(real * real + imag * imag), FLOOR)
     return (real * scale, imag * scale)
+
+
+def seat(pixels, reach):
+    section, block = lax.axis_index("section"), lax.axis_index("pix")
+    even = block % 2 == 0
+    return (
+        section, block, lax.axis_size("pix"), block * pixels,
+        jnp.where(even, pixels, -reach), jnp.where(even, -reach, pixels),
+    )
 
 
 def half(h):
@@ -241,7 +250,7 @@
         state_ref[5:8, half(h)] = jnp.zeros((3, LANES), jnp.float32)
 
 
-def own_kernel(at_ref, idx_hbm, slc_hbm, zr_ref, zi_ref, own_ref, idx_ref, slc_ref, hl_ref, sems):
+def own_kernel(idx_hbm, slc_hbm, zr_ref, zi_ref, own_ref, idx_ref, slc_ref, hl_ref, sems):
     copies = [
         pltpu.make_async_copy(slc_hbm, slc_ref, sems.at[0]),
         pltpu.make_async_copy(idx_hbm, idx_ref, sems.at[1]),
@@ -250,19 +259,22 @@
         copy.start()
     for copy in copies:
         copy.wait()
-    gather(at_ref[2], idx_ref, ((slc_ref, 0),), own_ref, hl_ref, zr_ref, zi_ref, False)
-
-
-def prepare_kernel(stack, first, at_ref, idx_ref, near_ref, far_ref, own_ref, *refs):
+    start = seat(slc_ref.shape[2], 0)[3]
+    gather(start, idx_ref, ((slc_ref, 0),), own_ref, hl_ref, zr_ref, zi_ref, False)
+
+
+def prepare_kernel(stack, first, idx_ref, near_ref, far_ref, own_ref, *refs):
     refs = refs[2 if first else 7 :]
     zr_ref, zi_ref, gr_ref, gi_ref, sum_ref, beta_ref, state_ref = refs[:7]
     xs_ref, hl_ref, pair_ref = refs[-3:]
 
-    @pl.when(at_ref[1] == 0 if first else at_ref[1] != 0)
+    section, _, _, start, near_at, far_at = seat(zr_ref.shape[2], near_ref.shape[2])
+
+    @pl.when(section == 0 if first else section != 0)
     def _():
         count = zr_ref.shape[0]
-        pieces = ((near_ref, at_ref[5]), (far_ref, at_ref[6]))
-        gather(at_ref[2], idx_ref, pieces, xs_ref, hl_ref, zr_ref, zi_ref, True)
+        pieces = ((near_ref, near_at), (far_ref, far_at))
+        gather(start, idx_ref, pieces, xs_ref, hl_ref, zr_ref, zi_ref, True)
         scale_dates(zr_ref, zi_ref)
         gram(pair_ref, zr_ref, zi_ref, own_ref, gr_ref, gi_ref, sum_ref)
         if first:
@@ -278,7 +290,7 @@
 
 
 def round_kernel(
-    rnd, stack, where_ref, idx_ref, low_ref, own_ref, high_ref,
+    rnd, stack, idx_ref, low_ref, own_ref, high_ref,
     gr_ref, gi_ref, sum_ref, beta0_ref, state0_ref, *refs,
 ):
     last = len(refs) > 5
@@ -292,8 +304,9 @@
     reach = low_ref.shape[1]
     beta_ref[...] = beta0_ref[...]
     state_ref[...] = state0_ref[...]
-
-    @pl.when(where_ref[1] == rnd)
+    section, _, _, start, _, _ = seat(own_ref.shape[1], reach)
+
+    @pl.when(section == rnd)
     def _():
         tiles = []
         for ref in (low_ref, own_ref, high_ref):
@@ -304,7 +317,7 @@
             parts = []
             for kt in range(KP // SUB):
                 rows = min(SUB, count - kt * SUB)
-                raw = idx_ref[pl.ds(kt * SUB, rows), half(h)] - where_ref[0]
+                raw = idx_ref[pl.ds(kt * SUB, rows), half(h)] - (start - reach)
                 if rows < SUB:
                     raw = jnp.concatenate([raw, jnp.full((SUB - rows, LANES), -1, jnp.int32)], axis=0)
                 lane = jnp.bitwise_and(raw, LANES - 1)
@@ -374,10 +387,11 @@
         slot_ref[n] = slot
 
 
-def finish_kernel(sections, where_ref, at_ref, vec_ref, got_ref, comp_ref, out_ref, small_ref):
+def finish_kernel(sections, at_ref, vec_ref, got_ref, comp_ref, out_ref, small_ref):
     small_ref[:, 0] = comp_ref[...]
     dates, pixels = vec_ref.shape[1:]
-    section, mine, blocks, root = where_ref[1], where_ref[3], where_ref[4], at_ref[1]
+    section, mine, blocks, _, _, _ = seat(pixels, 0)
+    root = at_ref[1]
     halves = pixels // LANES
     one = jnp.ones((1, LANES), jnp.float32)
     datum = [(one, 0.0 * one) for _ in range(halves)]
@@ -417,12 +431,10 @@
     reach = min(pixels, REACH_LIMIT)
     sections = lax.axis_size("section")
     blocks = lax.axis_size("pix")
-    section = lax.axis_index("section")
     block = lax.axis_index("pix")
     stack = dates + 1
     halves = pixels // LANES
     rows = up(dates, SUB)
-    base = block * pixels - reach
 
     even = block % 2 == 0
 
@@ -432,12 +444,10 @@
         sent = slc
         if reach < pixels:
             sent = jnp.where(upper, slc[:, :, pixels - reach :], slc[:, :, :reach])
-        return lax.ppermute(sent, "pix", pairs), jnp.where(upper, pixels, -reach)
-
-    near, near_at = swap(0, even)
-    far, far_at = swap(1, ~even)
-
-    at = jnp.stack([base, section, block * pixels, block, jnp.int32(blocks), near_at, far_at]).astype(jnp.int32)
+        return lax.ppermute(sent, "pix", pairs)
+
+    near = swap(0, even)
+    far = swap(1, ~even)
 
     made = [
         f32(count, rows, pixels), f32(count, rows, pixels),
@@ -447,7 +457,7 @@
     zr, zi, own, neighbours = pl.pallas_call(
         own_kernel,
         out_shape=made[:2] + [f32(2 * rows, pixels), jax.ShapeDtypeStruct(neighbours.shape, jnp.int32)],
-        in_specs=[SMEM, HBM, HBM],
+        in_specs=[HBM, HBM],
         out_specs=[VMEM] * 4,
         scratch_shapes=[
             pltpu.VMEM((dates, 2, pixels), jnp.float32),
@@ -457,23 +467,23 @@
         compiler_params=params(),
         cost_estimate=cost(2 * 4 * rows * pixels * pixels * count),
         name="own",
-    )(at, neighbours, slc)
+    )(pltpu.with_memory_space_constraint(neighbours, pltpu.HBM), pltpu.with_memory_space_constraint(slc, pltpu.HBM))
 
     def prepare(first, carried):
         return pl.pallas_call(
             functools.partial(prepare_kernel, stack, first),
             out_shape=made[: 8 if first else 7],
-            in_specs=[SMEM] + [VMEM] * (4 + len(carried)),
+            in_specs=[VMEM] * (4 + len(carried)),
             out_specs=[VMEM] * (8 if first else 7),
             scratch_shapes=[
                 pltpu.VMEM((2 * rows, 2 * reach), jnp.float32),
                 pltpu.VMEM((4 * rows, 2 * reach), jnp.bfloat16),
                 pltpu.VMEM((2, count + 1, count, SUB, LANES), jnp.float32),
             ],
-            input_output_aliases={5 + n: n for n in range(len(carried))},
+            input_output_aliases={4 + n: n for n in range(len(carried))},
             compiler_params=params(),
             cost_estimate=cost(50 * 12 * rows * reach * pixels * count),
-        )(at, neighbours, near, far, own, *carried)
+        )(neighbours, near, far, own, *carried)
 
     *made_0, comp = prepare(True, (zr, zi))
     zr, zi, gr, gi, sums, beta, state = prepare(False, made_0)
@@ -498,11 +508,11 @@
         made = pl.pallas_call(
             functools.partial(round_kernel, rnd, stack),
             out_shape=outs,
-            in_specs=[SMEM] + [VMEM] * 9 + specs,
+            in_specs=[VMEM] * 9 + specs,
             out_specs=[VMEM] * 3,
             scratch_shapes=scratch,
             compiler_params=params(),
-        )(at, neighbours, hop(1)[:, pixels - reach :], hop(0), hop(-1)[:, :reach], gr, gi, sums, beta, state, *late)
+        )(neighbours, hop(1)[:, pixels - reach :], hop(0), hop(-1)[:, :reach], gr, gi, sums, beta, state, *late)
         if last:
             comp, vec, sent = made
         else:
@@ -515,11 +525,11 @@
     out, small = pl.pallas_call(
         functools.partial(finish_kernel, sections),
         out_shape=[f32(dates, 2, pixels), f32(2, 1, pixels)],
-        in_specs=[SMEM, SMEM] + [VMEM] * 3,
+        in_specs=[SMEM] + [VMEM] * 3,
         out_specs=[VMEM] * 2,
         compiler_params=params(),
         name="finish",
-    )(at, ref_at, vec, got, comp)
+    )(ref_at, vec, got, comp)
     return (jnp.transpose(out, (1, 0, 2)), small)
 
 

time: 54.3 us -> 52.6 us (0.969)
  Pallas kernels: 11.2 us -> 9.23 us
  local copies, waits for them, and re-layouts: 1.59 us -> 0 us
  starting transfers between devices: 8.87 us -> 10.2 us
    unnamed x4 -> x0, local copies, waits for them, and re-layouts: 1.51 us -> none
    ppermute x9, starting transfers between devices: 7.65 us -> 9.03 us  [hop(): return lax.ppermute(comp, ('section', 'pix'), pairs)]
    pallas_call x2, Pallas kernels: 6.35 us -> 5.27 us  [prepare(): pl.pallas_call(functools.partial(prepare_kernel, stack, first), out_shape...]
    pallas_call x3, Pallas kernels: 2.06 us -> 0.99 us  [on_device(): pl.pallas_call(functools.partial(round_kernel, rnd, stack), out_shape=out...]
  transfers between devices with their start and end apart: 11 -> 11, of which waited for: 0 -> 1; matrix products, arithmetic and copies ran while one was open for 0% -> 0% of each run, Pallas kernels for 4% -> 3%
where the time goes in v5:
time: 52.6 us; the launch traced here: 52.3 us
  blocking collectives  30.6 us (58%)
  starting transfers between devices  10.2 us (19%)
  Pallas kernels  9.23 us (18%)
  between operations  1.47 us (3%)
  waiting for transfers between devices  0.61 us (1%)
    all_to_all x1, blocking collectives, on_device(): got = lax.all_to_all(sent, ('section', 'pix'), 0, 0, tiled=True)  30.6 us
    ppermute x9, starting transfers between devices, hop(): return lax.ppermute(comp, ('section', 'pix'), pairs)  9.03 us
    pallas_call x2, Pallas kernels, prepare(): pl.pallas_call(functools.partial(prepare_kernel, stack, first), out_shape...  5.27 us
    pallas_call x1, Pallas kernels, on_device(): pl.pallas_call(own_kernel, out_shape=made[:2] + [f32(2 * rows, pixels), j...  1.59 us
    pallas_call x1, Pallas kernels, on_device(): pl.pallas_call(functools.partial(finish_kernel, sections), out_shape=[f32...  1.38 us
    ppermute x2, starting transfers between devices, swap(): return lax.ppermute(sent, 'pix', pairs)  1.21 us
  transfers between devices with their start and end apart: 11, of which 1 were waited for; matrix products, arithmetic and copies ran while one was open for 0% of the time, Pallas kernels for 3%

profile of v5, /device:TPU:0, one launch (start us, length us, event | category | flops | bytes accessed | tf_op | source)
XLA Modules:
  0.0 52.3 jit_solution(11179560252883192898)
XLA Ops:
  0.6 0.6 %collective-permute-start = (f32[50,2,256]{2,1,0:T(2,128)}, f32[50,2,256]{2,1,0:T(2,128)S(1)}, u32[]{:S(2)}, u32[]{:S(2)}) collective-permute-start(f32[50,2,256]{2,1,0:T(2,128)} %bitcast.9), channel_id=1, source_target_pairs={{0,1},{2,3},{4,5},{6,7},{1,0},{3,2},{5,4},{7,6},{8,9},{10,11},{12,... | collective-permute-start | bytes 307208 | tf_op jit(solution)/shard_map/ppermute | solution.py:447
  1.2 0.7 %collective-permute-start.1 = (f32[50,2,256]{2,1,0:T(2,128)}, f32[50,2,256]{2,1,0:T(2,128)S(1)}, u32[]{:S(2)}, u32[]{:S(2)}) collective-permute-start(f32[50,2,256]{2,1,0:T(2,128)} %bitcast.10), channel_id=1, source_target_pairs={{1,2},{3,4},{5,6},{2,1},{4,3},{6,5},{9,10},{11,12},{13,14},{10,9},... | collective-permute-start | bytes 307208 | tf_op jit(solution)/shard_map/ppermute | solution.py:447
  1.9 1.6 %own.1 = (f32[15,56,256]{2,1,0:T(8,128)S(1)}, f32[15,56,256]{2,1,0:T(8,128)S(1)}, f32[112,256]{1,0:T(8,128)S(1)}, s32[15,256]{1,0:T(8,128)S(1)}) custom-call(s32[15,256]{1,0:T(8,128)} %idx_hbm.1, f32[50,2,256]{2,1,0:T(2,128)} %bitcast.11), custom_call_target="tpu_custom_call" | custom-call | flops 440401920 | tf_op jit(solution)/shard_map/own/pallas_call | solution.py:457
  3.5 0.0 collective-permute-done.near_ref
  3.5 0.0 collective-permute-done.1.far_ref
  3.5 5.2 %shard_map.50 = (f32[15,56,256]{2,1,0:T(8,128)S(1)}, f32[15,56,256]{2,1,0:T(8,128)S(1)}, f32[16,2,16,128]{3,2,1,0:T(8,128)S(1)}, f32[16,2,16,128]{3,2,1,0:T(8,12...) custom-call(s32[15,256]{1,0:T(8,128)S(1)} %get-tuple-element.33.idx_, ...), custom_call_target="tpu_custom_call", output_to_operand_aliasing={{0}: (4, {}), {1}: (5, {})} | custom-call | flops 33030144000 | tf_op jit(solution)/shard_map/pallas_call | solution.py:473
  8.7 3.1 %collective-permute-start.2 = (f32[2,256]{1,0:T(2,128)S(1)}, f32[2,256]{1,0:T(2,128)S(1)}, u32[]{:S(2)}, u32[]{:S(2)}) collective-permute-start(f32[2,256]{1,0:T(2,128)S(1)} %get-tuple-element.37), channel_id=1, source_target_pairs={{0,9},{1,10},{2,11},{3,12},{4,13},{5,14},{6,15}} | collective-permute-start | bytes 6152 | tf_op jit(solution)/shard_map/ppermute | solution.py:498
  11.9 1.3 %collective-permute-start.3 = (f32[2,256]{1,0:T(2,128)S(1)}, f32[2,256]{1,0:T(2,128)S(1)}, u32[]{:S(2)}, u32[]{:S(2)}) collective-permute-start(f32[2,256]{1,0:T(2,128)S(1)} %get-tuple-element.37), channel_id=1, source_target_pairs={{0,8},{1,9},{2,10},{3,11},{4,12},{5,13},{6,14},{7,15}} | collective-permute-start | bytes 6152 | tf_op jit(solution)/shard_map/ppermute | solution.py:498
  13.2 0.7 %collective-permute-start.4 = (f32[2,256]{1,0:T(2,128)S(1)}, f32[2,256]{1,0:T(2,128)S(1)}, u32[]{:S(2)}, u32[]{:S(2)}) collective-permute-start(f32[2,256]{1,0:T(2,128)S(1)} %get-tuple-element.37), channel_id=1, source_target_pairs={{1,8},{2,9},{3,10},{4,11},{5,12},{6,13},{7,14}} | collective-permute-start | bytes 6152 | tf_op jit(solution)/shard_map/ppermute | solution.py:498
  13.9 0.0 collective-permute-done.2.low_ref
  13.9 0.6 %collective-permute-done.3.own_ref = f32[2,256]{1,0:T(2,128)S(1)} collective-permute-done((f32[2,256]{1,0:T(2,128)S(1)}, f32[2,256]{1,0:T(2,128)S(1)}, u32[]{:S(2)}, u32[]{:S(2)}) %collective-permute-start.3) | collective-permute-done | bytes 2080 | tf_op jit(solution)/shard_map/ppermute | solution.py:498
  14.4 0.0 collective-permute-done.4.high_ref
  14.5 0.7 %collective-permute-start.5 = (f32[2,256]{1,0:T(2,128)S(1)}, f32[2,256]{1,0:T(2,128)S(1)}, u32[]{:S(2)}, u32[]{:S(2)}) collective-permute-start(f32[2,256]{1,0:T(2,128)S(1)} %get-tuple-element.50), channel_id=1, source_target_pairs={{8,17},{9,18},{10,19},{11,20},{12,21},{13,22},{14,23}} | collective-permute-start | bytes 6152 | tf_op jit(solution)/shard_map/ppermute | solution.py:498
  15.1 0.7 %collective-permute-start.6 = (f32[2,256]{1,0:T(2,128)S(1)}, f32[2,256]{1,0:T(2,128)S(1)}, u32[]{:S(2)}, u32[]{:S(2)}) collective-permute-start(f32[2,256]{1,0:T(2,128)S(1)} %get-tuple-element.50), channel_id=1, source_target_pairs={{8,16},{9,17},{10,18},{11,19},{12,20},{13,21},{14,22},{15,23}} | collective-permute-start | bytes 6152 | tf_op jit(solution)/shard_map/ppermute | solution.py:498
  15.8 0.7 %collective-permute-start.7 = (f32[2,256]{1,0:T(2,128)S(1)}, f32[2,256]{1,0:T(2,128)S(1)}, u32[]{:S(2)}, u32[]{:S(2)}) collective-permute-start(f32[2,256]{1,0:T(2,128)S(1)} %get-tuple-element.50), channel_id=1, source_target_pairs={{9,16},{10,17},{11,18},{12,19},{13,20},{14,21},{15,22}} | collective-permute-start | bytes 6152 | tf_op jit(solution)/shard_map/ppermute | solution.py:498
  17.1 0.0 collective-permute-done.5.low_ref
  17.1 0.0 collective-permute-done.6.own_ref
  17.2 0.0 collective-permute-done.7.high_ref
  17.2 0.7 %collective-permute-start.10 = (f32[2,256]{1,0:T(2,128)S(1)}, f32[2,256]{1,0:T(2,128)S(1)}, u32[]{:S(2)}, u32[]{:S(2)}) collective-permute-start(f32[2,256]{1,0:T(2,128)S(1)} %get-tuple-element.54), channel_id=1, source_target_pairs={{17,24},{18,25},{19,26},{20,27},{21,28},{22,29},{23,30}} | collective-permute-start | bytes 6152 | tf_op jit(solution)/shard_map/ppermute | solution.py:498
  17.9 0.7 %collective-permute-start.8 = (f32[2,256]{1,0:T(2,128)S(1)}, f32[2,256]{1,0:T(2,128)S(1)}, u32[]{:S(2)}, u32[]{:S(2)}) collective-permute-start(f32[2,256]{1,0:T(2,128)S(1)} %get-tuple-element.54), channel_id=1, source_target_pairs={{16,25},{17,26},{18,27},{19,28},{20,29},{21,30},{22,31}} | collective-permute-start | bytes 6152 | tf_op jit(solution)/shard_map/ppermute | solution.py:498
  18.5 0.7 %collective-permute-start.9 = (f32[2,256]{1,0:T(2,128)S(1)}, f32[2,256]{1,0:T(2,128)S(1)}, u32[]{:S(2)}, u32[]{:S(2)}) collective-permute-start(f32[2,256]{1,0:T(2,128)S(1)} %get-tuple-element.54), channel_id=1, source_target_pairs={{16,24},{17,25},{18,26},{19,27},{20,28},{21,29},{22,30},{23,31}} | collective-permute-start | bytes 6152 | tf_op jit(solution)/shard_map/ppermute | solution.py:498
  19.2 0.1 pad_add_fusion.refs_0_.at_ref
  19.3 0.0 collective-permute-done.10.high_ref
  19.3 0.0 collective-permute-done.8.low_ref
  19.3 0.0 collective-permute-done.9.own_ref
  19.3 1.0 %shard_map.54 = (f32[2,256]{1,0:T(2,128)S(1)}, f32[2,50,256]{2,1,0:T(8,128)S(1)}, f32[32,8,128]{2,1,0:T(8,128)S(1)}) custom-call(s32[15,256]{1,0:T(8,128)S(1)} %get-tuple-element.33.idx_ref, f32[2,256]{1,0:T(2,128)S(1)} %collective-permute-done.8.low_ref, f32[2,256]{1,0:T(2,128)S(1)} %collective-permute-done.9.own_ref, ...), custom_call_target="tpu_custom_call" | custom-call | tf_op jit(solution)/shard_map/pallas_call | solution.py:508
  20.3 30.6 %all_to_all.5.got_ref = f32[32,8,128]{2,1,0:T(8,128)S(1)} all-to-all(f32[32,8,128]{2,1,0:T(8,128)S(1)} %get-tuple-element.60), channel_id=1, replica_groups=mesh['section'=4,'pix'=8] {'section','pix'}, dimensions={0} | all-to-all | bytes 262144 | tf_op jit(solution)/shard_map/all_to_all | solution.py:524
  50.9 1.4 %finish.1 = (f32[50,2,256]{2,1,0:T(2,128)}, f32[2,1,256]{2,1,0:T(1,128)}) custom-call(s32[2]{0:T(128)S(1)} %pad_add_fusion.refs_0_.at_ref, f32[2,50,256]{2,1,0:T(8,128)S(1)} %get-tuple-element.59.vec_ref, f32[32,8,128]{2,1,0:T(8,128)S(1)} %all_to_all.5.got_ref, f32[2,256]{1,0:T(2,128)S(1)} %get-tuple-element.61.comp_ref), custom_call_target="tpu_custom_call" | custom-call | tf_op jit(solution)/shard_map/finish/pallas_call | solution.py:525
  (3 shorter events, 0.0 us)
Async XLA Ops:
  0.6 2.8 %collective-permute-start = (f32[50,2,256]{2,1,0:T(2,128)}, f32[50,2,256]{2,1,0:T(2,128)S(1)}, u32[]{:S(2)}, u32[]{:S(2)}) collective-permute-start(f32[50,2,256]{2,1,0:T(2,128)} %bitcast.9), channel_id=1, source_target_pairs={{0,1},{2,3},{4,5},{6,7},{1,0},{3,2},{5,4},{7,6},{8,9},{10,11},{12,... | collective-permute-start | bytes 307208 | tf_op jit(solution)/shard_map/ppermute | solution.py:447
  1.2 2.3 %collective-permute-start.1 = (f32[50,2,256]{2,1,0:T(2,128)}, f32[50,2,256]{2,1,0:T(2,128)S(1)}, u32[]{:S(2)}, u32[]{:S(2)}) collective-permute-start(f32[50,2,256]{2,1,0:T(2,128)} %bitcast.10), channel_id=1, source_target_pairs={{1,2},{3,4},{5,6},{2,1},{4,3},{6,5},{9,10},{11,12},{13,14},{10,9},... | collective-permute-start | bytes 307208 | tf_op jit(solution)/shard_map/ppermute | solution.py:447
  8.7 5.1 %collective-permute-start.2 = (f32[2,256]{1,0:T(2,128)S(1)}, f32[2,256]{1,0:T(2,128)S(1)}, u32[]{:S(2)}, u32[]{:S(2)}) collective-permute-start(f32[2,256]{1,0:T(2,128)S(1)} %get-tuple-element.37), channel_id=1, source_target_pairs={{0,9},{1,10},{2,11},{3,12},{4,13},{5,14},{6,15}} | collective-permute-start | bytes 6152 | tf_op jit(solution)/shard_map/ppermute | solution.py:498
  11.9 2.6 %collective-permute-start.3 = (f32[2,256]{1,0:T(2,128)S(1)}, f32[2,256]{1,0:T(2,128)S(1)}, u32[]{:S(2)}, u32[]{:S(2)}) collective-permute-start(f32[2,256]{1,0:T(2,128)S(1)} %get-tuple-element.37), channel_id=1, source_target_pairs={{0,8},{1,9},{2,10},{3,11},{4,12},{5,13},{6,14},{7,15}} | collective-permute-start | bytes 6152 | tf_op jit(solution)/shard_map/ppermute | solution.py:498
  13.2 1.3 %collective-permute-start.4 = (f32[2,256]{1,0:T(2,128)S(1)}, f32[2,256]{1,0:T(2,128)S(1)}, u32[]{:S(2)}, u32[]{:S(2)}) collective-permute-start(f32[2,256]{1,0:T(2,128)S(1)} %get-tuple-element.37), channel_id=1, source_target_pairs={{1,8},{2,9},{3,10},{4,11},{5,12},{6,13},{7,14}} | collective-permute-start | bytes 6152 | tf_op jit(solution)/shard_map/ppermute | solution.py:498
  14.5 2.7 %collective-permute-start.5 = (f32[2,256]{1,0:T(2,128)S(1)}, f32[2,256]{1,0:T(2,128)S(1)}, u32[]{:S(2)}, u32[]{:S(2)}) collective-permute-start(f32[2,256]{1,0:T(2,128)S(1)} %get-tuple-element.50), channel_id=1, source_target_pairs={{8,17},{9,18},{10,19},{11,20},{12,21},{13,22},{14,23}} | collective-permute-start | bytes 6152 | tf_op jit(solution)/shard_map/ppermute | solution.py:498
  15.1 2.0 %collective-permute-start.6 = (f32[2,256]{1,0:T(2,128)S(1)}, f32[2,256]{1,0:T(2,128)S(1)}, u32[]{:S(2)}, u32[]{:S(2)}) collective-permute-start(f32[2,256]{1,0:T(2,128)S(1)} %get-tuple-element.50), channel_id=1, source_target_pairs={{8,16},{9,17},{10,18},{11,19},{12,20},{13,21},{14,22},{15,23}} | collective-permute-start | bytes 6152 | tf_op jit(solution)/shard_map/ppermute | solution.py:498
  15.8 1.4 %collective-permute-start.7 = (f32[2,256]{1,0:T(2,128)S(1)}, f32[2,256]{1,0:T(2,128)S(1)}, u32[]{:S(2)}, u32[]{:S(2)}) collective-permute-start(f32[2,256]{1,0:T(2,128)S(1)} %get-tuple-element.50), channel_id=1, source_target_pairs={{9,16},{10,17},{11,18},{12,19},{13,20},{14,21},{15,22}} | collective-permute-start | bytes 6152 | tf_op jit(solution)/shard_map/ppermute | solution.py:498
  17.2 2.1 %collective-permute-start.10 = (f32[2,256]{1,0:T(2,128)S(1)}, f32[2,256]{1,0:T(2,128)S(1)}, u32[]{:S(2)}, u32[]{:S(2)}) collective-permute-start(f32[2,256]{1,0:T(2,128)S(1)} %get-tuple-element.54), channel_id=1, source_target_pairs={{17,24},{18,25},{19,26},{20,27},{21,28},{22,29},{23,30}} | collective-permute-start | bytes 6152 | tf_op jit(solution)/shard_map/ppermute | solution.py:498
  17.9 1.4 %collective-permute-start.8 = (f32[2,256]{1,0:T(2,128)S(1)}, f32[2,256]{1,0:T(2,128)S(1)}, u32[]{:S(2)}, u32[]{:S(2)}) collective-permute-start(f32[2,256]{1,0:T(2,128)S(1)} %get-tuple-element.54), channel_id=1, source_target_pairs={{16,25},{17,26},{18,27},{19,28},{20,29},{21,30},{22,31}} | collective-permute-start | bytes 6152 | tf_op jit(solution)/shard_map/ppermute | solution.py:498
  18.5 0.8 %collective-permute-start.9 = (f32[2,256]{1,0:T(2,128)S(1)}, f32[2,256]{1,0:T(2,128)S(1)}, u32[]{:S(2)}, u32[]{:S(2)}) collective-permute-start(f32[2,256]{1,0:T(2,128)S(1)} %get-tuple-element.54), channel_id=1, source_target_pairs={{16,24},{17,25},{18,26},{19,27},{20,28},{21,29},{22,30},{23,31}} | collective-permute-start | bytes 6152 | tf_op jit(solution)/shard_map/ppermute | solution.py:498

commit v6 on v5

--- a/solution.py
+++ b/solution.py
@@ -17,7 +17,6 @@
 KP = 16
 SHRINK = 2.0**-35
 
-SMEM = pl.BlockSpec(memory_space=pltpu.SMEM)
 VMEM = pl.BlockSpec(memory_space=pltpu.VMEM)
 HBM = pl.BlockSpec(memory_space=pltpu.HBM)
 
@@ -250,7 +249,7 @@
         state_ref[5:8, half(h)] = jnp.zeros((3, LANES), jnp.float32)
 
 
-def own_kernel(idx_hbm, slc_hbm, zr_ref, zi_ref, own_ref, idx_ref, slc_ref, hl_ref, sems):
+def own_kernel(idx_hbm, slc_hbm, near_ref, zr_ref, zi_ref, own_ref, idx_ref, slc_ref, hl_ref, sems):
     copies = [
         pltpu.make_async_copy(slc_hbm, slc_ref, sems.at[0]),
         pltpu.make_async_copy(idx_hbm, idx_ref, sems.at[1]),
@@ -259,22 +258,21 @@
         copy.start()
     for copy in copies:
         copy.wait()
-    start = seat(slc_ref.shape[2], 0)[3]
-    gather(start, idx_ref, ((slc_ref, 0),), own_ref, hl_ref, zr_ref, zi_ref, False)
-
-
-def prepare_kernel(stack, first, idx_ref, near_ref, far_ref, own_ref, *refs):
+    _, _, _, start, near_at, _ = seat(slc_ref.shape[2], near_ref.shape[2])
+    gather(start, idx_ref, ((slc_ref, 0), (near_ref, near_at)), own_ref, hl_ref, zr_ref, zi_ref, False)
+
+
+def prepare_kernel(stack, first, idx_ref, far_ref, own_ref, *refs):
     refs = refs[2 if first else 7 :]
     zr_ref, zi_ref, gr_ref, gi_ref, sum_ref, beta_ref, state_ref = refs[:7]
     xs_ref, hl_ref, pair_ref = refs[-3:]
 
-    section, _, _, start, near_at, far_at = seat(zr_ref.shape[2], near_ref.shape[2])
+    section, _, _, start, _, far_at = seat(zr_ref.shape[2], far_ref.shape[2])
 
     @pl.when(section == 0 if first else section != 0)
     def _():
         count = zr_ref.shape[0]
-        pieces = ((near_ref, near_at), (far_ref, far_at))
-        gather(start, idx_ref, pieces, xs_ref, hl_ref, zr_ref, zi_ref, True)
+        gather(start, idx_ref, ((far_ref, far_at),), xs_ref, hl_ref, zr_ref, zi_ref, True)
         scale_dates(zr_ref, zi_ref)
         gram(pair_ref, zr_ref, zi_ref, own_ref, gr_ref, gi_ref, sum_ref)
         if first:
@@ -296,7 +294,7 @@
     last = len(refs) > 5
     if last:
         late, (comp_ref, *made), refs = refs[:3], refs[3:6], refs[6:]
-        fr_ref, fi_ref, beta_ref, state_ref, turned_ref = refs
+        fr_ref, fi_ref, beta_ref, state_ref = refs
     else:
         beta_ref, state_ref, comp_ref, fr_ref, fi_ref = refs
     count = gr_ref.shape[0] - 1
@@ -347,14 +345,23 @@
 
     comp_ref[...] = state_ref[0:2]
     if last:
-        vectors(*late, beta_ref, state_ref, *made, turned_ref)
-
-
-def vectors(at_ref, zr_ref, zi_ref, beta_ref, state_ref, vec_ref, slot_ref, turned_ref):
+        vectors(*late, beta_ref, state_ref, *made)
+
+
+def slot_rows(halves):
+    return 2 * halves + 1
+
+
+def vectors(pixel_ref, zr_ref, zi_ref, beta_ref, state_ref, vec_ref, slot_ref):
     count, rows, pixels = zr_ref.shape
     dates = vec_ref.shape[1]
-    local = at_ref[0]
-    for h in range(pixels // LANES):
+    halves = pixels // LANES
+    _, _, _, start, _, _ = seat(pixels, 0)
+    local = pixel_ref[...] - start
+    lane = lax.broadcasted_iota(jnp.int32, (SUB, LANES), 1)
+    row = lax.broadcasted_iota(jnp.int32, (SUB, LANES), 0)
+    at_pixel = [jnp.zeros((SUB, LANES), jnp.float32) for _ in range(2)]
+    for h in range(halves):
         a = state_ref[4:5, half(h)]
         acc_r = [jnp.broadcast_to(a, (SUB, LANES)) for _ in range(0, rows, SUB)]
         acc_i = [jnp.zeros((SUB, LANES), jnp.float32) for _ in range(0, rows, SUB)]
@@ -370,36 +377,45 @@
             whole = jnp.concatenate(acc, axis=0)
             vec_ref[c, :, half(h)] = whole[0:dates]
             wide = jnp.concatenate([whole, jnp.zeros((up(rows, LANES) - rows, LANES), jnp.float32)], axis=0)
-            turned_ref[c, half(h)] = jnp.transpose(wide)
-    slot = [jnp.zeros((1, LANES), jnp.float32)] * slot_ref.shape[1]
-    lane = lax.broadcasted_iota(jnp.int32, (1, LANES), 1)
-    halves = pixels // LANES
+            turned = jnp.transpose(wide)
+            for r in range(0, LANES, SUB):
+                at_pixel[c] = at_pixel[c] + jnp.where(row == local - (h * LANES + r), turned[r : r + SUB], 0.0)
+    slot = [state_ref[2 + c : 3 + c, half(h)] for c in range(2) for h in range(halves)]
+    mixed = colsum(at_pixel[0]) + pltpu.roll(jnp.broadcast_to(colsum(at_pixel[1]), (SUB, LANES)), LANES // 2, 1)[0:1]
     for c in range(2):
-        for h in range(halves):
-            slot[c * halves + h] = state_ref[2 + c : 3 + c, half(h)]
-        slot[2 * halves + c] = turned_ref[c, pl.ds(local, 1), :]
         picked = jnp.zeros((1, LANES), jnp.float32)
         for h in range(halves):
-            picked = picked + jnp.where(lane == local - h * LANES, state_ref[2 + c : 3 + c, half(h)], 0.0)
-        slot[2 * halves + 2 + c] = jnp.broadcast_to(jnp.sum(picked, axis=1, keepdims=True), (1, LANES))
-    slot = jnp.concatenate(slot, axis=0)
+            picked = picked + jnp.where((lane == local - h * LANES)[0:1], state_ref[2 + c : 3 + c, half(h)], 0.0)
+        f = jnp.sum(picked, axis=1, keepdims=True)
+        mixed = jnp.where(lane[0:1] == LANES - 2 + c, jnp.broadcast_to(f, (1, LANES)), mixed)
+    slot.append(mixed)
     for n in range(slot_ref.shape[0]):
-        slot_ref[n] = slot
-
-
-def finish_kernel(sections, at_ref, vec_ref, got_ref, comp_ref, out_ref, small_ref):
+        for m, one in enumerate(slot):
+            slot_ref[n, m] = one
+
+
+def finish_kernel(sections, pixel_ref, vec_ref, got_ref, comp_ref, out_ref, small_ref):
     small_ref[:, 0] = comp_ref[...]
     dates, pixels = vec_ref.shape[1:]
     section, mine, blocks, _, _, _ = seat(pixels, 0)
-    root = at_ref[1]
     halves = pixels // LANES
     one = jnp.ones((1, LANES), jnp.float32)
+    lane = lax.broadcasted_iota(jnp.int32, (1, LANES), 1)
+
+    def of_pixel(s):
+        total = jnp.zeros((1, LANES), jnp.float32)
+        for q in range(blocks):
+            first = pixel_ref[0:1] - q * pixels
+            here = jnp.logical_and(first >= 0, first < pixels)
+            total = total + jnp.where(here, got_ref[s * blocks + q, 2 * halves], 0.0)
+        return total
+
     datum = [(one, 0.0 * one) for _ in range(halves)]
-    at_root = (one, 0.0 * one)
+    at_pixel = (one, 0.0 * one)
     for s in range(sections - 1, 0, -1):
         later = section < s
-        own = got_ref[s * blocks + mine]
-        ref = got_ref[s * blocks + root]
+        own = [got_ref[s * blocks + mine, m] for m in range(2 * halves)]
+        row = of_pixel(s)
 
         def times(d, fr, fi):
             fr = jnp.where(later, fr, 1.0)
@@ -407,11 +423,12 @@
             return (d[0] * fr - d[1] * fi, d[0] * fi + d[1] * fr)
 
         for h in range(halves):
-            datum[h] = times(datum[h], own[h : h + 1], own[halves + h : halves + h + 1])
-        at_root = times(at_root, ref[2 * halves + 2 : 2 * halves + 3], ref[2 * halves + 3 : 2 * halves + 4])
-    ref = got_ref[section * blocks + root]
-    vr, vi = ref[2 * halves : 2 * halves + 1], ref[2 * halves + 1 : 2 * halves + 2]
-    ur, ui = unit(vr * at_root[0] - vi * at_root[1], vr * at_root[1] + vi * at_root[0])
+            datum[h] = times(datum[h], own[h], own[halves + h])
+        f = [jnp.sum(jnp.where(lane == LANES - 2 + c, row, 0.0), axis=1, keepdims=True) for c in range(2)]
+        at_pixel = times(at_pixel, *[jnp.broadcast_to(x, (1, LANES)) for x in f])
+    vr = of_pixel(section)
+    vi = pltpu.roll(jnp.broadcast_to(vr, (SUB, LANES)), LANES // 2, 1)[0:1]
+    ur, ui = unit(vr * at_pixel[0] - vi * at_pixel[1], vr * at_pixel[1] + vi * at_pixel[0])
     gain = math.sqrt(dates + 1)
     ur = jnp.transpose(jnp.broadcast_to(ur * gain, (LANES, LANES)))[0:dates]
     ui = jnp.transpose(jnp.broadcast_to(ui * gain, (LANES, LANES)))[0:dates]
@@ -456,34 +473,34 @@
     ]
     zr, zi, own, neighbours = pl.pallas_call(
         own_kernel,
-        out_shape=made[:2] + [f32(2 * rows, pixels), jax.ShapeDtypeStruct(neighbours.shape, jnp.int32)],
-        in_specs=[HBM, HBM],
+        out_shape=made[:2] + [f32(2 * rows, pixels + reach), jax.ShapeDtypeStruct(neighbours.shape, jnp.int32)],
+        in_specs=[HBM, HBM, VMEM],
         out_specs=[VMEM] * 4,
         scratch_shapes=[
             pltpu.VMEM((dates, 2, pixels), jnp.float32),
-            pltpu.VMEM((4 * rows, pixels), jnp.bfloat16),
+            pltpu.VMEM((4 * rows, pixels + reach), jnp.bfloat16),
             pltpu.SemaphoreType.DMA((2,)),
         ],
         compiler_params=params(),
-        cost_estimate=cost(2 * 4 * rows * pixels * pixels * count),
+        cost_estimate=cost(2 * 4 * rows * pixels * (pixels + reach) * count),
         name="own",
-    )(pltpu.with_memory_space_constraint(neighbours, pltpu.HBM), pltpu.with_memory_space_constraint(slc, pltpu.HBM))
+    )(pltpu.with_memory_space_constraint(neighbours, pltpu.HBM), pltpu.with_memory_space_constraint(slc, pltpu.HBM), near)
 
     def prepare(first, carried):
         return pl.pallas_call(
             functools.partial(prepare_kernel, stack, first),
             out_shape=made[: 8 if first else 7],
-            in_specs=[VMEM] * (4 + len(carried)),
+            in_specs=[VMEM] * (3 + len(carried)),
             out_specs=[VMEM] * (8 if first else 7),
             scratch_shapes=[
-                pltpu.VMEM((2 * rows, 2 * reach), jnp.float32),
-                pltpu.VMEM((4 * rows, 2 * reach), jnp.bfloat16),
+                pltpu.VMEM((2 * rows, reach), jnp.float32),
+                pltpu.VMEM((4 * rows, reach), jnp.bfloat16),
                 pltpu.VMEM((2, count + 1, count, SUB, LANES), jnp.float32),
             ],
-            input_output_aliases={4 + n: n for n in range(len(carried))},
+            input_output_aliases={3 + n: n for n in range(len(carried))},
             compiler_params=params(),
             cost_estimate=cost(50 * 12 * rows * reach * pixels * count),
-        )(neighbours, near, far, own, *carried)
+        )(neighbours, far, own, *carried)
 
     *made_0, comp = prepare(True, (zr, zi))
     zr, zi, gr, gi, sums, beta, state = prepare(False, made_0)
@@ -502,9 +519,9 @@
         scratch = [pltpu.VMEM((count, halves, KP, LANES), jnp.float32)] * 2
         outs = [f32(2, halves, KP, LANES), f32(SUB, pixels), f32(2, pixels)]
         if last:
-            late, specs = (ref_at, zr, zi), [SMEM, VMEM, VMEM]
-            scratch += [pltpu.VMEM(o.shape, o.dtype) for o in outs[:2]] + [pltpu.VMEM((2, pixels, LANES), jnp.float32)]
-            outs = outs[2:] + [f32(2, dates, pixels), f32(sections * blocks, up(2 * halves + 4, SUB), LANES)]
+            late, specs = (ref_at, zr, zi), [VMEM] * 3
+            scratch += [pltpu.VMEM(o.shape, o.dtype) for o in outs[:2]]
+            outs = outs[2:] + [f32(2, dates, pixels), f32(sections * blocks, slot_rows(halves), 1, LANES)]
         made = pl.pallas_call(
             functools.partial(round_kernel, rnd, stack),
             out_shape=outs,
@@ -519,13 +536,13 @@
             beta, state, comp = made
         if rnd == 1:
             pixel = lax.optimization_barrier((reference_pixel, comp))[0][0]
-            ref_at = jnp.stack([pixel % pixels, pixel // pixels]).astype(jnp.int32)
+            ref_at = jnp.full((SUB, LANES), pixel, jnp.int32)
 
     got = lax.all_to_all(sent, ("section", "pix"), 0, 0, tiled=True)
     out, small = pl.pallas_call(
         functools.partial(finish_kernel, sections),
         out_shape=[f32(dates, 2, pixels), f32(2, 1, pixels)],
-        in_specs=[SMEM] + [VMEM] * 3,
+        in_specs=[VMEM] * 4,
         out_specs=[VMEM] * 2,
         compiler_params=params(),
         name="finish",

time: 52.6 us -> 50.6 us (0.962)
  Pallas kernels: 9.23 us -> 8.3 us
  blocking collectives: 30.6 us -> 29.7 us
    all_to_all x1, blocking collectives: 30.6 us -> 29.7 us  [on_device(): got = lax.all_to_all(sent, ('section', 'pix'), 0, 0, tiled=True)]
  transfers between devices with their start and end apart: 11 -> 11, of which waited for: 1 -> 2; matrix products, arithmetic and copies ran while one was open for 0% -> 0% of each run, Pallas kernels for 3% -> 4%
where the time goes in v6:
time: 50.6 us; the launch traced here: 50.3 us
  blocking collectives  29.7 us (59%)
  starting transfers between devices  9.75 us (19%)
  Pallas kernels  8.3 us (16%)
  between operations  1.47 us (3%)
  waiting for transfers between devices  1.1 us (2%)
    all_to_all x1, blocking collectives, on_device(): got = lax.all_to_all(sent, ('section', 'pix'), 0, 0, tiled=True)  29.7 us
    ppermute x9, starting transfers between devices, hop(): return lax.ppermute(comp, ('section', 'pix'), pairs)  8.53 us
    pallas_call x2, Pallas kernels, prepare(): pl.pallas_call(functools.partial(prepare_kernel, stack, first), out_shape...  4.83 us
    pallas_call x1, Pallas kernels, on_device(): pl.pallas_call(own_kernel, out_shape=made[:2] + [f32(2 * rows, pixels + r...  2.04 us
    ppermute x2, starting transfers between devices, swap(): return lax.ppermute(sent, 'pix', pairs)  1.21 us
  transfers between devices with their start and end apart: 11, of which 2 were waited for; matrix products, arithmetic and copies ran while one was open for 0% of the time, Pallas kernels for 4%

profile of v6, /device:TPU:0, one launch (start us, length us, event | category | flops | bytes accessed | tf_op | source)
XLA Modules:
  0.0 50.3 jit_solution(1614035182312006655)
XLA Ops:
  0.6 0.6 %collective-permute-start = (f32[50,2,256]{2,1,0:T(2,128)}, f32[50,2,256]{2,1,0:T(2,128)S(1)}, u32[]{:S(2)}, u32[]{:S(2)}) collective-permute-start(f32[50,2,256]{2,1,0:T(2,128)} %bitcast.4), channel_id=1, source_target_pairs={{0,1},{2,3},{4,5},{6,7},{1,0},{3,2},{5,4},{7,6},{8,9},{10,11},{12,... | collective-permute-start | bytes 307208 | tf_op jit(solution)/shard_map/ppermute | solution.py:464
  1.2 0.7 %collective-permute-start.1 = (f32[50,2,256]{2,1,0:T(2,128)}, f32[50,2,256]{2,1,0:T(2,128)S(1)}, u32[]{:S(2)}, u32[]{:S(2)}) collective-permute-start(f32[50,2,256]{2,1,0:T(2,128)} %bitcast.5), channel_id=1, source_target_pairs={{1,2},{3,4},{5,6},{2,1},{4,3},{6,5},{9,10},{11,12},{13,14},{10,9},... | collective-permute-start | bytes 307208 | tf_op jit(solution)/shard_map/ppermute | solution.py:464
  1.9 0.5 collective-permute-done.near_ref
  2.3 2.0 %own.1 = (f32[15,56,256]{2,1,0:T(8,128)S(1)}, f32[15,56,256]{2,1,0:T(8,128)S(1)}, f32[112,512]{1,0:T(8,128)S(1)}, s32[15,256]{1,0:T(8,128)S(1)}) custom-call(s32[15,256]{1,0:T(8,128)} %idx_hbm.1, f32[50,2,256]{2,1,0:T(2,128)} %bitcast.6, f32[50,2,256]{2,1,0:T(2,128)S(1)} %collective-permute-done.near_ref), custom_call_target="tpu_custom_call" | custom-call | flops 880803840 | tf_op jit(solution)/shard_map/own/pallas_call | solution.py:474
  4.4 0.0 collective-permute-done.1.far_ref
  4.4 4.8 %shard_map.50 = (f32[15,56,256]{2,1,0:T(8,128)S(1)}, f32[15,56,256]{2,1,0:T(8,128)S(1)}, f32[16,2,16,128]{3,2,1,0:T(8,128)S(1)}, f32[16,2,16,128]{3,2,1,0:T(8,12...) custom-call(s32[15,256]{1,0:T(8,128)S(1)} %get-tuple-element.33.idx_, ...), custom_call_target="tpu_custom_call", output_to_operand_aliasing={{0}: (3, {}), {1}: (4, {})} | custom-call | flops 33030144000 | tf_op jit(solution)/shard_map/pallas_call | solution.py:490
  9.2 2.6 %collective-permute-start.2 = (f32[2,256]{1,0:T(2,128)S(1)}, f32[2,256]{1,0:T(2,128)S(1)}, u32[]{:S(2)}, u32[]{:S(2)}) collective-permute-start(f32[2,256]{1,0:T(2,128)S(1)} %get-tuple-element.37), channel_id=1, source_target_pairs={{0,9},{1,10},{2,11},{3,12},{4,13},{5,14},{6,15}} | collective-permute-start | bytes 6152 | tf_op jit(solution)/shard_map/ppermute | solution.py:515
  11.9 1.3 %collective-permute-start.3 = (f32[2,256]{1,0:T(2,128)S(1)}, f32[2,256]{1,0:T(2,128)S(1)}, u32[]{:S(2)}, u32[]{:S(2)}) collective-permute-start(f32[2,256]{1,0:T(2,128)S(1)} %get-tuple-element.37), channel_id=1, source_target_pairs={{0,8},{1,9},{2,10},{3,11},{4,12},{5,13},{6,14},{7,15}} | collective-permute-start | bytes 6152 | tf_op jit(solution)/shard_map/ppermute | solution.py:515
  13.2 0.7 %collective-permute-start.4 = (f32[2,256]{1,0:T(2,128)S(1)}, f32[2,256]{1,0:T(2,128)S(1)}, u32[]{:S(2)}, u32[]{:S(2)}) collective-permute-start(f32[2,256]{1,0:T(2,128)S(1)} %get-tuple-element.37), channel_id=1, source_target_pairs={{1,8},{2,9},{3,10},{4,11},{5,12},{6,13},{7,14}} | collective-permute-start | bytes 6152 | tf_op jit(solution)/shard_map/ppermute | solution.py:515
  13.9 0.0 collective-permute-done.2.low_ref
  13.9 0.6 %collective-permute-done.3.own_ref = f32[2,256]{1,0:T(2,128)S(1)} collective-permute-done((f32[2,256]{1,0:T(2,128)S(1)}, f32[2,256]{1,0:T(2,128)S(1)}, u32[]{:S(2)}, u32[]{:S(2)}) %collective-permute-start.3) | collective-permute-done | bytes 2080 | tf_op jit(solution)/shard_map/ppermute | solution.py:515
  14.4 0.0 collective-permute-done.4.high_ref
  14.5 0.7 %collective-permute-start.5 = (f32[2,256]{1,0:T(2,128)S(1)}, f32[2,256]{1,0:T(2,128)S(1)}, u32[]{:S(2)}, u32[]{:S(2)}) collective-permute-start(f32[2,256]{1,0:T(2,128)S(1)} %get-tuple-element.50), channel_id=1, source_target_pairs={{8,17},{9,18},{10,19},{11,20},{12,21},{13,22},{14,23}} | collective-permute-start | bytes 6152 | tf_op jit(solution)/shard_map/ppermute | solution.py:515
  15.1 0.7 %collective-permute-start.6 = (f32[2,256]{1,0:T(2,128)S(1)}, f32[2,256]{1,0:T(2,128)S(1)}, u32[]{:S(2)}, u32[]{:S(2)}) collective-permute-start(f32[2,256]{1,0:T(2,128)S(1)} %get-tuple-element.50), channel_id=1, source_target_pairs={{8,16},{9,17},{10,18},{11,19},{12,20},{13,21},{14,22},{15,23}} | collective-permute-start | bytes 6152 | tf_op jit(solution)/shard_map/ppermute | solution.py:515
  15.8 0.7 %collective-permute-start.7 = (f32[2,256]{1,0:T(2,128)S(1)}, f32[2,256]{1,0:T(2,128)S(1)}, u32[]{:S(2)}, u32[]{:S(2)}) collective-permute-start(f32[2,256]{1,0:T(2,128)S(1)} %get-tuple-element.50), channel_id=1, source_target_pairs={{9,16},{10,17},{11,18},{12,19},{13,20},{14,21},{15,22}} | collective-permute-start | bytes 6152 | tf_op jit(solution)/shard_map/ppermute | solution.py:515
  16.5 0.0 collective-permute-done.5.low_ref
  16.5 0.0 collective-permute-done.6.own_ref
  16.5 0.0 collective-permute-done.7.high_ref
  16.5 0.7 %collective-permute-start.10 = (f32[2,256]{1,0:T(2,128)S(1)}, f32[2,256]{1,0:T(2,128)S(1)}, u32[]{:S(2)}, u32[]{:S(2)}) collective-permute-start(f32[2,256]{1,0:T(2,128)S(1)} %get-tuple-element.54), channel_id=1, source_target_pairs={{17,24},{18,25},{19,26},{20,27},{21,28},{22,29},{23,30}} | collective-permute-start | bytes 6152 | tf_op jit(solution)/shard_map/ppermute | solution.py:515
  17.2 0.7 %collective-permute-start.8 = (f32[2,256]{1,0:T(2,128)S(1)}, f32[2,256]{1,0:T(2,128)S(1)}, u32[]{:S(2)}, u32[]{:S(2)}) collective-permute-start(f32[2,256]{1,0:T(2,128)S(1)} %get-tuple-element.54), channel_id=1, source_target_pairs={{16,25},{17,26},{18,27},{19,28},{20,29},{21,30},{22,31}} | collective-permute-start | bytes 6152 | tf_op jit(solution)/shard_map/ppermute | solution.py:515
  17.9 0.7 %collective-permute-start.9 = (f32[2,256]{1,0:T(2,128)S(1)}, f32[2,256]{1,0:T(2,128)S(1)}, u32[]{:S(2)}, u32[]{:S(2)}) collective-permute-start(f32[2,256]{1,0:T(2,128)S(1)} %get-tuple-element.54), channel_id=1, source_target_pairs={{16,24},{17,25},{18,26},{19,27},{20,28},{21,29},{22,30},{23,31}} | collective-permute-start | bytes 6152 | tf_op jit(solution)/shard_map/ppermute | solution.py:515
  19.2 0.0 collective-permute-done.10.high_ref
  19.2 0.0 collective-permute-done.8.low_ref
  19.2 0.0 collective-permute-done.9.own_ref
  19.2 0.5 shard_map.54
  19.7 29.7 %all_to_all.5.got_ref = f32[32,5,1,128]{3,2,1,0:T(1,128)S(1)} all-to-all(f32[32,5,1,128]{3,2,1,0:T(1,128)S(1)} %get-tuple-element.60), channel_id=1, replica_groups=mesh['section'=4,'pix'=8] {'section','pix'}, dimensions={0} | all-to-all | bytes 163840 | tf_op jit(solution)/shard_map/all_to_all | solution.py:541
  49.4 0.9 %finish.1 = (f32[50,2,256]{2,1,0:T(2,128)}, f32[2,1,256]{2,1,0:T(1,128)}) custom-call(s32[8,128]{1,0:T(8,128)S(1)} %broadcast_in_dim.3.refs_0_.pixel_ref, f32[2,50,256]{2,1,0:T(8,128)S(1)} %get-tuple-element.59.vec_ref, f32[32,5,1,128]{3,2,1,0:T(1,128)S(1)} %all_to_all.5.got_ref, f32[2,256]{1,0:T(2,128)S(1)} %get-tuple-element.61.comp_ref), custom_call_target="tpu_custom_call" | custom-call | tf_op jit(solution)/shard_map/finish/pallas_call | solution.py:542
  (4 shorter events, 0.1 us)
Async XLA Ops:
  0.6 1.7 %collective-permute-start = (f32[50,2,256]{2,1,0:T(2,128)}, f32[50,2,256]{2,1,0:T(2,128)S(1)}, u32[]{:S(2)}, u32[]{:S(2)}) collective-permute-start(f32[50,2,256]{2,1,0:T(2,128)} %bitcast.4), channel_id=1, source_target_pairs={{0,1},{2,3},{4,5},{6,7},{1,0},{3,2},{5,4},{7,6},{8,9},{10,11},{12,... | collective-permute-start | bytes 307208 | tf_op jit(solution)/shard_map/ppermute | solution.py:464
  1.2 3.2 %collective-permute-start.1 = (f32[50,2,256]{2,1,0:T(2,128)}, f32[50,2,256]{2,1,0:T(2,128)S(1)}, u32[]{:S(2)}, u32[]{:S(2)}) collective-permute-start(f32[50,2,256]{2,1,0:T(2,128)} %bitcast.5), channel_id=1, source_target_pairs={{1,2},{3,4},{5,6},{2,1},{4,3},{6,5},{9,10},{11,12},{13,14},{10,9},... | collective-permute-start | bytes 307208 | tf_op jit(solution)/shard_map/ppermute | solution.py:464
  9.2 4.6 %collective-permute-start.2 = (f32[2,256]{1,0:T(2,128)S(1)}, f32[2,256]{1,0:T(2,128)S(1)}, u32[]{:S(2)}, u32[]{:S(2)}) collective-permute-start(f32[2,256]{1,0:T(2,128)S(1)} %get-tuple-element.37), channel_id=1, source_target_pairs={{0,9},{1,10},{2,11},{3,12},{4,13},{5,14},{6,15}} | collective-permute-start | bytes 6152 | tf_op jit(solution)/shard_map/ppermute | solution.py:515
  11.9 2.6 %collective-permute-start.3 = (f32[2,256]{1,0:T(2,128)S(1)}, f32[2,256]{1,0:T(2,128)S(1)}, u32[]{:S(2)}, u32[]{:S(2)}) collective-permute-start(f32[2,256]{1,0:T(2,128)S(1)} %get-tuple-element.37), channel_id=1, source_target_pairs={{0,8},{1,9},{2,10},{3,11},{4,12},{5,13},{6,14},{7,15}} | collective-permute-start | bytes 6152 | tf_op jit(solution)/shard_map/ppermute | solution.py:515
  13.2 1.3 %collective-permute-start.4 = (f32[2,256]{1,0:T(2,128)S(1)}, f32[2,256]{1,0:T(2,128)S(1)}, u32[]{:S(2)}, u32[]{:S(2)}) collective-permute-start(f32[2,256]{1,0:T(2,128)S(1)} %get-tuple-element.37), channel_id=1, source_target_pairs={{1,8},{2,9},{3,10},{4,11},{5,12},{6,13},{7,14}} | collective-permute-start | bytes 6152 | tf_op jit(solution)/shard_map/ppermute | solution.py:515
  14.5 2.0 %collective-permute-start.5 = (f32[2,256]{1,0:T(2,128)S(1)}, f32[2,256]{1,0:T(2,128)S(1)}, u32[]{:S(2)}, u32[]{:S(2)}) collective-permute-start(f32[2,256]{1,0:T(2,128)S(1)} %get-tuple-element.50), channel_id=1, source_target_pairs={{8,17},{9,18},{10,19},{11,20},{12,21},{13,22},{14,23}} | collective-permute-start | bytes 6152 | tf_op jit(solution)/shard_map/ppermute | solution.py:515
  15.1 1.4 %collective-permute-start.6 = (f32[2,256]{1,0:T(2,128)S(1)}, f32[2,256]{1,0:T(2,128)S(1)}, u32[]{:S(2)}, u32[]{:S(2)}) collective-permute-start(f32[2,256]{1,0:T(2,128)S(1)} %get-tuple-element.50), channel_id=1, source_target_pairs={{8,16},{9,17},{10,18},{11,19},{12,20},{13,21},{14,22},{15,23}} | collective-permute-start | bytes 6152 | tf_op jit(solution)/shard_map/ppermute | solution.py:515
  15.8 0.7 %collective-permute-start.7 = (f32[2,256]{1,0:T(2,128)S(1)}, f32[2,256]{1,0:T(2,128)S(1)}, u32[]{:S(2)}, u32[]{:S(2)}) collective-permute-start(f32[2,256]{1,0:T(2,128)S(1)} %get-tuple-element.50), channel_id=1, source_target_pairs={{9,16},{10,17},{11,18},{12,19},{13,20},{14,21},{15,22}} | collective-permute-start | bytes 6152 | tf_op jit(solution)/shard_map/ppermute | solution.py:515
  16.5 2.7 %collective-permute-start.10 = (f32[2,256]{1,0:T(2,128)S(1)}, f32[2,256]{1,0:T(2,128)S(1)}, u32[]{:S(2)}, u32[]{:S(2)}) collective-permute-start(f32[2,256]{1,0:T(2,128)S(1)} %get-tuple-element.54), channel_id=1, source_target_pairs={{17,24},{18,25},{19,26},{20,27},{21,28},{22,29},{23,30}} | collective-permute-start | bytes 6152 | tf_op jit(solution)/shard_map/ppermute | solution.py:515
  17.2 2.0 %collective-permute-start.8 = (f32[2,256]{1,0:T(2,128)S(1)}, f32[2,256]{1,0:T(2,128)S(1)}, u32[]{:S(2)}, u32[]{:S(2)}) collective-permute-start(f32[2,256]{1,0:T(2,128)S(1)} %get-tuple-element.54), channel_id=1, source_target_pairs={{16,25},{17,26},{18,27},{19,28},{20,29},{21,30},{22,31}} | collective-permute-start | bytes 6152 | tf_op jit(solution)/shard_map/ppermute | solution.py:515
  17.9 1.3 %collective-permute-start.9 = (f32[2,256]{1,0:T(2,128)S(1)}, f32[2,256]{1,0:T(2,128)S(1)}, u32[]{:S(2)}, u32[]{:S(2)}) collective-permute-start(f32[2,256]{1,0:T(2,128)S(1)} %get-tuple-element.54), channel_id=1, source_target_pairs={{16,24},{17,25},{18,26},{19,27},{20,28},{21,29},{22,30},{23,31}} | collective-permute-start | bytes 6152 | tf_op jit(solution)/shard_map/ppermute | solution.py:515

commit v7 on v6

--- a/solution.py
+++ b/solution.py
@@ -15,6 +15,7 @@
 LANES = 128
 SUB = 8
 KP = 16
+Z_LANE, Z_STEP = 20, 54
 SHRINK = 2.0**-35
 
 VMEM = pl.BlockSpec(memory_space=pltpu.VMEM)
@@ -209,13 +210,13 @@
     return b, g, product(b, g)
 
 
-def solve(virtual, gr_ref, gi_ref, hr, hi, sum_ref, stack, beta_ref, state_ref):
+def solve(virtual, gr_ref, gi_ref, hr, hi, sums, stack, beta_ref, state_ref):
     halves = gr_ref.shape[1]
     count = gr_ref.shape[0]
     first = 1.0 / math.sqrt(stack)
     g0 = []
     for h in range(halves):
-        zr, zi = sum_ref[0, h], sum_ref[1, h]
+        zr, zi = sums[h]
         row = lax.broadcasted_iota(jnp.int32, (KP, LANES), 0)
         zr = jnp.where(row < count, zr, 0.0)
         zi = jnp.where(row < count, zi, 0.0)
@@ -230,7 +231,7 @@
         br, bi = b[h][0] * inv, b[h][1] * inv
         a = inv * (SHRINK * first)
         xr, xi = hr[h], hi[h]
-        sr, si = sum_ref[0, h][count : count + 1], sum_ref[1, h][count : count + 1]
+        sr, si = (x[count : count + 1] for x in sums[h])
         fr, fi = a, jnp.zeros_like(a)
         if virtual is not None:
             (wr, wi), (zr, zi) = virtual[h]
@@ -263,6 +264,8 @@
 
 
 def prepare_kernel(stack, first, idx_ref, far_ref, own_ref, *refs):
+    if not first:
+        pixel_ref, refs = refs[0], refs[1:]
     refs = refs[2 if first else 7 :]
     zr_ref, zi_ref, gr_ref, gi_ref, sum_ref, beta_ref, state_ref = refs[:7]
     xs_ref, hl_ref, pair_ref = refs[-3:]
@@ -279,12 +282,100 @@
             halves = gr_ref.shape[1]
             hr = [gr_ref[count, h] for h in range(halves)]
             hi = [gi_ref[count, h] for h in range(halves)]
-            solve(None, gr_ref.at[0:count], gi_ref.at[0:count], hr, hi, sum_ref, stack, beta_ref, state_ref)
+            sums = [(sum_ref[0, h], sum_ref[1, h]) for h in range(halves)]
+            solve(None, gr_ref.at[0:count], gi_ref.at[0:count], hr, hi, sums, stack, beta_ref, state_ref)
             refs[7][...] = state_ref[0:2]
+
+    if not first:
+
+        @pl.when(section == lax.axis_size("section") - 1)
+        def _():
+            fold(start, pixel_ref, idx_ref, zr_ref, zi_ref, gr_ref, gi_ref, sum_ref, refs[7], refs[8])
+
+
+def fold(start, pixel_ref, idx_ref, zr_ref, zi_ref, gr_ref, gi_ref, sum_ref, fold_ref, tile_ref):
+    count, rows, pixels = zr_ref.shape
+    halves = pixels // LANES
+    k_row = lax.broadcasted_iota(jnp.int32, (KP, LANES), 0)
+    lane = lax.broadcasted_iota(jnp.int32, (KP, LANES), 1)
+    local = pixel_ref[...] - start
+    hit = [lax.broadcasted_iota(jnp.int32, (SUB, LANES), 1) == local - h * LANES for h in range(halves)]
+
+    def column(parts):
+        total = None
+        for h, part in enumerate(parts):
+            mask = jnp.concatenate([hit[h]] * (part.shape[0] // SUB), axis=0)
+            part = jnp.where(mask, part, 0.0)
+            total = part if total is None else total + part
+        return jnp.broadcast_to(jnp.sum(total, axis=1, keepdims=True), total.shape)
+
+    tile = jnp.zeros((KP, LANES), jnp.float32)
+    for l in range(count + 2):
+        parts = []
+        for h in range(halves):
+            if l < count:
+                part = jnp.where(k_row <= l, gr_ref[l, h], gi_ref[l, h])
+            else:
+                part = sum_ref[l - count, h]
+            fold_ref[l, h] = part
+            parts.append(part)
+        tile = jnp.where(lane == (l if l < count else KP + l - count), column(parts), tile)
+    pad = jnp.zeros((KP - count, LANES), jnp.float32)
+    near = [jnp.concatenate([idx_ref[:, half(h)].astype(jnp.float32), pad], axis=0) for h in range(halves)]
+    tile = jnp.where(lane == KP + 2, column(near), tile)
+    wide = lax.broadcasted_iota(jnp.int32, (rows, LANES), 1)
+    empty = jnp.zeros((LANES - rows, LANES), jnp.float32)
+    for c, ref in ((0, zr_ref), (1, zi_ref)):
+        both = jnp.zeros((rows, LANES), jnp.float32)
+        for k in range(count):
+            both = jnp.where(wide == k, column([ref[k, :, half(h)] for h in range(halves)]), both)
+        turned = jnp.transpose(jnp.concatenate([both, empty], axis=0))[0:KP]
+        at = Z_LANE + c * Z_STEP
+        tile = jnp.where(jnp.logical_and(lane >= at, lane < at + Z_STEP), pltpu.roll(turned, at, 1), tile)
+    tile_ref[...] = tile
 
 
 def lane_take(x, i):
     return jnp.take_along_axis(x, i, axis=1, mode="promise_in_bounds")
+
+
+def scaled(own, zr, zi):
+    scale = lax.rsqrt(jnp.maximum(colsum(zr * zr + zi * zi), 1.0))
+    return own, (zr * scale, zi * scale)
+
+
+def take_virtual(idx_ref, base, reach, tiles, halves, count):
+    virtual = []
+    for h in range(halves):
+        parts = []
+        for kt in range(KP // SUB):
+            rows = min(SUB, count - kt * SUB)
+            raw = idx_ref[pl.ds(kt * SUB, rows), half(h)] - base
+            if rows < SUB:
+                raw = jnp.concatenate([raw, jnp.full((SUB - rows, LANES), -1, jnp.int32)], axis=0)
+            lane = jnp.bitwise_and(raw, LANES - 1)
+            tile = jnp.right_shift(raw, 7)
+            both = []
+            for c in range(2):
+                out = jnp.zeros((SUB, LANES), jnp.float32)
+                for n in range(h, h + 2 * reach // LANES + 1):
+                    got = lane_take(jnp.broadcast_to(tiles[n][c], (SUB, LANES)), lane)
+                    out = jnp.where(tile == n, got, out)
+                both.append(out)
+            parts.append(both)
+        zr = jnp.concatenate([p[0] for p in parts], axis=0)
+        zi = jnp.concatenate([p[1] for p in parts], axis=0)
+        virtual.append(scaled(tiles[reach // LANES + h], zr, zi))
+    return virtual
+
+
+def update(virtual, gr_ref, gi_ref, fr_ref, fi_ref):
+    for h, (_, (zr, zi)) in enumerate(virtual):
+        for l in range(fr_ref.shape[0]):
+            br = jnp.broadcast_to(zr[l : l + 1], (KP, LANES))
+            bi = jnp.broadcast_to(zi[l : l + 1], (KP, LANES))
+            fr_ref[l, h] = gr_ref[l, h] + (zr * br + zi * bi)
+            fi_ref[l, h] = gi_ref[l, h] + (zr * bi - zi * br)
 
 
 def round_kernel(
@@ -293,7 +384,7 @@
 ):
     last = len(refs) > 5
     if last:
-        late, (comp_ref, *made), refs = refs[:3], refs[3:6], refs[6:]
+        late, (comp_ref, *made), refs = refs[:4], refs[4:7], refs[7:]
         fr_ref, fi_ref, beta_ref, state_ref = refs
     else:
         beta_ref, state_ref, comp_ref, fr_ref, fi_ref = refs
@@ -310,38 +401,12 @@
         for ref in (low_ref, own_ref, high_ref):
             for t in range(ref.shape[1] // LANES):
                 tiles.append([ref[c : c + 1, half(t)] for c in range(2)])
-        virtual = []
-        for h in range(halves):
-            parts = []
-            for kt in range(KP // SUB):
-                rows = min(SUB, count - kt * SUB)
-                raw = idx_ref[pl.ds(kt * SUB, rows), half(h)] - (start - reach)
-                if rows < SUB:
-                    raw = jnp.concatenate([raw, jnp.full((SUB - rows, LANES), -1, jnp.int32)], axis=0)
-                lane = jnp.bitwise_and(raw, LANES - 1)
-                tile = jnp.right_shift(raw, 7)
-                both = []
-                for c in range(2):
-                    out = jnp.zeros((SUB, LANES), jnp.float32)
-                    for n in range(h, h + 2 * reach // LANES + 1):
-                        got = lane_take(jnp.broadcast_to(tiles[n][c], (SUB, LANES)), lane)
-                        out = jnp.where(tile == n, got, out)
-                    both.append(out)
-                parts.append(both)
-            zr = jnp.concatenate([p[0] for p in parts], axis=0)
-            zi = jnp.concatenate([p[1] for p in parts], axis=0)
-            scale = lax.rsqrt(jnp.maximum(colsum(zr * zr + zi * zi), 1.0))
-            zr, zi = zr * scale, zi * scale
-            own = tiles[reach // LANES + h]
-            virtual.append((own, (zr, zi)))
-            for l in range(count):
-                br = jnp.broadcast_to(zr[l : l + 1], (KP, LANES))
-                bi = jnp.broadcast_to(zi[l : l + 1], (KP, LANES))
-                fr_ref[l, h] = gr_ref[l, h] + (zr * br + zi * bi)
-                fi_ref[l, h] = gi_ref[l, h] + (zr * bi - zi * br)
+        virtual = take_virtual(idx_ref, start - reach, reach, tiles, halves, count)
+        update(virtual, gr_ref, gi_ref, fr_ref, fi_ref)
         hr = [gr_ref[count, h] for h in range(halves)]
         hi = [gi_ref[count, h] for h in range(halves)]
-        solve(virtual, fr_ref, fi_ref, hr, hi, sum_ref, stack, beta_ref, state_ref)
+        sums = [(sum_ref[0, h], sum_ref[1, h]) for h in range(halves)]
+        solve(virtual, fr_ref, fi_ref, hr, hi, sums, stack, beta_ref, state_ref)
 
     comp_ref[...] = state_ref[0:2]
     if last:
@@ -349,19 +414,14 @@
 
 
 def slot_rows(halves):
-    return 2 * halves + 1
-
-
-def vectors(pixel_ref, zr_ref, zi_ref, beta_ref, state_ref, vec_ref, slot_ref):
+    return 4 * halves + 1
+
+
+def make_vectors(zr_ref, zi_ref, beta_ref, state_ref, vec_ref):
     count, rows, pixels = zr_ref.shape
     dates = vec_ref.shape[1]
-    halves = pixels // LANES
-    _, _, _, start, _, _ = seat(pixels, 0)
-    local = pixel_ref[...] - start
-    lane = lax.broadcasted_iota(jnp.int32, (SUB, LANES), 1)
-    row = lax.broadcasted_iota(jnp.int32, (SUB, LANES), 0)
-    at_pixel = [jnp.zeros((SUB, LANES), jnp.float32) for _ in range(2)]
-    for h in range(halves):
+    out = [[], []]
+    for h in range(pixels // LANES):
         a = state_ref[4:5, half(h)]
         acc_r = [jnp.broadcast_to(a, (SUB, LANES)) for _ in range(0, rows, SUB)]
         acc_i = [jnp.zeros((SUB, LANES), jnp.float32) for _ in range(0, rows, SUB)]
@@ -376,67 +436,180 @@
         for c, acc in ((0, acc_r), (1, acc_i)):
             whole = jnp.concatenate(acc, axis=0)
             vec_ref[c, :, half(h)] = whole[0:dates]
-            wide = jnp.concatenate([whole, jnp.zeros((up(rows, LANES) - rows, LANES), jnp.float32)], axis=0)
-            turned = jnp.transpose(wide)
-            for r in range(0, LANES, SUB):
-                at_pixel[c] = at_pixel[c] + jnp.where(row == local - (h * LANES + r), turned[r : r + SUB], 0.0)
-    slot = [state_ref[2 + c : 3 + c, half(h)] for c in range(2) for h in range(halves)]
-    mixed = colsum(at_pixel[0]) + pltpu.roll(jnp.broadcast_to(colsum(at_pixel[1]), (SUB, LANES)), LANES // 2, 1)[0:1]
+            out[c].append(whole)
+    return out
+
+
+def vectors(pixel_ref, zr_ref, zi_ref, tile_ref, beta_ref, state_ref, vec_ref, slot_ref):
+    _, rows, pixels = zr_ref.shape
+    halves = pixels // LANES
+    section, block, blocks, start, _, _ = seat(pixels, 0)
+
+    @pl.when(section < lax.axis_size("section") - 1)
+    def _():
+        local = pixel_ref[...] - start
+        lane = lax.broadcasted_iota(jnp.int32, (SUB, LANES), 1)
+        row = lax.broadcasted_iota(jnp.int32, (SUB, LANES), 0)
+        at_pixel = [jnp.zeros((SUB, LANES), jnp.float32) for _ in range(2)]
+        vecs = make_vectors(zr_ref, zi_ref, beta_ref, state_ref, vec_ref)
+        for c in range(2):
+            for h in range(halves):
+                empty = jnp.zeros((LANES - rows, LANES), jnp.float32)
+                turned = jnp.transpose(jnp.concatenate([vecs[c][h], empty], axis=0))
+                for r in range(0, LANES, SUB):
+                    at_pixel[c] = at_pixel[c] + jnp.where(row == local - (h * LANES + r), turned[r : r + SUB], 0.0)
+        slot = [state_ref[c : c + 1, half(h)] for c in range(4) for h in range(halves)]
+        mixed = colsum(at_pixel[0]) + pltpu.roll(jnp.broadcast_to(colsum(at_pixel[1]), (SUB, LANES)), LANES // 2, 1)[0:1]
+        for c in range(2):
+            picked = jnp.zeros((1, LANES), jnp.float32)
+            for h in range(halves):
+                picked = picked + jnp.where((lane == local - h * LANES)[0:1], state_ref[2 + c : 3 + c, half(h)], 0.0)
+            f = jnp.sum(picked, axis=1, keepdims=True)
+            mixed = jnp.where(lane[0:1] == LANES - 2 + c, jnp.broadcast_to(f, (1, LANES)), mixed)
+        slot.append(mixed)
+        for n in range(slot_ref.shape[0]):
+            for m, one in enumerate(slot):
+                slot_ref[n, m] = one
+
+    @pl.when(section == lax.axis_size("section") - 1)
+    def _():
+        piece = up(KP, blocks) // blocks
+        for i in range(piece):
+            at = jnp.minimum(block * piece + i, KP - 1)
+            one = tile_ref[pl.ds(at, 1), :]
+            for n in range(slot_ref.shape[0]):
+                slot_ref[n, i] = one
+
+
+def unfold(fold_ref, fr_ref, fi_ref):
+    count = fr_ref.shape[0]
+    k_row = lax.broadcasted_iota(jnp.int32, (KP, LANES), 0)
+    for h in range(fold_ref.shape[1]):
+        for l in range(count):
+            straight = fold_ref[l, h]
+            turned = jnp.concatenate(
+                [fold_ref[k, h, pl.ds(l, 1), :] for k in range(count)] + [jnp.zeros((KP - count, LANES), jnp.float32)], axis=0
+            )
+            fr_ref[l, h] = jnp.where(k_row <= l, straight, turned)
+            fi_ref[l, h] = jnp.where(k_row > l, straight, jnp.where(k_row < l, -turned, 0.0))
+
+
+def finish_kernel(
+    sections, stack, pixel_ref, idx_ref, got_ref, vec0_ref, comp0_ref, zr_ref, zi_ref, gr_ref, gi_ref, sum_ref, *refs
+):
+    folds, (out_ref, small_ref), refs = refs[:sections], refs[sections : sections + 2], refs[sections + 2 :]
+    fr_ref, fi_ref, add_ref, beta_ref, state_ref, vec_ref = refs
+    dates, pixels = vec_ref.shape[1:]
+    count = zr_ref.shape[0]
+    section, mine, blocks, start, _, _ = seat(pixels, 0)
+    halves = pixels // LANES
+    final = sections - 1
+    reach = min(pixels, REACH_LIMIT)
+
+    for s in range(sections):
+
+        @pl.when(section == s)
+        def _(s=s):
+            unfold(folds[s], fr_ref, fi_ref)
+            for c in range(2):
+                for h in range(halves):
+                    add_ref[c, h] = folds[s][count + c, h]
+
+    piece = up(KP, blocks) // blocks
+    tile = [got_ref[final * blocks + n // piece, n % piece] for n in range(KP)]
+    tile = jnp.concatenate(tile, axis=0)
+    k_row = lax.broadcasted_iota(jnp.int32, (KP, LANES), 0)
+    lane = lax.broadcasted_iota(jnp.int32, (KP, LANES), 1)
+    turned = jnp.transpose(jnp.concatenate([tile, jnp.zeros((LANES - KP, LANES), jnp.float32)], axis=0))[0:KP]
+    real = jnp.where(k_row <= lane, tile, turned)
+    imag = jnp.where(k_row > lane, tile, jnp.where(k_row < lane, -turned, 0.0))
+
+    def spread(x, l):
+        return jnp.broadcast_to(x[:, l : l + 1], (KP, LANES))
+
+    for l in range(count):
+        fr_ref[l, halves] = spread(real, l)
+        fi_ref[l, halves] = spread(imag, l)
+    sums = [(add_ref[0, h], add_ref[1, h]) for h in range(halves)] + [(spread(tile, KP), spread(tile, KP + 1))]
+
+    before = final - 1
+    tiles = []
+    per = reach // LANES
+    low, high = jnp.maximum(mine - 1, 0), jnp.minimum(mine + 1, blocks - 1)
+    for at, which in ((low, range(halves - per, halves)), (mine, range(halves)), (high, range(per))):
+        for h in which:
+            tiles.append([got_ref[before * blocks + at, c * halves + h] for c in range(2)])
+    virtual = take_virtual(idx_ref, start - reach, reach, tiles, halves, count)
+    near = spread(tile, KP + 2).astype(jnp.int32)
+    total = [jnp.zeros((KP, LANES), jnp.float32) for _ in range(2)]
+    for q in range(blocks):
+        for h in range(halves):
+            hit = lane == near - (q * pixels + h * LANES)
+            for c in range(2):
+                total[c] = total[c] + jnp.where(hit, got_ref[before * blocks + q, c * halves + h], 0.0)
+    total = [jnp.broadcast_to(jnp.sum(x, axis=1, keepdims=True), (KP, LANES)) for x in total]
+    total = [jnp.where(k_row < count, x, 0.0) for x in total]
+    virtual.append(scaled([x[0:1] for x in total], *total))
+    update(virtual, fr_ref, fi_ref, fr_ref, fi_ref)
+
+    zero = jnp.zeros((KP, LANES), jnp.float32)
+    hr = [gr_ref[count, h] for h in range(halves)] + [zero]
+    hi = [gi_ref[count, h] for h in range(halves)] + [zero]
+    solve(virtual, fr_ref, fi_ref, hr, hi, sums, stack, beta_ref, state_ref)
+    is_final = section == final
     for c in range(2):
-        picked = jnp.zeros((1, LANES), jnp.float32)
-        for h in range(halves):
-            picked = picked + jnp.where((lane == local - h * LANES)[0:1], state_ref[2 + c : 3 + c, half(h)], 0.0)
-        f = jnp.sum(picked, axis=1, keepdims=True)
-        mixed = jnp.where(lane[0:1] == LANES - 2 + c, jnp.broadcast_to(f, (1, LANES)), mixed)
-    slot.append(mixed)
-    for n in range(slot_ref.shape[0]):
-        for m, one in enumerate(slot):
-            slot_ref[n, m] = one
-
-
-def finish_kernel(sections, pixel_ref, vec_ref, got_ref, comp_ref, out_ref, small_ref):
-    small_ref[:, 0] = comp_ref[...]
-    dates, pixels = vec_ref.shape[1:]
-    section, mine, blocks, _, _, _ = seat(pixels, 0)
-    halves = pixels // LANES
-    one = jnp.ones((1, LANES), jnp.float32)
-    lane = lax.broadcasted_iota(jnp.int32, (1, LANES), 1)
+        small_ref[c] = jnp.where(is_final, state_ref[c : c + 1, 0:pixels], comp0_ref[c : c + 1])
 
     def of_pixel(s):
         total = jnp.zeros((1, LANES), jnp.float32)
         for q in range(blocks):
             first = pixel_ref[0:1] - q * pixels
             here = jnp.logical_and(first >= 0, first < pixels)
-            total = total + jnp.where(here, got_ref[s * blocks + q, 2 * halves], 0.0)
+            total = total + jnp.where(here, got_ref[s * blocks + q, 4 * halves], 0.0)
         return total
 
-    datum = [(one, 0.0 * one) for _ in range(halves)]
-    at_pixel = (one, 0.0 * one)
-    for s in range(sections - 1, 0, -1):
+    def times(d, later, fr, fi):
+        fr = jnp.where(later, fr, 1.0)
+        fi = jnp.where(later, fi, 0.0)
+        return (d[0] * fr - d[1] * fi, d[0] * fi + d[1] * fr)
+
+    one = jnp.ones((1, LANES), jnp.float32)
+    datum = [(one, 0.0 * one) for _ in range(halves + 1)]
+    for h in range(halves + 1):
+        datum[h] = times(datum[h], section < final, state_ref[2:3, half(h)], state_ref[3:4, half(h)])
+    for s in range(final - 1, 0, -1):
         later = section < s
-        own = [got_ref[s * blocks + mine, m] for m in range(2 * halves)]
+        own = [got_ref[s * blocks + mine, 2 * halves + m] for m in range(2 * halves)]
         row = of_pixel(s)
-
-        def times(d, fr, fi):
-            fr = jnp.where(later, fr, 1.0)
-            fi = jnp.where(later, fi, 0.0)
-            return (d[0] * fr - d[1] * fi, d[0] * fi + d[1] * fr)
-
         for h in range(halves):
-            datum[h] = times(datum[h], own[h], own[halves + h])
-        f = [jnp.sum(jnp.where(lane == LANES - 2 + c, row, 0.0), axis=1, keepdims=True) for c in range(2)]
-        at_pixel = times(at_pixel, *[jnp.broadcast_to(x, (1, LANES)) for x in f])
-    vr = of_pixel(section)
-    vi = pltpu.roll(jnp.broadcast_to(vr, (SUB, LANES)), LANES // 2, 1)[0:1]
-    ur, ui = unit(vr * at_pixel[0] - vi * at_pixel[1], vr * at_pixel[1] + vi * at_pixel[0])
+            datum[h] = times(datum[h], later, own[h], own[halves + h])
+        f = [jnp.sum(jnp.where(lane[0:1] == LANES - 2 + c, row, 0.0), axis=1, keepdims=True) for c in range(2)]
+        datum[halves] = times(datum[halves], later, *[jnp.broadcast_to(x, (1, LANES)) for x in f])
+
+    zr = pltpu.roll(tile, LANES - Z_LANE, 1)
+    zi = pltpu.roll(tile, LANES - Z_LANE - Z_STEP, 1)
+    br, bi = beta_ref[0, halves], beta_ref[1, halves]
+    zr, zi = jnp.where(k_row < count, zr, 0.0), jnp.where(k_row < count, zi, 0.0)
+    last_r = state_ref[4:5, half(halves)] + colsum(zr * br - zi * bi)
+    last_i = colsum(zr * bi + zi * br)
+    row = of_pixel(jnp.minimum(section, final - 1))
+    vr = jnp.where(is_final, last_r, row)
+    vi = jnp.where(is_final, last_i, pltpu.roll(jnp.broadcast_to(row, (SUB, LANES)), LANES // 2, 1)[0:1])
+    dr, di = datum[halves]
+    ur, ui = unit(vr * dr - vi * di, vr * di + vi * dr)
     gain = math.sqrt(dates + 1)
     ur = jnp.transpose(jnp.broadcast_to(ur * gain, (LANES, LANES)))[0:dates]
     ui = jnp.transpose(jnp.broadcast_to(ui * gain, (LANES, LANES)))[0:dates]
+
+    @pl.when(is_final)
+    def _():
+        make_vectors(zr_ref, zi_ref, beta_ref, state_ref, vec_ref)
+
     for h in range(halves):
         wr = ur * datum[h][0] + ui * datum[h][1]
         wi = ur * datum[h][1] - ui * datum[h][0]
-        vr = vec_ref[0, :, half(h)]
-        vi = vec_ref[1, :, half(h)]
+        vr = jnp.where(is_final, vec_ref[0, :, half(h)], vec0_ref[0, :, half(h)])
+        vi = jnp.where(is_final, vec_ref[1, :, half(h)], vec0_ref[1, :, half(h)])
         out_ref[:, 0, half(h)] = vr * wr - vi * wi
         out_ref[:, 1, half(h)] = vr * wi + vi * wr
 
@@ -486,26 +659,37 @@
         name="own",
     )(pltpu.with_memory_space_constraint(neighbours, pltpu.HBM), pltpu.with_memory_space_constraint(slc, pltpu.HBM), near)
 
+    pixel = jnp.full((SUB, LANES), reference_pixel[0], jnp.int32)
+
     def prepare(first, carried):
+        more = [] if first else [pixel]
+        outs = made if first else made[:7] + [f32(count + 2, halves, KP, LANES), f32(KP, LANES)]
         return pl.pallas_call(
             functools.partial(prepare_kernel, stack, first),
-            out_shape=made[: 8 if first else 7],
-            in_specs=[VMEM] * (3 + len(carried)),
-            out_specs=[VMEM] * (8 if first else 7),
+            out_shape=outs,
+            in_specs=[VMEM] * (3 + len(more) + len(carried)),
+            out_specs=[VMEM] * len(outs),
             scratch_shapes=[
                 pltpu.VMEM((2 * rows, reach), jnp.float32),
                 pltpu.VMEM((4 * rows, reach), jnp.bfloat16),
                 pltpu.VMEM((2, count + 1, count, SUB, LANES), jnp.float32),
             ],
-            input_output_aliases={3 + n: n for n in range(len(carried))},
+            input_output_aliases={3 + len(more) + n: n for n in range(len(carried))},
             compiler_params=params(),
             cost_estimate=cost(50 * 12 * rows * reach * pixels * count),
-        )(neighbours, far, own, *carried)
+        )(neighbours, far, own, *more, *carried)
 
     *made_0, comp = prepare(True, (zr, zi))
-    zr, zi, gr, gi, sums, beta, state = prepare(False, made_0)
-
-    for rnd in range(1, sections):
+    zr, zi, gr, gi, sums, beta, state, folded, tile = prepare(False, made_0)
+
+    final = sections - 1
+    step = 1
+    while step < blocks:
+        pairs = [(final * blocks + q, final * blocks + (q + step) % blocks) for q in range(blocks)]
+        tile = tile + lax.ppermute(tile, ("section", "pix"), pairs)
+        step *= 2
+
+    for rnd in range(1, final):
         def hop(shift):
             pairs = [
                 ((rnd - 1) * blocks + q, rnd * blocks + q + shift)
@@ -514,39 +698,53 @@
             ]
             return lax.ppermute(comp, ("section", "pix"), pairs)
 
-        last = rnd == sections - 1
-        late, specs = (), []
+        last = rnd == final - 1
+        late = (pixel, zr, zi, tile) if last else ()
         scratch = [pltpu.VMEM((count, halves, KP, LANES), jnp.float32)] * 2
         outs = [f32(2, halves, KP, LANES), f32(SUB, pixels), f32(2, pixels)]
         if last:
-            late, specs = (ref_at, zr, zi), [VMEM] * 3
             scratch += [pltpu.VMEM(o.shape, o.dtype) for o in outs[:2]]
             outs = outs[2:] + [f32(2, dates, pixels), f32(sections * blocks, slot_rows(halves), 1, LANES)]
-        made = pl.pallas_call(
+        call = pl.pallas_call(
             functools.partial(round_kernel, rnd, stack),
             out_shape=outs,
-            in_specs=[VMEM] * 9 + specs,
+            in_specs=[VMEM] * (9 + len(late)),
             out_specs=[VMEM] * 3,
             scratch_shapes=scratch,
             compiler_params=params(),
-        )(neighbours, hop(1)[:, pixels - reach :], hop(0), hop(-1)[:, :reach], gr, gi, sums, beta, state, *late)
+        )
+        near = (hop(1)[:, pixels - reach :], hop(0), hop(-1)[:, :reach])
+        made = call(neighbours, *near, gr, gi, sums, beta, state, *late)
         if last:
             comp, vec, sent = made
         else:
             beta, state, comp = made
         if rnd == 1:
-            pixel = lax.optimization_barrier((reference_pixel, comp))[0][0]
-            ref_at = jnp.full((SUB, LANES), pixel, jnp.int32)
-
+            later = lax.optimization_barrier((folded, comp))[0]
+            folds = []
+            for s in range(final):
+                pairs = [(final * blocks + q, s * blocks + q) for q in range(blocks)]
+                folds.append(lax.ppermute(later, ("section", "pix"), pairs))
+            folds.append(folded)
+
+    sent, *folds = lax.optimization_barrier((sent, *folds))
     got = lax.all_to_all(sent, ("section", "pix"), 0, 0, tiled=True)
     out, small = pl.pallas_call(
-        functools.partial(finish_kernel, sections),
+        functools.partial(finish_kernel, sections, stack),
         out_shape=[f32(dates, 2, pixels), f32(2, 1, pixels)],
-        in_specs=[VMEM] * 4,
+        in_specs=[VMEM] * (10 + sections),
         out_specs=[VMEM] * 2,
+        scratch_shapes=[
+            pltpu.VMEM((count, halves + 1, KP, LANES), jnp.float32),
+            pltpu.VMEM((count, halves + 1, KP, LANES), jnp.float32),
+            pltpu.VMEM((2, halves, KP, LANES), jnp.float32),
+            pltpu.VMEM((2, halves + 1, KP, LANES), jnp.float32),
+            pltpu.VMEM((SUB, pixels + LANES), jnp.float32),
+            pltpu.VMEM((2, dates, pixels), jnp.float32),
+        ],
         compiler_params=params(),
         name="finish",
-    )(ref_at, vec, got, comp)
+    )(pixel, neighbours, got, vec, comp, zr, zi, gr, gi, sums, *folds)
     return (jnp.transpose(out, (1, 0, 2)), small)
 
 

time: 50.6 us -> 60.4 us (1.19)
  waiting for transfers between devices: 1.1 us -> 9.71 us
  blocking collectives: 29.7 us -> 25.1 us
  starting transfers between devices: 9.75 us -> 12.8 us
  Pallas kernels: 8.3 us -> 10.8 us
    ppermute x0 -> x6, waiting for transfers between devices: none -> 8.47 us  [the longest x3 8.46 us: on_device(): folds.append(lax.ppermute(later, ('section', 'pix'), pairs))]
    ppermute x0 -> x6, starting transfers between devices: none -> 4.62 us  [the longest x3 2.64 us: on_device(): folds.append(lax.ppermute(later, ('section', 'pix'), pairs))]
    all_to_all x1, blocking collectives: 29.7 us -> 25.1 us  [on_device(): got = lax.all_to_all(sent, ('section', 'pix'), 0, 0, tiled=True)]
    pallas_call x4 -> x3, Pallas kernels: 1.43 us -> 3.9 us  [the longest x1 3.4 us: on_device(): pl.pallas_call(functools.partial(finish_kernel, sections, stack), out_sha...]
    ppermute x9 -> x6, starting transfers between devices: 8.53 us -> 7.01 us  [hop(): return lax.ppermute(comp, ('section', 'pix'), pairs)]
    ppermute x9 -> x6, waiting for transfers between devices: 0.6 us -> 1.24 us  [hop(): return lax.ppermute(comp, ('section', 'pix'), pairs)]
  transfers between devices with their start and end apart: 11 -> 14, of which waited for: 2 -> 2; matrix products, arithmetic and copies ran while one was open for 0% -> 0% of each run, Pallas kernels for 4% -> 4%
where the time goes in v7:
time: 60.4 us; the launch traced here: 60 us
  blocking collectives  25.1 us (42%)
  starting transfers between devices  12.8 us (21%)
  Pallas kernels  10.8 us (18%)
  waiting for transfers between devices  9.71 us (16%)
  between operations  1.53 us (3%)
    all_to_all x1, blocking collectives, on_device(): got = lax.all_to_all(sent, ('section', 'pix'), 0, 0, tiled=True)  25.1 us
    ppermute x3, waiting for transfers between devices, on_device(): folds.append(lax.ppermute(later, ('section', 'pix'), pairs))  8.46 us
    ppermute x6, starting transfers between devices, hop(): return lax.ppermute(comp, ('section', 'pix'), pairs)  7.01 us
    pallas_call x2, Pallas kernels, prepare(): pl.pallas_call(functools.partial(prepare_kernel, stack, first), out_shape...  4.85 us
    pallas_call x1, Pallas kernels, on_device(): pl.pallas_call(functools.partial(finish_kernel, sections, stack), out_sha...  3.4 us
    ppermute x3, starting transfers between devices, on_device(): folds.append(lax.ppermute(later, ('section', 'pix'), pairs))  2.64 us
    pallas_call x1, Pallas kernels, on_device(): pl.pallas_call(own_kernel, out_shape=made[:2] + [f32(2 * rows, pixels + r...  2.05 us
    ppermute x3, starting transfers between devices, on_device(): tile = tile + lax.ppermute(tile, ('section', 'pix'), pairs)  1.98 us
  transfers between devices with their start and end apart: 14, of which 2 were waited for; matrix products, arithmetic and copies ran while one was open for 0% of the time, Pallas kernels for 4%

profile of v7, /device:TPU:0, one launch (start us, length us, event | category | flops | bytes accessed | tf_op | source)
XLA Modules:
  0.0 60.0 jit_solution(10276733675966084223)
XLA Ops:
  0.6 0.6 collective-permute-start
  1.2 0.7 %collective-permute-start.1 = (f32[50,2,256]{2,1,0:T(2,128)}, f32[50,2,256]{2,1,0:T(2,128)S(1)}, u32[]{:S(2)}, u32[]{:S(2)}) collective-permute-start(f32[50,2,256]{2,1,0:T(2,128)} %bitcast.5), channel_id=1, source_target_pairs={{1,2},{3,4},{5,6},{2,1},{4,3},{6,5},{9,10},{11,12},{13,14},{10,9},... | collective-permute-start | bytes 307208 | tf_op jit(solution)/shard_map/ppermute | solution.py:637
  2.5 0.0 collective-permute-done.near_ref
  2.5 2.0 %own.1 = (f32[15,56,256]{2,1,0:T(8,128)S(1)}, f32[15,56,256]{2,1,0:T(8,128)S(1)}, f32[112,512]{1,0:T(8,128)S(1)}, s32[15,256]{1,0:T(8,128)S(1)}) custom-call(s32[15,256]{1,0:T(8,128)} %idx_hbm.1, f32[50,2,256]{2,1,0:T(2,128)} %bitcast.6, f32[50,2,256]{2,1,0:T(2,128)S(1)} %collective-permute-done.near_ref), custom_call_target="tpu_custom_call" | custom-call | flops 880803840 | tf_op jit(solution)/shard_map/own/pallas_call | solution.py:647
  4.6 0.0 collective-permute-done.1.far_ref
  4.6 4.8 %shard_map.50 = (f32[15,56,256]{2,1,0:T(8,128)S(1)}, f32[15,56,256]{2,1,0:T(8,128)S(1)}, f32[16,2,16,128]{3,2,1,0:T(8,128)S(1)}, f32[16,2,16,128]{3,2,1,0:T(8,12...) custom-call(s32[15,256]{1,0:T(8,128)S(1)} %get-tuple-element.37.idx_, ...), custom_call_target="tpu_custom_call", output_to_operand_aliasing={{0}: (3, {}), {1}: (4, {})} | custom-call | flops 33030144000 | tf_op jit(solution)/shard_map/pallas_call | solution.py:667
  9.4 0.7 %collective-permute-start.4 = (f32[2,256]{1,0:T(2,128)S(1)}, f32[2,256]{1,0:T(2,128)S(1)}, u32[]{:S(2)}, u32[]{:S(2)}) collective-permute-start(f32[2,256]{1,0:T(2,128)S(1)} %get-tuple-element.41), channel_id=1, source_target_pairs={{1,8},{2,9},{3,10},{4,11},{5,12},{6,13},{7,14}} | collective-permute-start | bytes 6152 | tf_op jit(solution)/shard_map/ppermute | solution.py:699
  10.1 1.3 %collective-permute-start.3 = (f32[2,256]{1,0:T(2,128)S(1)}, f32[2,256]{1,0:T(2,128)S(1)}, u32[]{:S(2)}, u32[]{:S(2)}) collective-permute-start(f32[2,256]{1,0:T(2,128)S(1)} %get-tuple-element.41), channel_id=1, source_target_pairs={{0,8},{1,9},{2,10},{3,11},{4,12},{5,13},{6,14},{7,15}} | collective-permute-start | bytes 6152 | tf_op jit(solution)/shard_map/ppermute | solution.py:699
  11.4 3.1 %collective-permute-start.2 = (f32[2,256]{1,0:T(2,128)S(1)}, f32[2,256]{1,0:T(2,128)S(1)}, u32[]{:S(2)}, u32[]{:S(2)}) collective-permute-start(f32[2,256]{1,0:T(2,128)S(1)} %get-tuple-element.41), channel_id=1, source_target_pairs={{0,9},{1,10},{2,11},{3,12},{4,13},{5,14},{6,15}} | collective-permute-start | bytes 6152 | tf_op jit(solution)/shard_map/ppermute | solution.py:699
  14.5 0.0 collective-permute-done.4.high_ref
  14.5 0.0 collective-permute-done.3.own_ref
  14.5 1.2 %collective-permute-done.2.low_ref = f32[2,256]{1,0:T(2,128)S(1)} collective-permute-done((f32[2,256]{1,0:T(2,128)S(1)}, f32[2,256]{1,0:T(2,128)S(1)}, u32[]{:S(2)}, u32[]{:S(2)}) %collective-permute-start.2) | collective-permute-done | bytes 2080 | tf_op jit(solution)/shard_map/ppermute | solution.py:699
  15.8 0.7 %collective-permute-start.13 = (f32[17,2,16,128]{3,2,1,0:T(8,128)S(1)}, f32[17,2,16,128]{3,2,1,0:T(8,128)S(1)}, u32[]{:S(2)}, u32[]{:S(2)}) collective-permute-start(f32[17,2,16,128]{3,2,1,0:T(8,128)S(1)} %get-tuple-element.69.refs_3_), channel_id=1, source_target_pairs={{24,16},{25,17},{26,18},{27,19},{28,20},{29,21},{30,22},{31,23}} | collective-permute-start | bytes 835592 | tf_op jit(solution)/shard_map/ppermute | solution.py:727
  16.4 0.7 %collective-permute-start.12 = (f32[17,2,16,128]{3,2,1,0:T(8,128)S(1)}, f32[17,2,16,128]{3,2,1,0:T(8,128)S(1)}, u32[]{:S(2)}, u32[]{:S(2)}) collective-permute-start(f32[17,2,16,128]{3,2,1,0:T(8,128)S(1)} %get-tuple-element.69.refs_3_), channel_id=1, source_target_pairs={{24,8},{25,9},{26,10},{27,11},{28,12},{29,13},{30,14},{31,15}} | collective-permute-start | bytes 835592 | tf_op jit(solution)/shard_map/ppermute | solution.py:727
  17.1 1.3 %collective-permute-start.11 = (f32[17,2,16,128]{3,2,1,0:T(8,128)S(1)}, f32[17,2,16,128]{3,2,1,0:T(8,128)S(1)}, u32[]{:S(2)}, u32[]{:S(2)}) collective-permute-start(f32[17,2,16,128]{3,2,1,0:T(8,128)S(1)} %get-tuple-element.69.refs_3_), channel_id=1, source_target_pairs={{24,0},{25,1},{26,2},{27,3},{28,4},{29,5},{30,6},{31,7}} | collective-permute-start | bytes 835592 | tf_op jit(solution)/shard_map/ppermute | solution.py:727
  18.4 0.7 %collective-permute-start.8 = (f32[16,128]{1,0:T(8,128)S(1)}, f32[16,128]{1,0:T(8,128)S(1)}, u32[]{:S(2)}, u32[]{:S(2)}) collective-permute-start(f32[16,128]{1,0:T(8,128)S(1)} %get-tuple-element.59), channel_id=1, source_target_pairs={{24,25},{25,26},{26,27},{27,28},{28,29},{29,30},{30,31},{31,24}} | collective-permute-start | bytes 24584 | tf_op jit(solution)/shard_map/ppermute | solution.py:689
  19.1 0.0 collective-permute-done.8
  19.1 0.7 %collective-permute-start.9 = (f32[16,128]{1,0:T(8,128)S(1)}, f32[16,128]{1,0:T(8,128)S(1)}, u32[]{:S(2)}, u32[]{:S(2)}) collective-permute-start(f32[16,128]{1,0:T(8,128)S(1)} %add.9), channel_id=1, source_target_pairs={{24,26},{25,27},{26,28},{27,29},{28,30},{29,31},{30,24},{31,25}} | collective-permute-start | bytes 24584 | tf_op jit(solution)/shard_map/ppermute | solution.py:689
  19.8 0.0 collective-permute-done.9
  19.8 0.7 %collective-permute-start.10 = (f32[16,128]{1,0:T(8,128)S(1)}, f32[16,128]{1,0:T(8,128)S(1)}, u32[]{:S(2)}, u32[]{:S(2)}) collective-permute-start(f32[16,128]{1,0:T(8,128)S(1)} %add.10), channel_id=1, source_target_pairs={{24,28},{25,29},{26,30},{27,31},{28,24},{29,25},{30,26},{31,27}} | collective-permute-start | bytes 24584 | tf_op jit(solution)/shard_map/ppermute | solution.py:689
  20.5 0.7 %collective-permute-start.7 = (f32[2,256]{1,0:T(2,128)S(1)}, f32[2,256]{1,0:T(2,128)S(1)}, u32[]{:S(2)}, u32[]{:S(2)}) collective-permute-start(f32[2,256]{1,0:T(2,128)S(1)} %get-tuple-element.54), channel_id=1, source_target_pairs={{9,16},{10,17},{11,18},{12,19},{13,20},{14,21},{15,22}} | collective-permute-start | bytes 6152 | tf_op jit(solution)/shard_map/ppermute | solution.py:699
  21.1 0.0 collective-permute-done.7.high_ref
  21.2 0.7 %collective-permute-start.6 = (f32[2,256]{1,0:T(2,128)S(1)}, f32[2,256]{1,0:T(2,128)S(1)}, u32[]{:S(2)}, u32[]{:S(2)}) collective-permute-start(f32[2,256]{1,0:T(2,128)S(1)} %get-tuple-element.54), channel_id=1, source_target_pairs={{8,16},{9,17},{10,18},{11,19},{12,20},{13,21},{14,22},{15,23}} | collective-permute-start | bytes 6152 | tf_op jit(solution)/shard_map/ppermute | solution.py:699
  21.8 0.0 collective-permute-done.10
  21.8 0.7 %collective-permute-start.5 = (f32[2,256]{1,0:T(2,128)S(1)}, f32[2,256]{1,0:T(2,128)S(1)}, u32[]{:S(2)}, u32[]{:S(2)}) collective-permute-start(f32[2,256]{1,0:T(2,128)S(1)} %get-tuple-element.54), channel_id=1, source_target_pairs={{8,17},{9,18},{10,19},{11,20},{12,21},{13,22},{14,23}} | collective-permute-start | bytes 6152 | tf_op jit(solution)/shard_map/ppermute | solution.py:699
  22.5 0.0 collective-permute-done.6.own_ref
  22.5 0.0 collective-permute-done.5.low_ref
  22.5 0.5 shard_map.53
  23.0 0.0 collective-permute-done.13.refs_2_
  23.0 0.0 collective-permute-done.12.refs_1_
  23.1 8.5 %collective-permute-done.11.refs_0_ = f32[17,2,16,128]{3,2,1,0:T(8,128)S(1)} collective-permute-done((f32[17,2,16,128]{3,2,1,0:T(8,128)S(1)}, f32[17,2,16,128]{3,2,1,0:T(8,128)S(1)}, u32[]{:S(2)}, u32[]{:S(2)}) %collective-permute-start.11) | collective-permute-done | bytes 278560 | tf_op jit(solution)/shard_map/ppermute | solution.py:727
  31.5 25.1 %all_to_all.5.got_ref = f32[32,9,1,128]{3,2,1,0:T(1,128)S(1)} all-to-all(f32[32,9,1,128]{3,2,1,0:T(1,128)S(1)} %get-tuple-element.63), channel_id=1, replica_groups=mesh['section'=4,'pix'=8] {'section','pix'}, dimensions={0} | all-to-all | bytes 294912 | tf_op jit(solution)/shard_map/all_to_all | solution.py:731
  56.6 3.4 %finish.1 = (f32[50,2,256]{2,1,0:T(2,128)}, f32[2,1,256]{2,1,0:T(1,128)}) custom-call(s32[8,128]{1,0:T(8,128)S(1)} %broadcast_in_dim.3.refs_0_.pixel_ref, s32[15,256]{1,0:T(8,128)S(1)} %get-tuple-element.37.idx_ref, f32[32,9,1,128]{3,2,1,0:T(1,128)S(1)} %all_to_all.5.got_ref, f32[2,50,256]{2,1,0:T(8,128)S(1)} %get-tuple-element.64.vec0_ref, ...), custom_call_target="tpu_custom_call" | custom-call | tf_op jit(solution)/shard_map/finish/pallas_call | solution.py:732
  (6 shorter events, 0.1 us)
Async XLA Ops:
  0.6 1.9 %collective-permute-start = (f32[50,2,256]{2,1,0:T(2,128)}, f32[50,2,256]{2,1,0:T(2,128)S(1)}, u32[]{:S(2)}, u32[]{:S(2)}) collective-permute-start(f32[50,2,256]{2,1,0:T(2,128)} %bitcast.4), channel_id=1, source_target_pairs={{0,1},{2,3},{4,5},{6,7},{1,0},{3,2},{5,4},{7,6},{8,9},{10,11},{12,... | collective-permute-start | bytes 307208 | tf_op jit(solution)/shard_map/ppermute | solution.py:637
  1.2 3.4 %collective-permute-start.1 = (f32[50,2,256]{2,1,0:T(2,128)}, f32[50,2,256]{2,1,0:T(2,128)S(1)}, u32[]{:S(2)}, u32[]{:S(2)}) collective-permute-start(f32[50,2,256]{2,1,0:T(2,128)} %bitcast.5), channel_id=1, source_target_pairs={{1,2},{3,4},{5,6},{2,1},{4,3},{6,5},{9,10},{11,12},{13,14},{10,9},... | collective-permute-start | bytes 307208 | tf_op jit(solution)/shard_map/ppermute | solution.py:637
  9.4 5.1 %collective-permute-start.4 = (f32[2,256]{1,0:T(2,128)S(1)}, f32[2,256]{1,0:T(2,128)S(1)}, u32[]{:S(2)}, u32[]{:S(2)}) collective-permute-start(f32[2,256]{1,0:T(2,128)S(1)} %get-tuple-element.41), channel_id=1, source_target_pairs={{1,8},{2,9},{3,10},{4,11},{5,12},{6,13},{7,14}} | collective-permute-start | bytes 6152 | tf_op jit(solution)/shard_map/ppermute | solution.py:699
  10.1 4.4 %collective-permute-start.3 = (f32[2,256]{1,0:T(2,128)S(1)}, f32[2,256]{1,0:T(2,128)S(1)}, u32[]{:S(2)}, u32[]{:S(2)}) collective-permute-start(f32[2,256]{1,0:T(2,128)S(1)} %get-tuple-element.41), channel_id=1, source_target_pairs={{0,8},{1,9},{2,10},{3,11},{4,12},{5,13},{6,14},{7,15}} | collective-permute-start | bytes 6152 | tf_op jit(solution)/shard_map/ppermute | solution.py:699
  11.4 4.4 %collective-permute-start.2 = (f32[2,256]{1,0:T(2,128)S(1)}, f32[2,256]{1,0:T(2,128)S(1)}, u32[]{:S(2)}, u32[]{:S(2)}) collective-permute-start(f32[2,256]{1,0:T(2,128)S(1)} %get-tuple-element.41), channel_id=1, source_target_pairs={{0,9},{1,10},{2,11},{3,12},{4,13},{5,14},{6,15}} | collective-permute-start | bytes 6152 | tf_op jit(solution)/shard_map/ppermute | solution.py:699
  15.8 7.3 %collective-permute-start.13 = (f32[17,2,16,128]{3,2,1,0:T(8,128)S(1)}, f32[17,2,16,128]{3,2,1,0:T(8,128)S(1)}, u32[]{:S(2)}, u32[]{:S(2)}) collective-permute-start(f32[17,2,16,128]{3,2,1,0:T(8,128)S(1)} %get-tuple-element.69.refs_3_), channel_id=1, source_target_pairs={{24,16},{25,17},{26,18},{27,19},{28,20},{29,21},{30,22},{31,23}} | collective-permute-start | bytes 835592 | tf_op jit(solution)/shard_map/ppermute | solution.py:727
  16.4 6.6 %collective-permute-start.12 = (f32[17,2,16,128]{3,2,1,0:T(8,128)S(1)}, f32[17,2,16,128]{3,2,1,0:T(8,128)S(1)}, u32[]{:S(2)}, u32[]{:S(2)}) collective-permute-start(f32[17,2,16,128]{3,2,1,0:T(8,128)S(1)} %get-tuple-element.69.refs_3_), channel_id=1, source_target_pairs={{24,8},{25,9},{26,10},{27,11},{28,12},{29,13},{30,14},{31,15}} | collective-permute-start | bytes 835592 | tf_op jit(solution)/shard_map/ppermute | solution.py:727
  17.1 14.4 %collective-permute-start.11 = (f32[17,2,16,128]{3,2,1,0:T(8,128)S(1)}, f32[17,2,16,128]{3,2,1,0:T(8,128)S(1)}, u32[]{:S(2)}, u32[]{:S(2)}) collective-permute-start(f32[17,2,16,128]{3,2,1,0:T(8,128)S(1)} %get-tuple-element.69.refs_3_), channel_id=1, source_target_pairs={{24,0},{25,1},{26,2},{27,3},{28,4},{29,5},{30,6},{31,7}} | collective-permute-start | bytes 835592 | tf_op jit(solution)/shard_map/ppermute | solution.py:727
  18.4 0.7 %collective-permute-start.8 = (f32[16,128]{1,0:T(8,128)S(1)}, f32[16,128]{1,0:T(8,128)S(1)}, u32[]{:S(2)}, u32[]{:S(2)}) collective-permute-start(f32[16,128]{1,0:T(8,128)S(1)} %get-tuple-element.59), channel_id=1, source_target_pairs={{24,25},{25,26},{26,27},{27,28},{28,29},{29,30},{30,31},{31,24}} | collective-permute-start | bytes 24584 | tf_op jit(solution)/shard_map/ppermute | solution.py:689
  19.1 0.7 %collective-permute-start.9 = (f32[16,128]{1,0:T(8,128)S(1)}, f32[16,128]{1,0:T(8,128)S(1)}, u32[]{:S(2)}, u32[]{:S(2)}) collective-permute-start(f32[16,128]{1,0:T(8,128)S(1)} %add.9), channel_id=1, source_target_pairs={{24,26},{25,27},{26,28},{27,29},{28,30},{29,31},{30,24},{31,25}} | collective-permute-start | bytes 24584 | tf_op jit(solution)/shard_map/ppermute | solution.py:689
  19.8 2.0 %collective-permute-start.10 = (f32[16,128]{1,0:T(8,128)S(1)}, f32[16,128]{1,0:T(8,128)S(1)}, u32[]{:S(2)}, u32[]{:S(2)}) collective-permute-start(f32[16,128]{1,0:T(8,128)S(1)} %add.10), channel_id=1, source_target_pairs={{24,28},{25,29},{26,30},{27,31},{28,24},{29,25},{30,26},{31,27}} | collective-permute-start | bytes 24584 | tf_op jit(solution)/shard_map/ppermute | solution.py:689
  20.5 0.7 %collective-permute-start.7 = (f32[2,256]{1,0:T(2,128)S(1)}, f32[2,256]{1,0:T(2,128)S(1)}, u32[]{:S(2)}, u32[]{:S(2)}) collective-permute-start(f32[2,256]{1,0:T(2,128)S(1)} %get-tuple-element.54), channel_id=1, source_target_pairs={{9,16},{10,17},{11,18},{12,19},{13,20},{14,21},{15,22}} | collective-permute-start | bytes 6152 | tf_op jit(solution)/shard_map/ppermute | solution.py:699
  21.2 1.4 %collective-permute-start.6 = (f32[2,256]{1,0:T(2,128)S(1)}, f32[2,256]{1,0:T(2,128)S(1)}, u32[]{:S(2)}, u32[]{:S(2)}) collective-permute-start(f32[2,256]{1,0:T(2,128)S(1)} %get-tuple-element.54), channel_id=1, source_target_pairs={{8,16},{9,17},{10,18},{11,19},{12,20},{13,21},{14,22},{15,23}} | collective-permute-start | bytes 6152 | tf_op jit(solution)/shard_map/ppermute | solution.py:699
  21.8 0.7 %collective-permute-start.5 = (f32[2,256]{1,0:T(2,128)S(1)}, f32[2,256]{1,0:T(2,128)S(1)}, u32[]{:S(2)}, u32[]{:S(2)}) collective-permute-start(f32[2,256]{1,0:T(2,128)S(1)} %get-tuple-element.54), channel_id=1, source_target_pairs={{8,17},{9,18},{10,19},{11,20},{12,21},{13,22},{14,23}} | collective-permute-start | bytes 6152 | tf_op jit(solution)/shard_map/ppermute | solution.py:699

commit v8 on v7

--- a/solution.py
+++ b/solution.py
@@ -414,7 +414,7 @@
 
 
 def slot_rows(halves):
-    return 4 * halves + 1
+    return max(up(4 * halves + 1, SUB), KP)
 
 
 def make_vectors(zr_ref, zi_ref, beta_ref, state_ref, vec_ref):
@@ -443,7 +443,7 @@
 def vectors(pixel_ref, zr_ref, zi_ref, tile_ref, beta_ref, state_ref, vec_ref, slot_ref):
     _, rows, pixels = zr_ref.shape
     halves = pixels // LANES
-    section, block, blocks, start, _, _ = seat(pixels, 0)
+    section, _, _, start, _, _ = seat(pixels, 0)
 
     @pl.when(section < lax.axis_size("section") - 1)
     def _():
@@ -467,18 +467,15 @@
             f = jnp.sum(picked, axis=1, keepdims=True)
             mixed = jnp.where(lane[0:1] == LANES - 2 + c, jnp.broadcast_to(f, (1, LANES)), mixed)
         slot.append(mixed)
+        slot.append(jnp.zeros((slot_ref.shape[1] - len(slot), LANES), jnp.float32))
+        slot = jnp.concatenate(slot, axis=0)
         for n in range(slot_ref.shape[0]):
-            for m, one in enumerate(slot):
-                slot_ref[n, m] = one
+            slot_ref[n] = slot
 
     @pl.when(section == lax.axis_size("section") - 1)
     def _():
-        piece = up(KP, blocks) // blocks
-        for i in range(piece):
-            at = jnp.minimum(block * piece + i, KP - 1)
-            one = tile_ref[pl.ds(at, 1), :]
-            for n in range(slot_ref.shape[0]):
-                slot_ref[n, i] = one
+        for n in range(slot_ref.shape[0]):
+            slot_ref[n, 0:KP] = tile_ref[...]
 
 
 def unfold(fold_ref, fr_ref, fi_ref):
@@ -515,9 +512,9 @@
                 for h in range(halves):
                     add_ref[c, h] = folds[s][count + c, h]
 
-    piece = up(KP, blocks) // blocks
-    tile = [got_ref[final * blocks + n // piece, n % piece] for n in range(KP)]
-    tile = jnp.concatenate(tile, axis=0)
+    tile = got_ref[final * blocks, 0:KP]
+    for q in range(1, blocks):
+        tile = tile + got_ref[final * blocks + q, 0:KP]
     k_row = lax.broadcasted_iota(jnp.int32, (KP, LANES), 0)
     lane = lax.broadcasted_iota(jnp.int32, (KP, LANES), 1)
     turned = jnp.transpose(jnp.concatenate([tile, jnp.zeros((LANES - KP, LANES), jnp.float32)], axis=0))[0:KP]
@@ -538,7 +535,7 @@
     low, high = jnp.maximum(mine - 1, 0), jnp.minimum(mine + 1, blocks - 1)
     for at, which in ((low, range(halves - per, halves)), (mine, range(halves)), (high, range(per))):
         for h in which:
-            tiles.append([got_ref[before * blocks + at, c * halves + h] for c in range(2)])
+            tiles.append([got_ref[before * blocks + at, c * halves + h : c * halves + h + 1] for c in range(2)])
     virtual = take_virtual(idx_ref, start - reach, reach, tiles, halves, count)
     near = spread(tile, KP + 2).astype(jnp.int32)
     total = [jnp.zeros((KP, LANES), jnp.float32) for _ in range(2)]
@@ -546,7 +543,8 @@
         for h in range(halves):
             hit = lane == near - (q * pixels + h * LANES)
             for c in range(2):
-                total[c] = total[c] + jnp.where(hit, got_ref[before * blocks + q, c * halves + h], 0.0)
+                row = got_ref[before * blocks + q, c * halves + h : c * halves + h + 1]
+                total[c] = total[c] + jnp.where(hit, row, 0.0)
     total = [jnp.broadcast_to(jnp.sum(x, axis=1, keepdims=True), (KP, LANES)) for x in total]
     total = [jnp.where(k_row < count, x, 0.0) for x in total]
     virtual.append(scaled([x[0:1] for x in total], *total))
@@ -565,7 +563,7 @@
         for q in range(blocks):
             first = pixel_ref[0:1] - q * pixels
             here = jnp.logical_and(first >= 0, first < pixels)
-            total = total + jnp.where(here, got_ref[s * blocks + q, 4 * halves], 0.0)
+            total = total + jnp.where(here, got_ref[s * blocks + q, 4 * halves : 4 * halves + 1], 0.0)
         return total
 
     def times(d, later, fr, fi):
@@ -579,7 +577,7 @@
         datum[h] = times(datum[h], section < final, state_ref[2:3, half(h)], state_ref[3:4, half(h)])
     for s in range(final - 1, 0, -1):
         later = section < s
-        own = [got_ref[s * blocks + mine, 2 * halves + m] for m in range(2 * halves)]
+        own = [got_ref[s * blocks + mine, 2 * halves + m : 2 * halves + m + 1] for m in range(2 * halves)]
         row = of_pixel(s)
         for h in range(halves):
             datum[h] = times(datum[h], later, own[h], own[halves + h])
@@ -683,11 +681,11 @@
     zr, zi, gr, gi, sums, beta, state, folded, tile = prepare(False, made_0)
 
     final = sections - 1
-    step = 1
-    while step < blocks:
-        pairs = [(final * blocks + q, final * blocks + (q + step) % blocks) for q in range(blocks)]
-        tile = tile + lax.ppermute(tile, ("section", "pix"), pairs)
-        step *= 2
+    folds = []
+    for s in range(final):
+        pairs = [(final * blocks + q, s * blocks + q) for q in range(blocks)]
+        folds.append(lax.ppermute(folded, ("section", "pix"), pairs))
+    folds.append(folded)
 
     for rnd in range(1, final):
         def hop(shift):
@@ -704,7 +702,7 @@
         outs = [f32(2, halves, KP, LANES), f32(SUB, pixels), f32(2, pixels)]
         if last:
             scratch += [pltpu.VMEM(o.shape, o.dtype) for o in outs[:2]]
-            outs = outs[2:] + [f32(2, dates, pixels), f32(sections * blocks, slot_rows(halves), 1, LANES)]
+            outs = outs[2:] + [f32(2, dates, pixels), f32(sections * blocks, slot_rows(halves), LANES)]
         call = pl.pallas_call(
             functools.partial(round_kernel, rnd, stack),
             out_shape=outs,
@@ -719,13 +717,6 @@
             comp, vec, sent = made
         else:
             beta, state, comp = made
-        if rnd == 1:
-            later = lax.optimization_barrier((folded, comp))[0]
-            folds = []
-            for s in range(final):
-                pairs = [(final * blocks + q, s * blocks + q) for q in range(blocks)]
-                folds.append(lax.ppermute(later, ("section", "pix"), pairs))
-            folds.append(folded)
 
     sent, *folds = lax.optimization_barrier((sent, *folds))
     got = lax.all_to_all(sent, ("section", "pix"), 0, 0, tiled=True)

time: 60.4 us -> 57.3 us (0.949)
  waiting for transfers between devices: 9.71 us -> 1.31 us
  starting transfers between devices: 12.8 us -> 17.6 us
    ppermute x6 -> x3, waiting for transfers between devices: 8.47 us -> 0.01 us  [on_device(): folds.append(lax.ppermute(folded, ('section', 'pix'), pairs))]
    ppermute x6, starting transfers between devices: 7.01 us -> 13.7 us  [hop(): return lax.ppermute(comp, ('section', 'pix'), pairs)]
    ppermute x6 -> x3, starting transfers between devices: 4.62 us -> 2.65 us  [on_device(): folds.append(lax.ppermute(folded, ('section', 'pix'), pairs))]
  transfers between devices with their start and end apart: 14 -> 11, of which waited for: 2 -> 1; matrix products, arithmetic and copies ran while one was open for 0% -> 0% of each run, Pallas kernels for 4% -> 4%
where the time goes in v8:
time: 57.3 us; the launch traced here: 56.7 us
  blocking collectives  25.6 us (45%)
  starting transfers between devices  17.6 us (31%)
  Pallas kernels  10.8 us (19%)
  between operations  1.47 us (3%)
  waiting for transfers between devices  1.31 us (2%)
    all_to_all x1, blocking collectives, on_device(): got = lax.all_to_all(sent, ('section', 'pix'), 0, 0, tiled=True)  25.6 us
    ppermute x6, starting transfers between devices, hop(): return lax.ppermute(comp, ('section', 'pix'), pairs)  13.7 us
    pallas_call x2, Pallas kernels, prepare(): pl.pallas_call(functools.partial(prepare_kernel, stack, first), out_shape...  4.85 us
    pallas_call x1, Pallas kernels, on_device(): pl.pallas_call(functools.partial(finish_kernel, sections, stack), out_sha...  3.4 us
    ppermute x3, starting transfers between devices, on_device(): folds.append(lax.ppermute(folded, ('section', 'pix'), pairs))  2.65 us
    pallas_call x1, Pallas kernels, on_device(): pl.pallas_call(own_kernel, out_shape=made[:2] + [f32(2 * rows, pixels + r...  2.05 us
    ppermute x6, waiting for transfers between devices, hop(): return lax.ppermute(comp, ('section', 'pix'), pairs)  1.29 us
    ppermute x2, starting transfers between devices, swap(): return lax.ppermute(sent, 'pix', pairs)  1.21 us
  transfers between devices with their start and end apart: 11, of which 1 were waited for; matrix products, arithmetic and copies ran while one was open for 0% of the time, Pallas kernels for 4%

profile of v8, /device:TPU:0, one launch (start us, length us, event | category | flops | bytes accessed | tf_op | source)
XLA Modules:
  0.0 56.7 jit_solution(845229381159975256)
XLA Ops:
  0.6 0.6 collective-permute-start
  1.2 0.7 %collective-permute-start.1 = (f32[50,2,256]{2,1,0:T(2,128)}, f32[50,2,256]{2,1,0:T(2,128)S(1)}, u32[]{:S(2)}, u32[]{:S(2)}) collective-permute-start(f32[50,2,256]{2,1,0:T(2,128)} %bitcast.5), channel_id=1, source_target_pairs={{1,2},{3,4},{5,6},{2,1},{4,3},{6,5},{9,10},{11,12},{13,14},{10,9},... | collective-permute-start | bytes 307208 | tf_op jit(solution)/shard_map/ppermute | solution.py:635
  2.5 0.0 collective-permute-done.near_ref
  2.5 2.0 %own.1 = (f32[15,56,256]{2,1,0:T(8,128)S(1)}, f32[15,56,256]{2,1,0:T(8,128)S(1)}, f32[112,512]{1,0:T(8,128)S(1)}, s32[15,256]{1,0:T(8,128)S(1)}) custom-call(s32[15,256]{1,0:T(8,128)} %idx_hbm.1, f32[50,2,256]{2,1,0:T(2,128)} %bitcast.6, f32[50,2,256]{2,1,0:T(2,128)S(1)} %collective-permute-done.near_ref), custom_call_target="tpu_custom_call" | custom-call | flops 880803840 | tf_op jit(solution)/shard_map/own/pallas_call | solution.py:645
  4.6 0.0 collective-permute-done.1.far_ref
  4.6 4.8 %shard_map.50 = (f32[15,56,256]{2,1,0:T(8,128)S(1)}, f32[15,56,256]{2,1,0:T(8,128)S(1)}, f32[16,2,16,128]{3,2,1,0:T(8,128)S(1)}, f32[16,2,16,128]{3,2,1,0:T(8,12...) custom-call(s32[15,256]{1,0:T(8,128)S(1)} %get-tuple-element.36.idx_, ...), custom_call_target="tpu_custom_call", output_to_operand_aliasing={{0}: (3, {}), {1}: (4, {})} | custom-call | flops 33030144000 | tf_op jit(solution)/shard_map/pallas_call | solution.py:665
  9.4 0.7 %collective-permute-start.10 = (f32[17,2,16,128]{3,2,1,0:T(8,128)S(1)}, f32[17,2,16,128]{3,2,1,0:T(8,128)S(1)}, u32[]{:S(2)}, u32[]{:S(2)}) collective-permute-start(f32[17,2,16,128]{3,2,1,0:T(8,128)S(1)} %get-tuple-element.67.refs_3_), channel_id=1, source_target_pairs={{24,16},{25,17},{26,18},{27,19},{28,20},{29,21},{30,22},{31,23}} | collective-permute-start | bytes 835592 | tf_op jit(solution)/shard_map/ppermute | solution.py:687
  10.1 0.7 %collective-permute-start.9 = (f32[17,2,16,128]{3,2,1,0:T(8,128)S(1)}, f32[17,2,16,128]{3,2,1,0:T(8,128)S(1)}, u32[]{:S(2)}, u32[]{:S(2)}) collective-permute-start(f32[17,2,16,128]{3,2,1,0:T(8,128)S(1)} %get-tuple-element.67.refs_3_), channel_id=1, source_target_pairs={{24,8},{25,9},{26,10},{27,11},{28,12},{29,13},{30,14},{31,15}} | collective-permute-start | bytes 835592 | tf_op jit(solution)/shard_map/ppermute | solution.py:687
  10.8 1.3 %collective-permute-start.8 = (f32[17,2,16,128]{3,2,1,0:T(8,128)S(1)}, f32[17,2,16,128]{3,2,1,0:T(8,128)S(1)}, u32[]{:S(2)}, u32[]{:S(2)}) collective-permute-start(f32[17,2,16,128]{3,2,1,0:T(8,128)S(1)} %get-tuple-element.67.refs_3_), channel_id=1, source_target_pairs={{24,0},{25,1},{26,2},{27,3},{28,4},{29,5},{30,6},{31,7}} | collective-permute-start | bytes 835592 | tf_op jit(solution)/shard_map/ppermute | solution.py:687
  12.1 0.7 %collective-permute-start.4 = (f32[2,256]{1,0:T(2,128)S(1)}, f32[2,256]{1,0:T(2,128)S(1)}, u32[]{:S(2)}, u32[]{:S(2)}) collective-permute-start(f32[2,256]{1,0:T(2,128)S(1)} %get-tuple-element.40), channel_id=1, source_target_pairs={{1,8},{2,9},{3,10},{4,11},{5,12},{6,13},{7,14}} | collective-permute-start | bytes 6152 | tf_op jit(solution)/shard_map/ppermute | solution.py:697
  12.8 4.0 %collective-permute-start.3 = (f32[2,256]{1,0:T(2,128)S(1)}, f32[2,256]{1,0:T(2,128)S(1)}, u32[]{:S(2)}, u32[]{:S(2)}) collective-permute-start(f32[2,256]{1,0:T(2,128)S(1)} %get-tuple-element.40), channel_id=1, source_target_pairs={{0,8},{1,9},{2,10},{3,11},{4,12},{5,13},{6,14},{7,15}} | collective-permute-start | bytes 6152 | tf_op jit(solution)/shard_map/ppermute | solution.py:697
  16.8 0.0 collective-permute-done.4.high_ref
  16.8 7.1 %collective-permute-start.2 = (f32[2,256]{1,0:T(2,128)S(1)}, f32[2,256]{1,0:T(2,128)S(1)}, u32[]{:S(2)}, u32[]{:S(2)}) collective-permute-start(f32[2,256]{1,0:T(2,128)S(1)} %get-tuple-element.40), channel_id=1, source_target_pairs={{0,9},{1,10},{2,11},{3,12},{4,13},{5,14},{6,15}} | collective-permute-start | bytes 6152 | tf_op jit(solution)/shard_map/ppermute | solution.py:697
  23.9 0.0 collective-permute-done.3.own_ref
  23.9 1.3 %collective-permute-done.2.low_ref = f32[2,256]{1,0:T(2,128)S(1)} collective-permute-done((f32[2,256]{1,0:T(2,128)S(1)}, f32[2,256]{1,0:T(2,128)S(1)}, u32[]{:S(2)}, u32[]{:S(2)}) %collective-permute-start.2) | collective-permute-done | bytes 2080 | tf_op jit(solution)/shard_map/ppermute | solution.py:697
  25.2 0.6 %collective-permute-start.7 = (f32[2,256]{1,0:T(2,128)S(1)}, f32[2,256]{1,0:T(2,128)S(1)}, u32[]{:S(2)}, u32[]{:S(2)}) collective-permute-start(f32[2,256]{1,0:T(2,128)S(1)} %get-tuple-element.53), channel_id=1, source_target_pairs={{9,16},{10,17},{11,18},{12,19},{13,20},{14,21},{15,22}} | collective-permute-start | bytes 6152 | tf_op jit(solution)/shard_map/ppermute | solution.py:697
  25.9 0.7 %collective-permute-start.6 = (f32[2,256]{1,0:T(2,128)S(1)}, f32[2,256]{1,0:T(2,128)S(1)}, u32[]{:S(2)}, u32[]{:S(2)}) collective-permute-start(f32[2,256]{1,0:T(2,128)S(1)} %get-tuple-element.53), channel_id=1, source_target_pairs={{8,16},{9,17},{10,18},{11,19},{12,20},{13,21},{14,22},{15,23}} | collective-permute-start | bytes 6152 | tf_op jit(solution)/shard_map/ppermute | solution.py:697
  26.5 0.0 collective-permute-done.7.high_ref
  26.5 0.7 %collective-permute-start.5 = (f32[2,256]{1,0:T(2,128)S(1)}, f32[2,256]{1,0:T(2,128)S(1)}, u32[]{:S(2)}, u32[]{:S(2)}) collective-permute-start(f32[2,256]{1,0:T(2,128)S(1)} %get-tuple-element.53), channel_id=1, source_target_pairs={{8,17},{9,18},{10,19},{11,20},{12,21},{13,22},{14,23}} | collective-permute-start | bytes 6152 | tf_op jit(solution)/shard_map/ppermute | solution.py:697
  27.2 0.0 collective-permute-done.6.own_ref
  27.2 0.0 collective-permute-done.5.low_ref
  27.2 0.5 shard_map.53
  27.7 0.0 collective-permute-done.10.refs_2_
  27.7 0.0 collective-permute-done.9.refs_1_
  27.7 0.0 collective-permute-done.8.refs_0_
  27.8 25.6 %all_to_all.5.got_ref = f32[32,16,128]{2,1,0:T(8,128)S(1)} all-to-all(f32[32,16,128]{2,1,0:T(8,128)S(1)} %get-tuple-element.61), channel_id=1, replica_groups=mesh['section'=4,'pix'=8] {'section','pix'}, dimensions={0} | all-to-all | bytes 524288 | tf_op jit(solution)/shard_map/all_to_all | solution.py:722
  53.3 3.4 %finish.1 = (f32[50,2,256]{2,1,0:T(2,128)}, f32[2,1,256]{2,1,0:T(1,128)}) custom-call(s32[8,128]{1,0:T(8,128)S(1)} %broadcast_in_dim.3.refs_0_.pixel_ref, s32[15,256]{1,0:T(8,128)S(1)} %get-tuple-element.36.idx_ref, f32[32,16,128]{2,1,0:T(8,128)S(1)} %all_to_all.5.got_ref, f32[2,50,256]{2,1,0:T(8,128)S(1)} %get-tuple-element.62.vec0_ref, ...), custom_call_target="tpu_custom_call" | custom-call | tf_op jit(solution)/shard_map/finish/pallas_call | solution.py:723
  (3 shorter events, 0.0 us)
Async XLA Ops:
  0.6 1.9 %collective-permute-start = (f32[50,2,256]{2,1,0:T(2,128)}, f32[50,2,256]{2,1,0:T(2,128)S(1)}, u32[]{:S(2)}, u32[]{:S(2)}) collective-permute-start(f32[50,2,256]{2,1,0:T(2,128)} %bitcast.4), channel_id=1, source_target_pairs={{0,1},{2,3},{4,5},{6,7},{1,0},{3,2},{5,4},{7,6},{8,9},{10,11},{12,... | collective-permute-start | bytes 307208 | tf_op jit(solution)/shard_map/ppermute | solution.py:635
  1.2 3.4 %collective-permute-start.1 = (f32[50,2,256]{2,1,0:T(2,128)}, f32[50,2,256]{2,1,0:T(2,128)S(1)}, u32[]{:S(2)}, u32[]{:S(2)}) collective-permute-start(f32[50,2,256]{2,1,0:T(2,128)} %bitcast.5), channel_id=1, source_target_pairs={{1,2},{3,4},{5,6},{2,1},{4,3},{6,5},{9,10},{11,12},{13,14},{10,9},... | collective-permute-start | bytes 307208 | tf_op jit(solution)/shard_map/ppermute | solution.py:635
  9.4 18.3 %collective-permute-start.10 = (f32[17,2,16,128]{3,2,1,0:T(8,128)S(1)}, f32[17,2,16,128]{3,2,1,0:T(8,128)S(1)}, u32[]{:S(2)}, u32[]{:S(2)}) collective-permute-start(f32[17,2,16,128]{3,2,1,0:T(8,128)S(1)} %get-tuple-element.67.refs_3_), channel_id=1, source_target_pairs={{24,16},{25,17},{26,18},{27,19},{28,20},{29,21},{30,22},{31,23}} | collective-permute-start | bytes 835592 | tf_op jit(solution)/shard_map/ppermute | solution.py:687
  10.1 17.6 %collective-permute-start.9 = (f32[17,2,16,128]{3,2,1,0:T(8,128)S(1)}, f32[17,2,16,128]{3,2,1,0:T(8,128)S(1)}, u32[]{:S(2)}, u32[]{:S(2)}) collective-permute-start(f32[17,2,16,128]{3,2,1,0:T(8,128)S(1)} %get-tuple-element.67.refs_3_), channel_id=1, source_target_pairs={{24,8},{25,9},{26,10},{27,11},{28,12},{29,13},{30,14},{31,15}} | collective-permute-start | bytes 835592 | tf_op jit(solution)/shard_map/ppermute | solution.py:687
  10.8 16.9 %collective-permute-start.8 = (f32[17,2,16,128]{3,2,1,0:T(8,128)S(1)}, f32[17,2,16,128]{3,2,1,0:T(8,128)S(1)}, u32[]{:S(2)}, u32[]{:S(2)}) collective-permute-start(f32[17,2,16,128]{3,2,1,0:T(8,128)S(1)} %get-tuple-element.67.refs_3_), channel_id=1, source_target_pairs={{24,0},{25,1},{26,2},{27,3},{28,4},{29,5},{30,6},{31,7}} | collective-permute-start | bytes 835592 | tf_op jit(solution)/shard_map/ppermute | solution.py:687
  12.1 4.6 %collective-permute-start.4 = (f32[2,256]{1,0:T(2,128)S(1)}, f32[2,256]{1,0:T(2,128)S(1)}, u32[]{:S(2)}, u32[]{:S(2)}) collective-permute-start(f32[2,256]{1,0:T(2,128)S(1)} %get-tuple-element.40), channel_id=1, source_target_pairs={{1,8},{2,9},{3,10},{4,11},{5,12},{6,13},{7,14}} | collective-permute-start | bytes 6152 | tf_op jit(solution)/shard_map/ppermute | solution.py:697
  12.8 11.1 %collective-permute-start.3 = (f32[2,256]{1,0:T(2,128)S(1)}, f32[2,256]{1,0:T(2,128)S(1)}, u32[]{:S(2)}, u32[]{:S(2)}) collective-permute-start(f32[2,256]{1,0:T(2,128)S(1)} %get-tuple-element.40), channel_id=1, source_target_pairs={{0,8},{1,9},{2,10},{3,11},{4,12},{5,13},{6,14},{7,15}} | collective-permute-start | bytes 6152 | tf_op jit(solution)/shard_map/ppermute | solution.py:697
  16.8 8.4 %collective-permute-start.2 = (f32[2,256]{1,0:T(2,128)S(1)}, f32[2,256]{1,0:T(2,128)S(1)}, u32[]{:S(2)}, u32[]{:S(2)}) collective-permute-start(f32[2,256]{1,0:T(2,128)S(1)} %get-tuple-element.40), channel_id=1, source_target_pairs={{0,9},{1,10},{2,11},{3,12},{4,13},{5,14},{6,15}} | collective-permute-start | bytes 6152 | tf_op jit(solution)/shard_map/ppermute | solution.py:697
  25.2 1.3 %collective-permute-start.7 = (f32[2,256]{1,0:T(2,128)S(1)}, f32[2,256]{1,0:T(2,128)S(1)}, u32[]{:S(2)}, u32[]{:S(2)}) collective-permute-start(f32[2,256]{1,0:T(2,128)S(1)} %get-tuple-element.53), channel_id=1, source_target_pairs={{9,16},{10,17},{11,18},{12,19},{13,20},{14,21},{15,22}} | collective-permute-start | bytes 6152 | tf_op jit(solution)/shard_map/ppermute | solution.py:697
  25.9 1.4 %collective-permute-start.6 = (f32[2,256]{1,0:T(2,128)S(1)}, f32[2,256]{1,0:T(2,128)S(1)}, u32[]{:S(2)}, u32[]{:S(2)}) collective-permute-start(f32[2,256]{1,0:T(2,128)S(1)} %get-tuple-element.53), channel_id=1, source_target_pairs={{8,16},{9,17},{10,18},{11,19},{12,20},{13,21},{14,22},{15,23}} | collective-permute-start | bytes 6152 | tf_op jit(solution)/shard_map/ppermute | solution.py:697
  26.5 0.7 %collective-permute-start.5 = (f32[2,256]{1,0:T(2,128)S(1)}, f32[2,256]{1,0:T(2,128)S(1)}, u32[]{:S(2)}, u32[]{:S(2)}) collective-permute-start(f32[2,256]{1,0:T(2,128)S(1)} %get-tuple-element.53), channel_id=1, source_target_pairs={{8,17},{9,18},{10,19},{11,20},{12,21},{13,22},{14,23}} | collective-permute-start | bytes 6152 | tf_op jit(solution)/shard_map/ppermute | solution.py:697

commit v9 on v8

--- a/solution.py
+++ b/solution.py
@@ -181,20 +181,18 @@
                 sum_ref[c, h, pl.ds(kt * SUB, SUB), :] = merge_rows(tiles[kt * SUB : kt * SUB + SUB])
 
 
-def turns(gr_ref, gi_ref, g0, count):
+def turns(gr_ref, gs_ref, gd_ref, g0, count):
     halves = gr_ref.shape[1]
 
     def product(b, g):
-        acc = [list(x) for x in g]
+        acc = [None] * halves
         for l in range(count):
             for h in range(halves):
                 br = jnp.broadcast_to(b[h][0][l : l + 1], (KP, LANES))
                 bi = jnp.broadcast_to(b[h][1][l : l + 1], (KP, LANES))
-                gr = gr_ref[l, h]
-                gi = gi_ref[l, h]
-                acc[h][0] = acc[h][0] + (gr * br - gi * bi)
-                acc[h][1] = acc[h][1] + (gr * bi + gi * br)
-        return acc
+                new = [gr_ref[l, h] * (br + bi), gs_ref[l, h] * bi, gd_ref[l, h] * br]
+                acc[h] = new if l == 0 else [x + y for x, y in zip(acc[h], new)]
+        return [(g[h][0] + (t - u), g[h][1] + (t + v)) for h, (t, u, v) in enumerate(acc)]
 
     def step(_, carry):
         b, g = carry
@@ -210,7 +208,7 @@
     return b, g, product(b, g)
 
 
-def solve(virtual, gr_ref, gi_ref, hr, hi, sums, stack, beta_ref, state_ref):
+def solve(virtual, gr_ref, gs_ref, gd_ref, hr, hi, sums, stack, beta_ref, state_ref):
     halves = gr_ref.shape[1]
     count = gr_ref.shape[0]
     first = 1.0 / math.sqrt(stack)
@@ -224,7 +222,7 @@
             zr = zr + virtual[h][1][0]
             zi = zi + virtual[h][1][1]
         g0.append((zr * first, zi * -first))
-    b, g, t = turns(gr_ref, gi_ref, g0, count)
+    b, g, t = turns(gr_ref, gs_ref, gd_ref, g0, count)
     for h in range(halves):
         norm = colsum(b[h][0] * (g[h][0] + t[h][0]) + b[h][1] * (g[h][1] + t[h][1]))
         inv = lax.rsqrt(SHRINK * SHRINK + norm)
@@ -264,8 +262,6 @@
 
 
 def prepare_kernel(stack, first, idx_ref, far_ref, own_ref, *refs):
-    if not first:
-        pixel_ref, refs = refs[0], refs[1:]
     refs = refs[2 if first else 7 :]
     zr_ref, zi_ref, gr_ref, gi_ref, sum_ref, beta_ref, state_ref = refs[:7]
     xs_ref, hl_ref, pair_ref = refs[-3:]
@@ -283,20 +279,39 @@
             hr = [gr_ref[count, h] for h in range(halves)]
             hi = [gi_ref[count, h] for h in range(halves)]
             sums = [(sum_ref[0, h], sum_ref[1, h]) for h in range(halves)]
-            solve(None, gr_ref.at[0:count], gi_ref.at[0:count], hr, hi, sums, stack, beta_ref, state_ref)
+            gs_ref, gd_ref = refs[8:10]
+            for l in range(count):
+                for h in range(halves):
+                    gs_ref[l, h] = gi_ref[l, h] + gr_ref[l, h]
+                    gd_ref[l, h] = gi_ref[l, h] - gr_ref[l, h]
+            solve(None, gr_ref.at[0:count], gs_ref, gd_ref, hr, hi, sums, stack, beta_ref, state_ref)
             refs[7][...] = state_ref[0:2]
 
     if not first:
 
         @pl.when(section == lax.axis_size("section") - 1)
         def _():
-            fold(start, pixel_ref, idx_ref, zr_ref, zi_ref, gr_ref, gi_ref, sum_ref, refs[7], refs[8])
-
-
-def fold(start, pixel_ref, idx_ref, zr_ref, zi_ref, gr_ref, gi_ref, sum_ref, fold_ref, tile_ref):
+            fold(gr_ref, gi_ref, sum_ref, refs[7])
+
+
+def folded_column(l, h, gr_ref, gi_ref, sum_ref):
+    count = gr_ref.shape[0] - 1
+    if l >= count:
+        return sum_ref[l - count, h]
+    k_row = lax.broadcasted_iota(jnp.int32, (KP, LANES), 0)
+    return jnp.where(k_row <= l, gr_ref[l, h], gi_ref[l, h])
+
+
+def fold(gr_ref, gi_ref, sum_ref, fold_ref):
+    halves = gr_ref.shape[1]
+    for l in range(gr_ref.shape[0] + 1):
+        for h in range(halves):
+            fold_ref[pl.ds((l * halves + h) * KP, KP), :] = folded_column(l, h, gr_ref, gi_ref, sum_ref)
+
+
+def make_tile(start, pixel_ref, idx_ref, zr_ref, zi_ref, gr_ref, gi_ref, sum_ref):
     count, rows, pixels = zr_ref.shape
     halves = pixels // LANES
-    k_row = lax.broadcasted_iota(jnp.int32, (KP, LANES), 0)
     lane = lax.broadcasted_iota(jnp.int32, (KP, LANES), 1)
     local = pixel_ref[...] - start
     hit = [lax.broadcasted_iota(jnp.int32, (SUB, LANES), 1) == local - h * LANES for h in range(halves)]
@@ -311,14 +326,7 @@
 
     tile = jnp.zeros((KP, LANES), jnp.float32)
     for l in range(count + 2):
-        parts = []
-        for h in range(halves):
-            if l < count:
-                part = jnp.where(k_row <= l, gr_ref[l, h], gi_ref[l, h])
-            else:
-                part = sum_ref[l - count, h]
-            fold_ref[l, h] = part
-            parts.append(part)
+        parts = [folded_column(l, h, gr_ref, gi_ref, sum_ref) for h in range(halves)]
         tile = jnp.where(lane == (l if l < count else KP + l - count), column(parts), tile)
     pad = jnp.zeros((KP - count, LANES), jnp.float32)
     near = [jnp.concatenate([idx_ref[:, half(h)].astype(jnp.float32), pad], axis=0) for h in range(halves)]
@@ -332,7 +340,7 @@
         turned = jnp.transpose(jnp.concatenate([both, empty], axis=0))[0:KP]
         at = Z_LANE + c * Z_STEP
         tile = jnp.where(jnp.logical_and(lane >= at, lane < at + Z_STEP), pltpu.roll(turned, at, 1), tile)
-    tile_ref[...] = tile
+    return tile
 
 
 def lane_take(x, i):
@@ -369,25 +377,29 @@
     return virtual
 
 
-def update(virtual, gr_ref, gi_ref, fr_ref, fi_ref):
+def update(virtual, gram_of, fr_ref, fs_ref, fd_ref):
     for h, (_, (zr, zi)) in enumerate(virtual):
         for l in range(fr_ref.shape[0]):
+            gr, gi = gram_of(l, h)
             br = jnp.broadcast_to(zr[l : l + 1], (KP, LANES))
             bi = jnp.broadcast_to(zi[l : l + 1], (KP, LANES))
-            fr_ref[l, h] = gr_ref[l, h] + (zr * br + zi * bi)
-            fi_ref[l, h] = gi_ref[l, h] + (zr * bi - zi * br)
+            gr = gr + (zr * br + zi * bi)
+            gi = gi + (zr * bi - zi * br)
+            fr_ref[l, h] = gr
+            fs_ref[l, h] = gi + gr
+            fd_ref[l, h] = gi - gr
 
 
 def round_kernel(
     rnd, stack, idx_ref, low_ref, own_ref, high_ref,
     gr_ref, gi_ref, sum_ref, beta0_ref, state0_ref, *refs,
 ):
-    last = len(refs) > 5
+    last = len(refs) > 6
     if last:
-        late, (comp_ref, *made), refs = refs[:4], refs[4:7], refs[7:]
-        fr_ref, fi_ref, beta_ref, state_ref = refs
+        late, (comp_ref, *made), refs = refs[:3], refs[3:6], refs[6:]
+        fr_ref, fs_ref, fd_ref, beta_ref, state_ref = refs
     else:
-        beta_ref, state_ref, comp_ref, fr_ref, fi_ref = refs
+        beta_ref, state_ref, comp_ref, fr_ref, fs_ref, fd_ref = refs
     count = gr_ref.shape[0] - 1
     halves = gr_ref.shape[1]
     reach = low_ref.shape[1]
@@ -402,15 +414,15 @@
             for t in range(ref.shape[1] // LANES):
                 tiles.append([ref[c : c + 1, half(t)] for c in range(2)])
         virtual = take_virtual(idx_ref, start - reach, reach, tiles, halves, count)
-        update(virtual, gr_ref, gi_ref, fr_ref, fi_ref)
+        update(virtual, lambda l, h: (gr_ref[l, h], gi_ref[l, h]), fr_ref, fs_ref, fd_ref)
         hr = [gr_ref[count, h] for h in range(halves)]
         hi = [gi_ref[count, h] for h in range(halves)]
         sums = [(sum_ref[0, h], sum_ref[1, h]) for h in range(halves)]
-        solve(virtual, fr_ref, fi_ref, hr, hi, sums, stack, beta_ref, state_ref)
+        solve(virtual, fr_ref, fs_ref, fd_ref, hr, hi, sums, stack, beta_ref, state_ref)
 
     comp_ref[...] = state_ref[0:2]
     if last:
-        vectors(*late, beta_ref, state_ref, *made)
+        vectors(*late, idx_ref, gr_ref, gi_ref, sum_ref, beta_ref, state_ref, *made)
 
 
 def slot_rows(halves):
@@ -440,7 +452,7 @@
     return out
 
 
-def vectors(pixel_ref, zr_ref, zi_ref, tile_ref, beta_ref, state_ref, vec_ref, slot_ref):
+def vectors(pixel_ref, zr_ref, zi_ref, idx_ref, gr_ref, gi_ref, sum_ref, beta_ref, state_ref, vec_ref, slot_ref):
     _, rows, pixels = zr_ref.shape
     halves = pixels // LANES
     section, _, _, start, _, _ = seat(pixels, 0)
@@ -474,28 +486,24 @@
 
     @pl.when(section == lax.axis_size("section") - 1)
     def _():
+        tile = make_tile(start, pixel_ref, idx_ref, zr_ref, zi_ref, gr_ref, gi_ref, sum_ref)
         for n in range(slot_ref.shape[0]):
-            slot_ref[n, 0:KP] = tile_ref[...]
-
-
-def unfold(fold_ref, fr_ref, fi_ref):
-    count = fr_ref.shape[0]
-    k_row = lax.broadcasted_iota(jnp.int32, (KP, LANES), 0)
-    for h in range(fold_ref.shape[1]):
-        for l in range(count):
-            straight = fold_ref[l, h]
-            turned = jnp.concatenate(
-                [fold_ref[k, h, pl.ds(l, 1), :] for k in range(count)] + [jnp.zeros((KP - count, LANES), jnp.float32)], axis=0
-            )
-            fr_ref[l, h] = jnp.where(k_row <= l, straight, turned)
-            fi_ref[l, h] = jnp.where(k_row > l, straight, jnp.where(k_row < l, -turned, 0.0))
+            slot_ref[n, 0:KP] = tile
+
+
+def unfold(fold, l, h, k_row, count):
+    straight, turned = fold[0](l, h), jnp.where(k_row < count, fold[1](l, h), 0.0)
+    return (
+        jnp.where(k_row <= l, straight, turned),
+        jnp.where(k_row > l, straight, jnp.where(k_row < l, -turned, 0.0)),
+    )
 
 
 def finish_kernel(
     sections, stack, pixel_ref, idx_ref, got_ref, vec0_ref, comp0_ref, zr_ref, zi_ref, gr_ref, gi_ref, sum_ref, *refs
 ):
     folds, (out_ref, small_ref), refs = refs[:sections], refs[sections : sections + 2], refs[sections + 2 :]
-    fr_ref, fi_ref, add_ref, beta_ref, state_ref, vec_ref = refs
+    fold_ref, fr_ref, fs_ref, fd_ref, beta_ref, state_ref, vec_ref = refs
     dates, pixels = vec_ref.shape[1:]
     count = zr_ref.shape[0]
     section, mine, blocks, start, _, _ = seat(pixels, 0)
@@ -507,10 +515,7 @@
 
         @pl.when(section == s)
         def _(s=s):
-            unfold(folds[s], fr_ref, fi_ref)
-            for c in range(2):
-                for h in range(halves):
-                    add_ref[c, h] = folds[s][count + c, h]
+            fold_ref[...] = folds[s][...]
 
     tile = got_ref[final * blocks, 0:KP]
     for q in range(1, blocks):
@@ -524,10 +529,23 @@
     def spread(x, l):
         return jnp.broadcast_to(x[:, l : l + 1], (KP, LANES))
 
-    for l in range(count):
-        fr_ref[l, halves] = spread(real, l)
-        fi_ref[l, halves] = spread(imag, l)
-    sums = [(add_ref[0, h], add_ref[1, h]) for h in range(halves)] + [(spread(tile, KP), spread(tile, KP + 1))]
+    per_l = halves * KP
+
+    def fold_of(l, h):
+        return fold_ref[pl.ds(l * per_l + h * KP, KP), :]
+
+    def fold_turned(l, h):
+        return jnp.concatenate(
+            [fold_ref[pl.ds(k0 * per_l + h * KP + l, SUB, stride=per_l), :] for k0 in range(0, KP, SUB)], axis=0
+        )
+
+    def gram_of(l, h):
+        if h == halves:
+            return spread(real, l), spread(imag, l)
+        return unfold((fold_of, fold_turned), l, h, k_row, count)
+
+    sums = [(fold_of(count, h), fold_of(count + 1, h)) for h in range(halves)]
+    sums.append((spread(tile, KP), spread(tile, KP + 1)))
 
     before = final - 1
     tiles = []
@@ -548,12 +566,12 @@
     total = [jnp.broadcast_to(jnp.sum(x, axis=1, keepdims=True), (KP, LANES)) for x in total]
     total = [jnp.where(k_row < count, x, 0.0) for x in total]
     virtual.append(scaled([x[0:1] for x in total], *total))
-    update(virtual, fr_ref, fi_ref, fr_ref, fi_ref)
+    update(virtual, gram_of, fr_ref, fs_ref, fd_ref)
 
     zero = jnp.zeros((KP, LANES), jnp.float32)
     hr = [gr_ref[count, h] for h in range(halves)] + [zero]
     hi = [gi_ref[count, h] for h in range(halves)] + [zero]
-    solve(virtual, fr_ref, fi_ref, hr, hi, sums, stack, beta_ref, state_ref)
+    solve(virtual, fr_ref, fs_ref, fd_ref, hr, hi, sums, stack, beta_ref, state_ref)
     is_final = section == final
     for c in range(2):
         small_ref[c] = jnp.where(is_final, state_ref[c : c + 1, 0:pixels], comp0_ref[c : c + 1])
@@ -644,7 +662,9 @@
     ]
     zr, zi, own, neighbours = pl.pallas_call(
         own_kernel,
-        out_shape=made[:2] + [f32(2 * rows, pixels + reach), jax.ShapeDtypeStruct(neighbours.shape, jnp.int32)],
+        out_shape=made[:2]
+        + [f32(2 * rows, pixels + reach)]
+        + [jax.ShapeDtypeStruct(neighbours.shape, jnp.int32)],
         in_specs=[HBM, HBM, VMEM],
         out_specs=[VMEM] * 4,
         scratch_shapes=[
@@ -655,30 +675,28 @@
         compiler_params=params(),
         cost_estimate=cost(2 * 4 * rows * pixels * (pixels + reach) * count),
         name="own",
-    )(pltpu.with_memory_space_constraint(neighbours, pltpu.HBM), pltpu.with_memory_space_constraint(slc, pltpu.HBM), near)
-
-    pixel = jnp.full((SUB, LANES), reference_pixel[0], jnp.int32)
+    )(*[pltpu.with_memory_space_constraint(x, pltpu.HBM) for x in (neighbours, slc)], near)
 
     def prepare(first, carried):
-        more = [] if first else [pixel]
-        outs = made if first else made[:7] + [f32(count + 2, halves, KP, LANES), f32(KP, LANES)]
+        outs = made if first else made[:7] + [f32((count + 2) * halves * KP, LANES)]
         return pl.pallas_call(
             functools.partial(prepare_kernel, stack, first),
             out_shape=outs,
-            in_specs=[VMEM] * (3 + len(more) + len(carried)),
+            in_specs=[VMEM] * (3 + len(carried)),
             out_specs=[VMEM] * len(outs),
-            scratch_shapes=[
+            scratch_shapes=([pltpu.VMEM((count, halves, KP, LANES), jnp.float32)] * 2 if first else [])
+            + [
                 pltpu.VMEM((2 * rows, reach), jnp.float32),
                 pltpu.VMEM((4 * rows, reach), jnp.bfloat16),
                 pltpu.VMEM((2, count + 1, count, SUB, LANES), jnp.float32),
             ],
-            input_output_aliases={3 + len(more) + n: n for n in range(len(carried))},
+            input_output_aliases={3 + n: n for n in range(len(carried))},
             compiler_params=params(),
             cost_estimate=cost(50 * 12 * rows * reach * pixels * count),
-        )(neighbours, far, own, *more, *carried)
+        )(neighbours, far, own, *carried)
 
     *made_0, comp = prepare(True, (zr, zi))
-    zr, zi, gr, gi, sums, beta, state, folded, tile = prepare(False, made_0)
+    zr, zi, gr, gi, sums, beta, state, folded = prepare(False, made_0)
 
     final = sections - 1
     folds = []
@@ -697,8 +715,8 @@
             return lax.ppermute(comp, ("section", "pix"), pairs)
 
         last = rnd == final - 1
-        late = (pixel, zr, zi, tile) if last else ()
-        scratch = [pltpu.VMEM((count, halves, KP, LANES), jnp.float32)] * 2
+        late = (pixel, zr, zi) if last else ()
+        scratch = [pltpu.VMEM((count, halves, KP, LANES), jnp.float32)] * 3
         outs = [f32(2, halves, KP, LANES), f32(SUB, pixels), f32(2, pixels)]
         if last:
             scratch += [pltpu.VMEM(o.shape, o.dtype) for o in outs[:2]]
@@ -717,6 +735,9 @@
             comp, vec, sent = made
         else:
             beta, state, comp = made
+        if rnd == 1:
+            pixel = lax.optimization_barrier((reference_pixel, comp))[0][0]
+            pixel = jnp.full((SUB, LANES), pixel, jnp.int32)
 
     sent, *folds = lax.optimization_barrier((sent, *folds))
     got = lax.all_to_all(sent, ("section", "pix"), 0, 0, tiled=True)
@@ -726,9 +747,10 @@
         in_specs=[VMEM] * (10 + sections),
         out_specs=[VMEM] * 2,
         scratch_shapes=[
+            pltpu.VMEM(folded.shape, jnp.float32),
             pltpu.VMEM((count, halves + 1, KP, LANES), jnp.float32),
             pltpu.VMEM((count, halves + 1, KP, LANES), jnp.float32),
-            pltpu.VMEM((2, halves, KP, LANES), jnp.float32),
+            pltpu.VMEM((count, halves + 1, KP, LANES), jnp.float32),
             pltpu.VMEM((2, halves + 1, KP, LANES), jnp.float32),
             pltpu.VMEM((SUB, pixels + LANES), jnp.float32),
             pltpu.VMEM((2, dates, pixels), jnp.float32),

time: 57.3 us -> 56.8 us (level)
  starting transfers between devices: 17.6 us -> 14.1 us
  blocking collectives: 25.6 us -> 27.7 us
  waiting for transfers between devices: 1.31 us -> 2.85 us
  Pallas kernels: 10.8 us -> 10.2 us
    ppermute x6, starting transfers between devices: 13.7 us -> 10.2 us  [hop(): return lax.ppermute(comp, ('section', 'pix'), pairs)]
    all_to_all x1, blocking collectives: 25.6 us -> 27.7 us  [on_device(): got = lax.all_to_all(sent, ('section', 'pix'), 0, 0, tiled=True)]
    ppermute x3, waiting for transfers between devices: 0.01 us -> 1.72 us  [on_device(): folds.append(lax.ppermute(folded, ('section', 'pix'), pairs))]
    ppermute x6, waiting for transfers between devices: 1.29 us -> 0.62 us  [hop(): return lax.ppermute(comp, ('section', 'pix'), pairs)]
  transfers between devices with their start and end apart: 11 -> 11, of which waited for: 1 -> 3; matrix products, arithmetic and copies ran while one was open for 0% -> 0% of each run, Pallas kernels for 4% -> 4%
where the time goes in v9:
time: 56.8 us; the launch traced here: 56.3 us
  blocking collectives  27.7 us (49%)
  starting transfers between devices  14.1 us (25%)
  Pallas kernels  10.2 us (18%)
  waiting for transfers between devices  2.85 us (5%)
  between operations  1.44 us (3%)
    all_to_all x1, blocking collectives, on_device(): got = lax.all_to_all(sent, ('section', 'pix'), 0, 0, tiled=True)  27.7 us
    ppermute x6, starting transfers between devices, hop(): return lax.ppermute(comp, ('section', 'pix'), pairs)  10.2 us
    pallas_call x2, Pallas kernels, prepare(): pl.pallas_call(functools.partial(prepare_kernel, stack, first), out_shape...  4.69 us
    pallas_call x1, Pallas kernels, on_device(): pl.pallas_call(functools.partial(finish_kernel, sections, stack), out_sha...  2.99 us
    ppermute x3, starting transfers between devices, on_device(): folds.append(lax.ppermute(folded, ('section', 'pix'), pairs))  2.65 us
    pallas_call x1, Pallas kernels, on_device(): pl.pallas_call(own_kernel, out_shape=made[:2] + [f32(2 * rows, pixels + r...  2.04 us
    ppermute x3, waiting for transfers between devices, on_device(): folds.append(lax.ppermute(folded, ('section', 'pix'), pairs))  1.72 us
    ppermute x2, starting transfers between devices, swap(): return lax.ppermute(sent, 'pix', pairs)  1.21 us
  transfers between devices with their start and end apart: 11, of which 3 were waited for; matrix products, arithmetic and copies ran while one was open for 0% of the time, Pallas kernels for 4%

profile of v9, /device:TPU:0, one launch (start us, length us, event | category | flops | bytes accessed | tf_op | source)
XLA Modules:
  0.0 56.3 jit_solution(7225735176826940480)
XLA Ops:
  0.6 0.6 collective-permute-start
  1.2 0.7 %collective-permute-start.1 = (f32[50,2,256]{2,1,0:T(2,128)}, f32[50,2,256]{2,1,0:T(2,128)S(1)}, u32[]{:S(2)}, u32[]{:S(2)}) collective-permute-start(f32[50,2,256]{2,1,0:T(2,128)} %bitcast.5), channel_id=1, source_target_pairs={{1,2},{3,4},{5,6},{2,1},{4,3},{6,5},{9,10},{11,12},{13,14},{10,9},... | collective-permute-start | bytes 307208 | tf_op jit(solution)/shard_map/ppermute | solution.py:653
  1.9 0.5 collective-permute-done.near_ref
  2.3 2.0 %own.1 = (f32[15,56,256]{2,1,0:T(8,128)S(1)}, f32[15,56,256]{2,1,0:T(8,128)S(1)}, f32[112,512]{1,0:T(8,128)S(1)}, s32[15,256]{1,0:T(8,128)S(1)}) custom-call(s32[15,256]{1,0:T(8,128)} %idx_hbm.1, f32[50,2,256]{2,1,0:T(2,128)} %bitcast.6, f32[50,2,256]{2,1,0:T(2,128)S(1)} %collective-permute-done.near_ref), custom_call_target="tpu_custom_call" | custom-call | flops 880803840 | tf_op jit(solution)/shard_map/own/pallas_call | solution.py:663
  4.4 0.0 collective-permute-done.1.far_ref
  4.4 4.7 %shard_map.50 = (f32[15,56,256]{2,1,0:T(8,128)S(1)}, f32[15,56,256]{2,1,0:T(8,128)S(1)}, f32[16,2,16,128]{3,2,1,0:T(8,128)S(1)}, f32[16,2,16,128]{3,2,1,0:T(8,12...) custom-call(s32[15,256]{1,0:T(8,128)S(1)} %get-tuple-element.36.idx_, ...), custom_call_target="tpu_custom_call", output_to_operand_aliasing={{0}: (3, {}), {1}: (4, {})} | custom-call | flops 33030144000 | tf_op jit(solution)/shard_map/pallas_call | solution.py:682
  9.1 0.7 %collective-permute-start.10 = (f32[544,128]{1,0:T(8,128)S(1)}, f32[544,128]{1,0:T(8,128)S(1)}, u32[]{:S(2)}, u32[]{:S(2)}) collective-permute-start(f32[544,128]{1,0:T(8,128)S(1)} %get-tuple-element.67.refs_3_), channel_id=1, source_target_pairs={{24,16},{25,17},{26,18},{27,19},{28,20},{29,21},{30,22},{31,23}} | collective-permute-start | bytes 835592 | tf_op jit(solution)/shard_map/ppermute | solution.py:705
  9.8 1.3 %collective-permute-start.8 = (f32[544,128]{1,0:T(8,128)S(1)}, f32[544,128]{1,0:T(8,128)S(1)}, u32[]{:S(2)}, u32[]{:S(2)}) collective-permute-start(f32[544,128]{1,0:T(8,128)S(1)} %get-tuple-element.67.refs_3_), channel_id=1, source_target_pairs={{24,0},{25,1},{26,2},{27,3},{28,4},{29,5},{30,6},{31,7}} | collective-permute-start | bytes 835592 | tf_op jit(solution)/shard_map/ppermute | solution.py:705
  11.1 0.7 %collective-permute-start.9 = (f32[544,128]{1,0:T(8,128)S(1)}, f32[544,128]{1,0:T(8,128)S(1)}, u32[]{:S(2)}, u32[]{:S(2)}) collective-permute-start(f32[544,128]{1,0:T(8,128)S(1)} %get-tuple-element.67.refs_3_), channel_id=1, source_target_pairs={{24,8},{25,9},{26,10},{27,11},{28,12},{29,13},{30,14},{31,15}} | collective-permute-start | bytes 835592 | tf_op jit(solution)/shard_map/ppermute | solution.py:705
  11.8 6.3 %collective-permute-start.2 = (f32[2,256]{1,0:T(2,128)S(1)}, f32[2,256]{1,0:T(2,128)S(1)}, u32[]{:S(2)}, u32[]{:S(2)}) collective-permute-start(f32[2,256]{1,0:T(2,128)S(1)} %get-tuple-element.40), channel_id=1, source_target_pairs={{0,9},{1,10},{2,11},{3,12},{4,13},{5,14},{6,15}} | collective-permute-start | bytes 6152 | tf_op jit(solution)/shard_map/ppermute | solution.py:715
  18.1 1.3 %collective-permute-start.3 = (f32[2,256]{1,0:T(2,128)S(1)}, f32[2,256]{1,0:T(2,128)S(1)}, u32[]{:S(2)}, u32[]{:S(2)}) collective-permute-start(f32[2,256]{1,0:T(2,128)S(1)} %get-tuple-element.40), channel_id=1, source_target_pairs={{0,8},{1,9},{2,10},{3,11},{4,12},{5,13},{6,14},{7,15}} | collective-permute-start | bytes 6152 | tf_op jit(solution)/shard_map/ppermute | solution.py:715
  19.4 0.0 collective-permute-done.2.low_ref
  19.4 0.7 %collective-permute-start.4 = (f32[2,256]{1,0:T(2,128)S(1)}, f32[2,256]{1,0:T(2,128)S(1)}, u32[]{:S(2)}, u32[]{:S(2)}) collective-permute-start(f32[2,256]{1,0:T(2,128)S(1)} %get-tuple-element.40), channel_id=1, source_target_pairs={{1,8},{2,9},{3,10},{4,11},{5,12},{6,13},{7,14}} | collective-permute-start | bytes 6152 | tf_op jit(solution)/shard_map/ppermute | solution.py:715
  20.1 0.6 %collective-permute-done.3.own_ref = f32[2,256]{1,0:T(2,128)S(1)} collective-permute-done((f32[2,256]{1,0:T(2,128)S(1)}, f32[2,256]{1,0:T(2,128)S(1)}, u32[]{:S(2)}, u32[]{:S(2)}) %collective-permute-start.3) | collective-permute-done | bytes 2080 | tf_op jit(solution)/shard_map/ppermute | solution.py:715
  20.7 0.0 collective-permute-done.4.high_ref
  20.7 0.7 %collective-permute-start.5 = (f32[2,256]{1,0:T(2,128)S(1)}, f32[2,256]{1,0:T(2,128)S(1)}, u32[]{:S(2)}, u32[]{:S(2)}) collective-permute-start(f32[2,256]{1,0:T(2,128)S(1)} %get-tuple-element.53), channel_id=1, source_target_pairs={{8,17},{9,18},{10,19},{11,20},{12,21},{13,22},{14,23}} | collective-permute-start | bytes 6152 | tf_op jit(solution)/shard_map/ppermute | solution.py:715
  21.4 0.7 %collective-permute-start.6 = (f32[2,256]{1,0:T(2,128)S(1)}, f32[2,256]{1,0:T(2,128)S(1)}, u32[]{:S(2)}, u32[]{:S(2)}) collective-permute-start(f32[2,256]{1,0:T(2,128)S(1)} %get-tuple-element.53), channel_id=1, source_target_pairs={{8,16},{9,17},{10,18},{11,19},{12,20},{13,21},{14,22},{15,23}} | collective-permute-start | bytes 6152 | tf_op jit(solution)/shard_map/ppermute | solution.py:715
  22.0 0.0 collective-permute-done.5.low_ref
  22.0 0.7 %collective-permute-start.7 = (f32[2,256]{1,0:T(2,128)S(1)}, f32[2,256]{1,0:T(2,128)S(1)}, u32[]{:S(2)}, u32[]{:S(2)}) collective-permute-start(f32[2,256]{1,0:T(2,128)S(1)} %get-tuple-element.53), channel_id=1, source_target_pairs={{9,16},{10,17},{11,18},{12,19},{13,20},{14,21},{15,22}} | collective-permute-start | bytes 6152 | tf_op jit(solution)/shard_map/ppermute | solution.py:715
  23.4 0.0 collective-permute-done.6.own_ref
  23.4 0.0 collective-permute-done.7.high_ref
  23.4 0.5 shard_map.53
  23.9 0.0 collective-permute-done.10.refs_2_
  23.9 1.7 %collective-permute-done.8.refs_0_ = f32[544,128]{1,0:T(8,128)S(1)} collective-permute-done((f32[544,128]{1,0:T(8,128)S(1)}, f32[544,128]{1,0:T(8,128)S(1)}, u32[]{:S(2)}, u32[]{:S(2)}) %collective-permute-start.8) | collective-permute-done | bytes 278560 | tf_op jit(solution)/shard_map/ppermute | solution.py:705
  25.6 0.0 collective-permute-done.9.refs_1_
  25.6 27.7 %all_to_all.5.got_ref = f32[32,16,128]{2,1,0:T(8,128)S(1)} all-to-all(f32[32,16,128]{2,1,0:T(8,128)S(1)} %get-tuple-element.61), channel_id=1, replica_groups=mesh['section'=4,'pix'=8] {'section','pix'}, dimensions={0} | all-to-all | bytes 524288 | tf_op jit(solution)/shard_map/all_to_all | solution.py:743
  53.3 3.0 %finish.1 = (f32[50,2,256]{2,1,0:T(2,128)}, f32[2,1,256]{2,1,0:T(1,128)}) custom-call(s32[8,128]{1,0:T(8,128)S(1)} %broadcast_in_dim.3.refs_0_.pixel_ref, s32[15,256]{1,0:T(8,128)S(1)} %get-tuple-element.36.idx_ref, f32[32,16,128]{2,1,0:T(8,128)S(1)} %all_to_all.5.got_ref, f32[2,50,256]{2,1,0:T(8,128)S(1)} %get-tuple-element.62.vec0_ref, ...), custom_call_target="tpu_custom_call" | custom-call | tf_op jit(solution)/shard_map/finish/pallas_call | solution.py:744
  (3 shorter events, 0.0 us)
Async XLA Ops:
  0.6 1.7 %collective-permute-start = (f32[50,2,256]{2,1,0:T(2,128)}, f32[50,2,256]{2,1,0:T(2,128)S(1)}, u32[]{:S(2)}, u32[]{:S(2)}) collective-permute-start(f32[50,2,256]{2,1,0:T(2,128)} %bitcast.4), channel_id=1, source_target_pairs={{0,1},{2,3},{4,5},{6,7},{1,0},{3,2},{5,4},{7,6},{8,9},{10,11},{12,... | collective-permute-start | bytes 307208 | tf_op jit(solution)/shard_map/ppermute | solution.py:653
  1.2 3.2 %collective-permute-start.1 = (f32[50,2,256]{2,1,0:T(2,128)}, f32[50,2,256]{2,1,0:T(2,128)S(1)}, u32[]{:S(2)}, u32[]{:S(2)}) collective-permute-start(f32[50,2,256]{2,1,0:T(2,128)} %bitcast.5), channel_id=1, source_target_pairs={{1,2},{3,4},{5,6},{2,1},{4,3},{6,5},{9,10},{11,12},{13,14},{10,9},... | collective-permute-start | bytes 307208 | tf_op jit(solution)/shard_map/ppermute | solution.py:653
  9.1 14.8 %collective-permute-start.10 = (f32[544,128]{1,0:T(8,128)S(1)}, f32[544,128]{1,0:T(8,128)S(1)}, u32[]{:S(2)}, u32[]{:S(2)}) collective-permute-start(f32[544,128]{1,0:T(8,128)S(1)} %get-tuple-element.67.refs_3_), channel_id=1, source_target_pairs={{24,16},{25,17},{26,18},{27,19},{28,20},{29,21},{30,22},{31,23}} | collective-permute-start | bytes 835592 | tf_op jit(solution)/shard_map/ppermute | solution.py:705
  9.8 15.8 %collective-permute-start.8 = (f32[544,128]{1,0:T(8,128)S(1)}, f32[544,128]{1,0:T(8,128)S(1)}, u32[]{:S(2)}, u32[]{:S(2)}) collective-permute-start(f32[544,128]{1,0:T(8,128)S(1)} %get-tuple-element.67.refs_3_), channel_id=1, source_target_pairs={{24,0},{25,1},{26,2},{27,3},{28,4},{29,5},{30,6},{31,7}} | collective-permute-start | bytes 835592 | tf_op jit(solution)/shard_map/ppermute | solution.py:705
  11.1 14.5 %collective-permute-start.9 = (f32[544,128]{1,0:T(8,128)S(1)}, f32[544,128]{1,0:T(8,128)S(1)}, u32[]{:S(2)}, u32[]{:S(2)}) collective-permute-start(f32[544,128]{1,0:T(8,128)S(1)} %get-tuple-element.67.refs_3_), channel_id=1, source_target_pairs={{24,8},{25,9},{26,10},{27,11},{28,12},{29,13},{30,14},{31,15}} | collective-permute-start | bytes 835592 | tf_op jit(solution)/shard_map/ppermute | solution.py:705
  11.8 7.6 %collective-permute-start.2 = (f32[2,256]{1,0:T(2,128)S(1)}, f32[2,256]{1,0:T(2,128)S(1)}, u32[]{:S(2)}, u32[]{:S(2)}) collective-permute-start(f32[2,256]{1,0:T(2,128)S(1)} %get-tuple-element.40), channel_id=1, source_target_pairs={{0,9},{1,10},{2,11},{3,12},{4,13},{5,14},{6,15}} | collective-permute-start | bytes 6152 | tf_op jit(solution)/shard_map/ppermute | solution.py:715
  18.1 2.6 %collective-permute-start.3 = (f32[2,256]{1,0:T(2,128)S(1)}, f32[2,256]{1,0:T(2,128)S(1)}, u32[]{:S(2)}, u32[]{:S(2)}) collective-permute-start(f32[2,256]{1,0:T(2,128)S(1)} %get-tuple-element.40), channel_id=1, source_target_pairs={{0,8},{1,9},{2,10},{3,11},{4,12},{5,13},{6,14},{7,15}} | collective-permute-start | bytes 6152 | tf_op jit(solution)/shard_map/ppermute | solution.py:715
  19.4 1.3 %collective-permute-start.4 = (f32[2,256]{1,0:T(2,128)S(1)}, f32[2,256]{1,0:T(2,128)S(1)}, u32[]{:S(2)}, u32[]{:S(2)}) collective-permute-start(f32[2,256]{1,0:T(2,128)S(1)} %get-tuple-element.40), channel_id=1, source_target_pairs={{1,8},{2,9},{3,10},{4,11},{5,12},{6,13},{7,14}} | collective-permute-start | bytes 6152 | tf_op jit(solution)/shard_map/ppermute | solution.py:715
  20.7 1.3 %collective-permute-start.5 = (f32[2,256]{1,0:T(2,128)S(1)}, f32[2,256]{1,0:T(2,128)S(1)}, u32[]{:S(2)}, u32[]{:S(2)}) collective-permute-start(f32[2,256]{1,0:T(2,128)S(1)} %get-tuple-element.53), channel_id=1, source_target_pairs={{8,17},{9,18},{10,19},{11,20},{12,21},{13,22},{14,23}} | collective-permute-start | bytes 6152 | tf_op jit(solution)/shard_map/ppermute | solution.py:715
  21.4 2.0 %collective-permute-start.6 = (f32[2,256]{1,0:T(2,128)S(1)}, f32[2,256]{1,0:T(2,128)S(1)}, u32[]{:S(2)}, u32[]{:S(2)}) collective-permute-start(f32[2,256]{1,0:T(2,128)S(1)} %get-tuple-element.53), channel_id=1, source_target_pairs={{8,16},{9,17},{10,18},{11,19},{12,20},{13,21},{14,22},{15,23}} | collective-permute-start | bytes 6152 | tf_op jit(solution)/shard_map/ppermute | solution.py:715
  22.0 1.3 %collective-permute-start.7 = (f32[2,256]{1,0:T(2,128)S(1)}, f32[2,256]{1,0:T(2,128)S(1)}, u32[]{:S(2)}, u32[]{:S(2)}) collective-permute-start(f32[2,256]{1,0:T(2,128)S(1)} %get-tuple-element.53), channel_id=1, source_target_pairs={{9,16},{10,17},{11,18},{12,19},{13,20},{14,21},{15,22}} | collective-permute-start | bytes 6152 | tf_op jit(solution)/shard_map/ppermute | solution.py:715

commit v10 on v9

--- a/solution.py
+++ b/solution.py
@@ -396,7 +396,7 @@
 ):
     last = len(refs) > 6
     if last:
-        late, (comp_ref, *made), refs = refs[:3], refs[3:6], refs[6:]
+        late, (comp_ref, *made), refs = refs[:5], refs[5:8], refs[8:]
         fr_ref, fs_ref, fd_ref, beta_ref, state_ref = refs
     else:
         beta_ref, state_ref, comp_ref, fr_ref, fs_ref, fd_ref = refs
@@ -422,11 +422,24 @@
 
     comp_ref[...] = state_ref[0:2]
     if last:
-        vectors(*late, idx_ref, gr_ref, gi_ref, sum_ref, beta_ref, state_ref, *made)
+        vectors(*late, beta_ref, state_ref, *made)
 
 
 def slot_rows(halves):
-    return max(up(4 * halves + 1, SUB), KP)
+    return max(up(4 * halves, SUB), KP // 2)
+
+
+def tile_kernel(pixel_ref, idx_ref, zr_ref, zi_ref, gr_ref, gi_ref, sum_ref, tile_ref):
+    section, _, _, start, _, _ = seat(zr_ref.shape[2], 0)
+    final = lax.axis_size("section") - 1
+
+    @pl.when(section == final)
+    def _():
+        tile_ref[...] = make_tile(start, pixel_ref, idx_ref, zr_ref, zi_ref, gr_ref, gi_ref, sum_ref)
+
+    @pl.when(section != final)
+    def _():
+        tile_ref[...] = jnp.zeros_like(tile_ref)
 
 
 def make_vectors(zr_ref, zi_ref, beta_ref, state_ref, vec_ref):
@@ -452,10 +465,10 @@
     return out
 
 
-def vectors(pixel_ref, zr_ref, zi_ref, idx_ref, gr_ref, gi_ref, sum_ref, beta_ref, state_ref, vec_ref, slot_ref):
+def vectors(pixel_ref, zr_ref, zi_ref, tile_ref, other_ref, beta_ref, state_ref, vec_ref, slot_ref):
     _, rows, pixels = zr_ref.shape
     halves = pixels // LANES
-    section, _, _, start, _, _ = seat(pixels, 0)
+    section, block, blocks, start, _, _ = seat(pixels, 0)
 
     @pl.when(section < lax.axis_size("section") - 1)
     def _():
@@ -470,7 +483,9 @@
                 turned = jnp.transpose(jnp.concatenate([vecs[c][h], empty], axis=0))
                 for r in range(0, LANES, SUB):
                     at_pixel[c] = at_pixel[c] + jnp.where(row == local - (h * LANES + r), turned[r : r + SUB], 0.0)
-        slot = [state_ref[c : c + 1, half(h)] for c in range(4) for h in range(halves)]
+        virtual, f_rows = (
+            [state_ref[c : c + 1, half(h)] for c in cs for h in range(halves)] for cs in ((0, 1), (2, 3))
+        )
         mixed = colsum(at_pixel[0]) + pltpu.roll(jnp.broadcast_to(colsum(at_pixel[1]), (SUB, LANES)), LANES // 2, 1)[0:1]
         for c in range(2):
             picked = jnp.zeros((1, LANES), jnp.float32)
@@ -478,17 +493,21 @@
                 picked = picked + jnp.where((lane == local - h * LANES)[0:1], state_ref[2 + c : 3 + c, half(h)], 0.0)
             f = jnp.sum(picked, axis=1, keepdims=True)
             mixed = jnp.where(lane[0:1] == LANES - 2 + c, jnp.broadcast_to(f, (1, LANES)), mixed)
-        slot.append(mixed)
-        slot.append(jnp.zeros((slot_ref.shape[1] - len(slot), LANES), jnp.float32))
-        slot = jnp.concatenate(slot, axis=0)
+        spare = slot_ref.shape[1] - 2 * halves
+        kinds = []
+        for more in (f_rows, [mixed]):
+            empty = [jnp.zeros((1, LANES), jnp.float32)] * (spare - len(more))
+            kinds.append(jnp.concatenate(virtual + more + empty, axis=0))
         for n in range(slot_ref.shape[0]):
-            slot_ref[n] = slot
+            with_f = jnp.logical_and(block == n % blocks, n // blocks < section)
+            slot_ref[n] = jnp.where(with_f, *kinds)
 
     @pl.when(section == lax.axis_size("section") - 1)
     def _():
-        tile = make_tile(start, pixel_ref, idx_ref, zr_ref, zi_ref, gr_ref, gi_ref, sum_ref)
+        tile = tile_ref[...] + other_ref[...]
+        tile = jnp.where(block % 2 == 0, tile[0 : KP // 2], tile[KP // 2 :])
         for n in range(slot_ref.shape[0]):
-            slot_ref[n, 0:KP] = tile
+            slot_ref[n, 0 : KP // 2] = tile
 
 
 def unfold(fold, l, h, k_row, count):
@@ -517,9 +536,10 @@
         def _(s=s):
             fold_ref[...] = folds[s][...]
 
-    tile = got_ref[final * blocks, 0:KP]
-    for q in range(1, blocks):
-        tile = tile + got_ref[final * blocks + q, 0:KP]
+    tile = [got_ref[final * blocks + q, 0 : KP // 2] for q in range(2)]
+    for q in range(2, blocks):
+        tile[q % 2] = tile[q % 2] + got_ref[final * blocks + q, 0 : KP // 2]
+    tile = jnp.concatenate(tile, axis=0)
     k_row = lax.broadcasted_iota(jnp.int32, (KP, LANES), 0)
     lane = lax.broadcasted_iota(jnp.int32, (KP, LANES), 1)
     turned = jnp.transpose(jnp.concatenate([tile, jnp.zeros((LANES - KP, LANES), jnp.float32)], axis=0))[0:KP]
@@ -576,12 +596,13 @@
     for c in range(2):
         small_ref[c] = jnp.where(is_final, state_ref[c : c + 1, 0:pixels], comp0_ref[c : c + 1])
 
-    def of_pixel(s):
+    def of_pixel(s, later):
         total = jnp.zeros((1, LANES), jnp.float32)
         for q in range(blocks):
             first = pixel_ref[0:1] - q * pixels
             here = jnp.logical_and(first >= 0, first < pixels)
-            total = total + jnp.where(here, got_ref[s * blocks + q, 4 * halves : 4 * halves + 1], 0.0)
+            here = jnp.logical_and(here, jnp.logical_not(jnp.logical_and(later, mine == q)))
+            total = total + jnp.where(here, got_ref[s * blocks + q, 2 * halves : 2 * halves + 1], 0.0)
         return total
 
     def times(d, later, fr, fi):
@@ -596,10 +617,15 @@
     for s in range(final - 1, 0, -1):
         later = section < s
         own = [got_ref[s * blocks + mine, 2 * halves + m : 2 * halves + m + 1] for m in range(2 * halves)]
-        row = of_pixel(s)
+        row = of_pixel(s, later)
         for h in range(halves):
             datum[h] = times(datum[h], later, own[h], own[halves + h])
-        f = [jnp.sum(jnp.where(lane[0:1] == LANES - 2 + c, row, 0.0), axis=1, keepdims=True) for c in range(2)]
+        f = []
+        for c in range(2):
+            total = jnp.where(lane[0:1] == LANES - 2 + c, row, 0.0)
+            for h in range(halves):
+                total = total + jnp.where(lane[0:1] == pixel_ref[0:1] - start - h * LANES, own[c * halves + h], 0.0)
+            f.append(jnp.sum(total, axis=1, keepdims=True))
         datum[halves] = times(datum[halves], later, *[jnp.broadcast_to(x, (1, LANES)) for x in f])
 
     zr = pltpu.roll(tile, LANES - Z_LANE, 1)
@@ -608,7 +634,7 @@
     zr, zi = jnp.where(k_row < count, zr, 0.0), jnp.where(k_row < count, zi, 0.0)
     last_r = state_ref[4:5, half(halves)] + colsum(zr * br - zi * bi)
     last_i = colsum(zr * bi + zi * br)
-    row = of_pixel(jnp.minimum(section, final - 1))
+    row = of_pixel(jnp.minimum(section, final - 1), False)
     vr = jnp.where(is_final, last_r, row)
     vi = jnp.where(is_final, last_i, pltpu.roll(jnp.broadcast_to(row, (SUB, LANES)), LANES // 2, 1)[0:1])
     dr, di = datum[halves]
@@ -715,7 +741,7 @@
             return lax.ppermute(comp, ("section", "pix"), pairs)
 
         last = rnd == final - 1
-        late = (pixel, zr, zi) if last else ()
+        late = (pixel, zr, zi, tile, other) if last else ()
         scratch = [pltpu.VMEM((count, halves, KP, LANES), jnp.float32)] * 3
         outs = [f32(2, halves, KP, LANES), f32(SUB, pixels), f32(2, pixels)]
         if last:
@@ -738,6 +764,16 @@
         if rnd == 1:
             pixel = lax.optimization_barrier((reference_pixel, comp))[0][0]
             pixel = jnp.full((SUB, LANES), pixel, jnp.int32)
+            tile = pl.pallas_call(
+                tile_kernel,
+                out_shape=f32(KP, LANES),
+                in_specs=[VMEM] * 7,
+                out_specs=VMEM,
+                compiler_params=params(),
+                name="tile",
+            )(pixel, neighbours, zr, zi, gr, gi, sums)
+            pairs = [(final * blocks + q, final * blocks + (q ^ 1)) for q in range(blocks)]
+            other = lax.ppermute(tile, ("section", "pix"), pairs)
 
     sent, *folds = lax.optimization_barrier((sent, *folds))
     got = lax.all_to_all(sent, ("section", "pix"), 0, 0, tiled=True)

time: 56.8 us -> 61.2 us (1.077)
  blocking collectives: 27.7 us -> 30.9 us
  starting transfers between devices: 14.1 us -> 14.8 us
    all_to_all x1, blocking collectives: 27.7 us -> 30.9 us  [on_device(): got = lax.all_to_all(sent, ('section', 'pix'), 0, 0, tiled=True)]
    ppermute x3, waiting for transfers between devices: 1.72 us -> 2.86 us  [on_device(): folds.append(lax.ppermute(folded, ('section', 'pix'), pairs))]
    ppermute x0 -> x1, starting transfers between devices: none -> 0.66 us  [on_device(): other = lax.ppermute(tile, ('section', 'pix'), pairs)]
  transfers between devices with their start and end apart: 11 -> 12, of which waited for: 3 -> 2; matrix products, arithmetic and copies ran while one was open for 0% -> 0% of each run, Pallas kernels for 4% -> 4%
where the time goes in v10:
time: 61.2 us; the launch traced here: 60.9 us
  blocking collectives  30.9 us (50%)
  starting transfers between devices  14.8 us (24%)
  Pallas kernels  10.3 us (17%)
  waiting for transfers between devices  3.37 us (6%)
  between operations  1.5 us (2%)
    all_to_all x1, blocking collectives, on_device(): got = lax.all_to_all(sent, ('section', 'pix'), 0, 0, tiled=True)  30.9 us
    ppermute x6, starting transfers between devices, hop(): return lax.ppermute(comp, ('section', 'pix'), pairs)  10.2 us
    pallas_call x2, Pallas kernels, prepare(): pl.pallas_call(functools.partial(prepare_kernel, stack, first), out_shape...  4.7 us
    pallas_call x1, Pallas kernels, on_device(): pl.pallas_call(functools.partial(finish_kernel, sections, stack), out_sha...  3.02 us
    ppermute x3, waiting for transfers between devices, on_device(): folds.append(lax.ppermute(folded, ('section', 'pix'), pairs))  2.86 us
    ppermute x3, starting transfers between devices, on_device(): folds.append(lax.ppermute(folded, ('section', 'pix'), pairs))  2.65 us
    pallas_call x1, Pallas kernels, on_device(): pl.pallas_call(own_kernel, out_shape=made[:2] + [f32(2 * rows, pixels + r...  2.04 us
  transfers between devices with their start and end apart: 12, of which 2 were waited for; matrix products, arithmetic and copies ran while one was open for 0% of the time, Pallas kernels for 4%

profile of v10, /device:TPU:0, one launch (start us, length us, event | category | flops | bytes accessed | tf_op | source)
XLA Modules:
  0.0 60.9 jit_solution(6082347277553921894)
XLA Ops:
  0.6 0.6 collective-permute-start
  1.2 0.7 %collective-permute-start.1 = (f32[50,2,256]{2,1,0:T(2,128)}, f32[50,2,256]{2,1,0:T(2,128)S(1)}, u32[]{:S(2)}, u32[]{:S(2)}) collective-permute-start(f32[50,2,256]{2,1,0:T(2,128)} %bitcast.5), channel_id=1, source_target_pairs={{1,2},{3,4},{5,6},{2,1},{4,3},{6,5},{9,10},{11,12},{13,14},{10,9},... | collective-permute-start | bytes 307208 | tf_op jit(solution)/shard_map/ppermute | solution.py:679
  1.9 0.5 collective-permute-done.near_ref
  2.3 2.0 %own.1 = (f32[15,56,256]{2,1,0:T(8,128)S(1)}, f32[15,56,256]{2,1,0:T(8,128)S(1)}, f32[112,512]{1,0:T(8,128)S(1)}, s32[15,256]{1,0:T(8,128)S(1)}) custom-call(s32[15,256]{1,0:T(8,128)} %idx_hbm.1, f32[50,2,256]{2,1,0:T(2,128)} %bitcast.6, f32[50,2,256]{2,1,0:T(2,128)S(1)} %collective-permute-done.near_ref), custom_call_target="tpu_custom_call" | custom-call | flops 880803840 | tf_op jit(solution)/shard_map/own/pallas_call | solution.py:689
  4.4 0.0 collective-permute-done.1.far_ref
  4.4 4.7 %shard_map.50 = (f32[15,56,256]{2,1,0:T(8,128)S(1)}, f32[15,56,256]{2,1,0:T(8,128)S(1)}, f32[16,2,16,128]{3,2,1,0:T(8,128)S(1)}, f32[16,2,16,128]{3,2,1,0:T(8,12...) custom-call(s32[15,256]{1,0:T(8,128)S(1)} %get-tuple-element.36.idx_, ...), custom_call_target="tpu_custom_call", output_to_operand_aliasing={{0}: (3, {}), {1}: (4, {})} | custom-call | flops 33030144000 | tf_op jit(solution)/shard_map/pallas_call | solution.py:708
  9.1 0.7 %collective-permute-start.10 = (f32[544,128]{1,0:T(8,128)S(1)}, f32[544,128]{1,0:T(8,128)S(1)}, u32[]{:S(2)}, u32[]{:S(2)}) collective-permute-start(f32[544,128]{1,0:T(8,128)S(1)} %get-tuple-element.67.refs_3_), channel_id=1, source_target_pairs={{24,8},{25,9},{26,10},{27,11},{28,12},{29,13},{30,14},{31,15}} | collective-permute-start | bytes 835592 | tf_op jit(solution)/shard_map/ppermute | solution.py:731
  9.8 0.7 %collective-permute-start.11 = (f32[544,128]{1,0:T(8,128)S(1)}, f32[544,128]{1,0:T(8,128)S(1)}, u32[]{:S(2)}, u32[]{:S(2)}) collective-permute-start(f32[544,128]{1,0:T(8,128)S(1)} %get-tuple-element.67.refs_3_), channel_id=1, source_target_pairs={{24,16},{25,17},{26,18},{27,19},{28,20},{29,21},{30,22},{31,23}} | collective-permute-start | bytes 835592 | tf_op jit(solution)/shard_map/ppermute | solution.py:731
  10.5 1.3 %collective-permute-start.9 = (f32[544,128]{1,0:T(8,128)S(1)}, f32[544,128]{1,0:T(8,128)S(1)}, u32[]{:S(2)}, u32[]{:S(2)}) collective-permute-start(f32[544,128]{1,0:T(8,128)S(1)} %get-tuple-element.67.refs_3_), channel_id=1, source_target_pairs={{24,0},{25,1},{26,2},{27,3},{28,4},{29,5},{30,6},{31,7}} | collective-permute-start | bytes 835592 | tf_op jit(solution)/shard_map/ppermute | solution.py:731
  11.8 6.3 %collective-permute-start.2 = (f32[2,256]{1,0:T(2,128)S(1)}, f32[2,256]{1,0:T(2,128)S(1)}, u32[]{:S(2)}, u32[]{:S(2)}) collective-permute-start(f32[2,256]{1,0:T(2,128)S(1)} %get-tuple-element.40), channel_id=1, source_target_pairs={{0,9},{1,10},{2,11},{3,12},{4,13},{5,14},{6,15}} | collective-permute-start | bytes 6152 | tf_op jit(solution)/shard_map/ppermute | solution.py:741
  18.1 1.3 %collective-permute-start.3 = (f32[2,256]{1,0:T(2,128)S(1)}, f32[2,256]{1,0:T(2,128)S(1)}, u32[]{:S(2)}, u32[]{:S(2)}) collective-permute-start(f32[2,256]{1,0:T(2,128)S(1)} %get-tuple-element.40), channel_id=1, source_target_pairs={{0,8},{1,9},{2,10},{3,11},{4,12},{5,13},{6,14},{7,15}} | collective-permute-start | bytes 6152 | tf_op jit(solution)/shard_map/ppermute | solution.py:741
  20.1 0.0 collective-permute-done.2.low_ref
  20.1 0.7 %collective-permute-start.4 = (f32[2,256]{1,0:T(2,128)S(1)}, f32[2,256]{1,0:T(2,128)S(1)}, u32[]{:S(2)}, u32[]{:S(2)}) collective-permute-start(f32[2,256]{1,0:T(2,128)S(1)} %get-tuple-element.40), channel_id=1, source_target_pairs={{1,8},{2,9},{3,10},{4,11},{5,12},{6,13},{7,14}} | collective-permute-start | bytes 6152 | tf_op jit(solution)/shard_map/ppermute | solution.py:741
  20.8 0.0 collective-permute-done.3.own_ref
  20.8 0.7 %collective-permute-start.8 = (f32[16,128]{1,0:T(8,128)S(1)}, f32[16,128]{1,0:T(8,128)S(1)}, u32[]{:S(2)}, u32[]{:S(2)}) collective-permute-start(f32[16,128]{1,0:T(8,128)S(1)} %tile.1.refs_3_), channel_id=1, source_target_pairs={{24,25},{25,24},{26,27},{27,26},{28,29},{29,28},{30,31},{31,30}} | collective-permute-start | bytes 24584 | tf_op jit(solution)/shard_map/ppermute | solution.py:776
  21.5 0.0 collective-permute-done.4.high_ref
  21.5 0.7 %collective-permute-start.5 = (f32[2,256]{1,0:T(2,128)S(1)}, f32[2,256]{1,0:T(2,128)S(1)}, u32[]{:S(2)}, u32[]{:S(2)}) collective-permute-start(f32[2,256]{1,0:T(2,128)S(1)} %get-tuple-element.53), channel_id=1, source_target_pairs={{8,17},{9,18},{10,19},{11,20},{12,21},{13,22},{14,23}} | collective-permute-start | bytes 6152 | tf_op jit(solution)/shard_map/ppermute | solution.py:741
  22.2 0.0 collective-permute-done.5.low_ref
  22.2 0.7 %collective-permute-start.6 = (f32[2,256]{1,0:T(2,128)S(1)}, f32[2,256]{1,0:T(2,128)S(1)}, u32[]{:S(2)}, u32[]{:S(2)}) collective-permute-start(f32[2,256]{1,0:T(2,128)S(1)} %get-tuple-element.53), channel_id=1, source_target_pairs={{8,16},{9,17},{10,18},{11,19},{12,20},{13,21},{14,22},{15,23}} | collective-permute-start | bytes 6152 | tf_op jit(solution)/shard_map/ppermute | solution.py:741
  22.8 0.0 collective-permute-done.6.own_ref
  22.9 0.7 %collective-permute-start.7 = (f32[2,256]{1,0:T(2,128)S(1)}, f32[2,256]{1,0:T(2,128)S(1)}, u32[]{:S(2)}, u32[]{:S(2)}) collective-permute-start(f32[2,256]{1,0:T(2,128)S(1)} %get-tuple-element.53), channel_id=1, source_target_pairs={{9,16},{10,17},{11,18},{12,19},{13,20},{14,21},{15,22}} | collective-permute-start | bytes 6152 | tf_op jit(solution)/shard_map/ppermute | solution.py:741
  23.5 0.0 collective-permute-done.7.high_ref
  23.5 0.0 collective-permute-done.8.refs_4_
  23.5 0.5 shard_map.53
  24.0 0.0 collective-permute-done.10.refs_1_
  24.0 0.0 collective-permute-done.11.refs_2_
  24.1 2.9 %collective-permute-done.9.refs_0_ = f32[544,128]{1,0:T(8,128)S(1)} collective-permute-done((f32[544,128]{1,0:T(8,128)S(1)}, f32[544,128]{1,0:T(8,128)S(1)}, u32[]{:S(2)}, u32[]{:S(2)}) %collective-permute-start.9) | collective-permute-done | bytes 278560 | tf_op jit(solution)/shard_map/ppermute | solution.py:731
  26.9 30.9 %all_to_all.5.got_ref = f32[32,8,128]{2,1,0:T(8,128)S(1)} all-to-all(f32[32,8,128]{2,1,0:T(8,128)S(1)} %get-tuple-element.61), channel_id=1, replica_groups=mesh['section'=4,'pix'=8] {'section','pix'}, dimensions={0} | all-to-all | bytes 262144 | tf_op jit(solution)/shard_map/all_to_all | solution.py:779
  57.9 3.0 %finish.1 = (f32[50,2,256]{2,1,0:T(2,128)}, f32[2,1,256]{2,1,0:T(1,128)}) custom-call(s32[8,128]{1,0:T(8,128)S(1)} %broadcast_in_dim.3.pixel_ref.refs_0_, s32[15,256]{1,0:T(8,128)S(1)} %get-tuple-element.36.idx_ref, f32[32,8,128]{2,1,0:T(8,128)S(1)} %all_to_all.5.got_ref, f32[2,50,256]{2,1,0:T(8,128)S(1)} %get-tuple-element.62.vec0_ref, ...), custom_call_target="tpu_custom_call" | custom-call | tf_op jit(solution)/shard_map/finish/pallas_call | solution.py:780
  (4 shorter events, 0.1 us)
Async XLA Ops:
  0.6 1.7 %collective-permute-start = (f32[50,2,256]{2,1,0:T(2,128)}, f32[50,2,256]{2,1,0:T(2,128)S(1)}, u32[]{:S(2)}, u32[]{:S(2)}) collective-permute-start(f32[50,2,256]{2,1,0:T(2,128)} %bitcast.4), channel_id=1, source_target_pairs={{0,1},{2,3},{4,5},{6,7},{1,0},{3,2},{5,4},{7,6},{8,9},{10,11},{12,... | collective-permute-start | bytes 307208 | tf_op jit(solution)/shard_map/ppermute | solution.py:679
  1.2 3.2 %collective-permute-start.1 = (f32[50,2,256]{2,1,0:T(2,128)}, f32[50,2,256]{2,1,0:T(2,128)S(1)}, u32[]{:S(2)}, u32[]{:S(2)}) collective-permute-start(f32[50,2,256]{2,1,0:T(2,128)} %bitcast.5), channel_id=1, source_target_pairs={{1,2},{3,4},{5,6},{2,1},{4,3},{6,5},{9,10},{11,12},{13,14},{10,9},... | collective-permute-start | bytes 307208 | tf_op jit(solution)/shard_map/ppermute | solution.py:679
  9.1 14.9 %collective-permute-start.10 = (f32[544,128]{1,0:T(8,128)S(1)}, f32[544,128]{1,0:T(8,128)S(1)}, u32[]{:S(2)}, u32[]{:S(2)}) collective-permute-start(f32[544,128]{1,0:T(8,128)S(1)} %get-tuple-element.67.refs_3_), channel_id=1, source_target_pairs={{24,8},{25,9},{26,10},{27,11},{28,12},{29,13},{30,14},{31,15}} | collective-permute-start | bytes 835592 | tf_op jit(solution)/shard_map/ppermute | solution.py:731
  9.8 14.2 %collective-permute-start.11 = (f32[544,128]{1,0:T(8,128)S(1)}, f32[544,128]{1,0:T(8,128)S(1)}, u32[]{:S(2)}, u32[]{:S(2)}) collective-permute-start(f32[544,128]{1,0:T(8,128)S(1)} %get-tuple-element.67.refs_3_), channel_id=1, source_target_pairs={{24,16},{25,17},{26,18},{27,19},{28,20},{29,21},{30,22},{31,23}} | collective-permute-start | bytes 835592 | tf_op jit(solution)/shard_map/ppermute | solution.py:731
  10.5 16.4 %collective-permute-start.9 = (f32[544,128]{1,0:T(8,128)S(1)}, f32[544,128]{1,0:T(8,128)S(1)}, u32[]{:S(2)}, u32[]{:S(2)}) collective-permute-start(f32[544,128]{1,0:T(8,128)S(1)} %get-tuple-element.67.refs_3_), channel_id=1, source_target_pairs={{24,0},{25,1},{26,2},{27,3},{28,4},{29,5},{30,6},{31,7}} | collective-permute-start | bytes 835592 | tf_op jit(solution)/shard_map/ppermute | solution.py:731
  11.8 8.3 %collective-permute-start.2 = (f32[2,256]{1,0:T(2,128)S(1)}, f32[2,256]{1,0:T(2,128)S(1)}, u32[]{:S(2)}, u32[]{:S(2)}) collective-permute-start(f32[2,256]{1,0:T(2,128)S(1)} %get-tuple-element.40), channel_id=1, source_target_pairs={{0,9},{1,10},{2,11},{3,12},{4,13},{5,14},{6,15}} | collective-permute-start | bytes 6152 | tf_op jit(solution)/shard_map/ppermute | solution.py:741
  18.1 2.7 %collective-permute-start.3 = (f32[2,256]{1,0:T(2,128)S(1)}, f32[2,256]{1,0:T(2,128)S(1)}, u32[]{:S(2)}, u32[]{:S(2)}) collective-permute-start(f32[2,256]{1,0:T(2,128)S(1)} %get-tuple-element.40), channel_id=1, source_target_pairs={{0,8},{1,9},{2,10},{3,11},{4,12},{5,13},{6,14},{7,15}} | collective-permute-start | bytes 6152 | tf_op jit(solution)/shard_map/ppermute | solution.py:741
  20.1 1.4 %collective-permute-start.4 = (f32[2,256]{1,0:T(2,128)S(1)}, f32[2,256]{1,0:T(2,128)S(1)}, u32[]{:S(2)}, u32[]{:S(2)}) collective-permute-start(f32[2,256]{1,0:T(2,128)S(1)} %get-tuple-element.40), channel_id=1, source_target_pairs={{1,8},{2,9},{3,10},{4,11},{5,12},{6,13},{7,14}} | collective-permute-start | bytes 6152 | tf_op jit(solution)/shard_map/ppermute | solution.py:741
  20.8 2.7 %collective-permute-start.8 = (f32[16,128]{1,0:T(8,128)S(1)}, f32[16,128]{1,0:T(8,128)S(1)}, u32[]{:S(2)}, u32[]{:S(2)}) collective-permute-start(f32[16,128]{1,0:T(8,128)S(1)} %tile.1.refs_3_), channel_id=1, source_target_pairs={{24,25},{25,24},{26,27},{27,26},{28,29},{29,28},{30,31},{31,30}} | collective-permute-start | bytes 24584 | tf_op jit(solution)/shard_map/ppermute | solution.py:776
  21.5 0.7 %collective-permute-start.5 = (f32[2,256]{1,0:T(2,128)S(1)}, f32[2,256]{1,0:T(2,128)S(1)}, u32[]{:S(2)}, u32[]{:S(2)}) collective-permute-start(f32[2,256]{1,0:T(2,128)S(1)} %get-tuple-element.53), channel_id=1, source_target_pairs={{8,17},{9,18},{10,19},{11,20},{12,21},{13,22},{14,23}} | collective-permute-start | bytes 6152 | tf_op jit(solution)/shard_map/ppermute | solution.py:741
  22.2 0.7 %collective-permute-start.6 = (f32[2,256]{1,0:T(2,128)S(1)}, f32[2,256]{1,0:T(2,128)S(1)}, u32[]{:S(2)}, u32[]{:S(2)}) collective-permute-start(f32[2,256]{1,0:T(2,128)S(1)} %get-tuple-element.53), channel_id=1, source_target_pairs={{8,16},{9,17},{10,18},{11,19},{12,20},{13,21},{14,22},{15,23}} | collective-permute-start | bytes 6152 | tf_op jit(solution)/shard_map/ppermute | solution.py:741
  22.9 0.7 %collective-permute-start.7 = (f32[2,256]{1,0:T(2,128)S(1)}, f32[2,256]{1,0:T(2,128)S(1)}, u32[]{:S(2)}, u32[]{:S(2)}) collective-permute-start(f32[2,256]{1,0:T(2,128)S(1)} %get-tuple-element.53), channel_id=1, source_target_pairs={{9,16},{10,17},{11,18},{12,19},{13,20},{14,21},{15,22}} | collective-permute-start | bytes 6152 | tf_op jit(solution)/shard_map/ppermute | solution.py:741

commit v11 on v10

--- a/solution.py
+++ b/solution.py
@@ -268,30 +268,34 @@
 
     section, _, _, start, _, far_at = seat(zr_ref.shape[2], far_ref.shape[2])
 
-    @pl.when(section == 0 if first else section != 0)
+    final = lax.axis_size("section") - 1
+    ends = jnp.logical_or(section == 0, section == final)
+
+    @pl.when(ends if first else jnp.logical_not(ends))
     def _():
-        count = zr_ref.shape[0]
         gather(start, idx_ref, ((far_ref, far_at),), xs_ref, hl_ref, zr_ref, zi_ref, True)
         scale_dates(zr_ref, zi_ref)
         gram(pair_ref, zr_ref, zi_ref, own_ref, gr_ref, gi_ref, sum_ref)
-        if first:
-            halves = gr_ref.shape[1]
+
+    if first:
+        count, halves = gr_ref.shape[0] - 1, gr_ref.shape[1]
+        comp_ref, fold_ref, gs_ref, gd_ref = refs[7:11]
+
+        @pl.when(section == final)
+        def _():
+            fold(gr_ref, gi_ref, sum_ref, fold_ref)
+
+        @pl.when(section == 0)
+        def _():
             hr = [gr_ref[count, h] for h in range(halves)]
             hi = [gi_ref[count, h] for h in range(halves)]
             sums = [(sum_ref[0, h], sum_ref[1, h]) for h in range(halves)]
-            gs_ref, gd_ref = refs[8:10]
             for l in range(count):
                 for h in range(halves):
                     gs_ref[l, h] = gi_ref[l, h] + gr_ref[l, h]
                     gd_ref[l, h] = gi_ref[l, h] - gr_ref[l, h]
             solve(None, gr_ref.at[0:count], gs_ref, gd_ref, hr, hi, sums, stack, beta_ref, state_ref)
-            refs[7][...] = state_ref[0:2]
-
-    if not first:
-
-        @pl.when(section == lax.axis_size("section") - 1)
-        def _():
-            fold(gr_ref, gi_ref, sum_ref, refs[7])
+            comp_ref[...] = state_ref[0:2]
 
 
 def folded_column(l, h, gr_ref, gi_ref, sum_ref):
@@ -704,7 +708,7 @@
     )(*[pltpu.with_memory_space_constraint(x, pltpu.HBM) for x in (neighbours, slc)], near)
 
     def prepare(first, carried):
-        outs = made if first else made[:7] + [f32((count + 2) * halves * KP, LANES)]
+        outs = made + [f32((count + 2) * halves * KP, LANES)] if first else made[:7]
         return pl.pallas_call(
             functools.partial(prepare_kernel, stack, first),
             out_shape=outs,
@@ -721,8 +725,8 @@
             cost_estimate=cost(50 * 12 * rows * reach * pixels * count),
         )(neighbours, far, own, *carried)
 
-    *made_0, comp = prepare(True, (zr, zi))
-    zr, zi, gr, gi, sums, beta, state, folded = prepare(False, made_0)
+    *made_0, comp, folded = prepare(True, (zr, zi))
+    zr, zi, gr, gi, sums, beta, state = prepare(False, made_0)
 
     final = sections - 1
     folds = []

time: 61.2 us -> 58.6 us (0.958)
  starting transfers between devices: 14.8 us -> 11.1 us
  waiting for transfers between devices: 3.37 us -> 7.02 us
  blocking collectives: 30.9 us -> 28.4 us
    ppermute x3, waiting for transfers between devices: 2.86 us -> 6.99 us  [on_device(): folds.append(lax.ppermute(folded, ('section', 'pix'), pairs))]
    ppermute x6, starting transfers between devices: 10.2 us -> 6.54 us  [hop(): return lax.ppermute(comp, ('section', 'pix'), pairs)]
    all_to_all x1, blocking collectives: 30.9 us -> 28.4 us  [on_device(): got = lax.all_to_all(sent, ('section', 'pix'), 0, 0, tiled=True)]
  transfers between devices with their start and end apart: 12 -> 12, of which waited for: 2 -> 1; matrix products, arithmetic and copies ran while one was open for 0% -> 0% of each run, Pallas kernels for 4% -> 4%
where the time goes in v11:
time: 58.6 us; the launch traced here: 58.3 us
  blocking collectives  28.4 us (48%)
  starting transfers between devices  11.1 us (19%)
  Pallas kernels  10.3 us (18%)
  waiting for transfers between devices  7.02 us (12%)
  between operations  1.5 us (3%)
    all_to_all x1, blocking collectives, on_device(): got = lax.all_to_all(sent, ('section', 'pix'), 0, 0, tiled=True)  28.4 us
    ppermute x3, waiting for transfers between devices, on_device(): folds.append(lax.ppermute(folded, ('section', 'pix'), pairs))  6.99 us
    ppermute x6, starting transfers between devices, hop(): return lax.ppermute(comp, ('section', 'pix'), pairs)  6.54 us
    pallas_call x2, Pallas kernels, prepare(): pl.pallas_call(functools.partial(prepare_kernel, stack, first), out_shape...  4.69 us
    pallas_call x1, Pallas kernels, on_device(): pl.pallas_call(functools.partial(finish_kernel, sections, stack), out_sha...  3.02 us
    ppermute x3, starting transfers between devices, on_device(): folds.append(lax.ppermute(folded, ('section', 'pix'), pairs))  2.65 us
    pallas_call x1, Pallas kernels, on_device(): pl.pallas_call(own_kernel, out_shape=made[:2] + [f32(2 * rows, pixels + r...  2.04 us
    ppermute x2, starting transfers between devices, swap(): return lax.ppermute(sent, 'pix', pairs)  1.21 us
  transfers between devices with their start and end apart: 12, of which 1 were waited for; matrix products, arithmetic and copies ran while one was open for 0% of the time, Pallas kernels for 4%

profile of v11, /device:TPU:0, one launch (start us, length us, event | category | flops | bytes accessed | tf_op | source)
XLA Modules:
  0.0 58.3 jit_solution(5553177873093186194)
XLA Ops:
  0.6 0.6 collective-permute-start
  1.2 0.7 %collective-permute-start.1 = (f32[50,2,256]{2,1,0:T(2,128)}, f32[50,2,256]{2,1,0:T(2,128)S(1)}, u32[]{:S(2)}, u32[]{:S(2)}) collective-permute-start(f32[50,2,256]{2,1,0:T(2,128)} %bitcast.5), channel_id=1, source_target_pairs={{1,2},{3,4},{5,6},{2,1},{4,3},{6,5},{9,10},{11,12},{13,14},{10,9},... | collective-permute-start | bytes 307208 | tf_op jit(solution)/shard_map/ppermute | solution.py:683
  2.5 0.0 collective-permute-done.near_ref
  2.5 2.0 %own.1 = (f32[15,56,256]{2,1,0:T(8,128)S(1)}, f32[15,56,256]{2,1,0:T(8,128)S(1)}, f32[112,512]{1,0:T(8,128)S(1)}, s32[15,256]{1,0:T(8,128)S(1)}) custom-call(s32[15,256]{1,0:T(8,128)} %idx_hbm.1, f32[50,2,256]{2,1,0:T(2,128)} %bitcast.6, f32[50,2,256]{2,1,0:T(2,128)S(1)} %collective-permute-done.near_ref), custom_call_target="tpu_custom_call" | custom-call | flops 880803840 | tf_op jit(solution)/shard_map/own/pallas_call | solution.py:693
  4.6 0.0 collective-permute-done.1.far_ref
  4.6 4.7 %shard_map.50 = (f32[15,56,256]{2,1,0:T(8,128)S(1)}, f32[15,56,256]{2,1,0:T(8,128)S(1)}, f32[16,2,16,128]{3,2,1,0:T(8,128)S(1)}, f32[16,2,16,128]{3,2,1,0:T(8,12...) custom-call(s32[15,256]{1,0:T(8,128)S(1)} %get-tuple-element.36.idx_, ...), custom_call_target="tpu_custom_call", output_to_operand_aliasing={{0}: (3, {}), {1}: (4, {})} | custom-call | flops 33030144000 | tf_op jit(solution)/shard_map/pallas_call | solution.py:712
  9.2 2.6 %collective-permute-start.2 = (f32[2,256]{1,0:T(2,128)S(1)}, f32[2,256]{1,0:T(2,128)S(1)}, u32[]{:S(2)}, u32[]{:S(2)}) collective-permute-start(f32[2,256]{1,0:T(2,128)S(1)} %get-tuple-element.40), channel_id=1, source_target_pairs={{0,9},{1,10},{2,11},{3,12},{4,13},{5,14},{6,15}} | collective-permute-start | bytes 6152 | tf_op jit(solution)/shard_map/ppermute | solution.py:745
  11.9 1.3 %collective-permute-start.3 = (f32[2,256]{1,0:T(2,128)S(1)}, f32[2,256]{1,0:T(2,128)S(1)}, u32[]{:S(2)}, u32[]{:S(2)}) collective-permute-start(f32[2,256]{1,0:T(2,128)S(1)} %get-tuple-element.40), channel_id=1, source_target_pairs={{0,8},{1,9},{2,10},{3,11},{4,12},{5,13},{6,14},{7,15}} | collective-permute-start | bytes 6152 | tf_op jit(solution)/shard_map/ppermute | solution.py:745
  13.2 0.7 %collective-permute-start.10 = (f32[544,128]{1,0:T(8,128)S(1)}, f32[544,128]{1,0:T(8,128)S(1)}, u32[]{:S(2)}, u32[]{:S(2)}) collective-permute-start(f32[544,128]{1,0:T(8,128)S(1)} %get-tuple-element.67.refs_3_), channel_id=1, source_target_pairs={{24,8},{25,9},{26,10},{27,11},{28,12},{29,13},{30,14},{31,15}} | collective-permute-start | bytes 835592 | tf_op jit(solution)/shard_map/ppermute | solution.py:735
  13.8 0.7 %collective-permute-start.11 = (f32[544,128]{1,0:T(8,128)S(1)}, f32[544,128]{1,0:T(8,128)S(1)}, u32[]{:S(2)}, u32[]{:S(2)}) collective-permute-start(f32[544,128]{1,0:T(8,128)S(1)} %get-tuple-element.67.refs_3_), channel_id=1, source_target_pairs={{24,16},{25,17},{26,18},{27,19},{28,20},{29,21},{30,22},{31,23}} | collective-permute-start | bytes 835592 | tf_op jit(solution)/shard_map/ppermute | solution.py:735
  14.5 1.3 %collective-permute-start.9 = (f32[544,128]{1,0:T(8,128)S(1)}, f32[544,128]{1,0:T(8,128)S(1)}, u32[]{:S(2)}, u32[]{:S(2)}) collective-permute-start(f32[544,128]{1,0:T(8,128)S(1)} %get-tuple-element.67.refs_3_), channel_id=1, source_target_pairs={{24,0},{25,1},{26,2},{27,3},{28,4},{29,5},{30,6},{31,7}} | collective-permute-start | bytes 835592 | tf_op jit(solution)/shard_map/ppermute | solution.py:735
  15.9 0.0 collective-permute-done.2.low_ref
  15.9 0.7 %collective-permute-start.4 = (f32[2,256]{1,0:T(2,128)S(1)}, f32[2,256]{1,0:T(2,128)S(1)}, u32[]{:S(2)}, u32[]{:S(2)}) collective-permute-start(f32[2,256]{1,0:T(2,128)S(1)} %get-tuple-element.40), channel_id=1, source_target_pairs={{1,8},{2,9},{3,10},{4,11},{5,12},{6,13},{7,14}} | collective-permute-start | bytes 6152 | tf_op jit(solution)/shard_map/ppermute | solution.py:745
  16.6 0.0 collective-permute-done.3.own_ref
  16.6 0.7 %collective-permute-start.8 = (f32[16,128]{1,0:T(8,128)S(1)}, f32[16,128]{1,0:T(8,128)S(1)}, u32[]{:S(2)}, u32[]{:S(2)}) collective-permute-start(f32[16,128]{1,0:T(8,128)S(1)} %tile.1.refs_3_), channel_id=1, source_target_pairs={{24,25},{25,24},{26,27},{27,26},{28,29},{29,28},{30,31},{31,30}} | collective-permute-start | bytes 24584 | tf_op jit(solution)/shard_map/ppermute | solution.py:780
  17.3 0.0 collective-permute-done.4.high_ref
  17.3 0.7 %collective-permute-start.5 = (f32[2,256]{1,0:T(2,128)S(1)}, f32[2,256]{1,0:T(2,128)S(1)}, u32[]{:S(2)}, u32[]{:S(2)}) collective-permute-start(f32[2,256]{1,0:T(2,128)S(1)} %get-tuple-element.53), channel_id=1, source_target_pairs={{8,17},{9,18},{10,19},{11,20},{12,21},{13,22},{14,23}} | collective-permute-start | bytes 6152 | tf_op jit(solution)/shard_map/ppermute | solution.py:745
  18.0 0.0 collective-permute-done.5.low_ref
  18.0 0.7 %collective-permute-start.6 = (f32[2,256]{1,0:T(2,128)S(1)}, f32[2,256]{1,0:T(2,128)S(1)}, u32[]{:S(2)}, u32[]{:S(2)}) collective-permute-start(f32[2,256]{1,0:T(2,128)S(1)} %get-tuple-element.53), channel_id=1, source_target_pairs={{8,16},{9,17},{10,18},{11,19},{12,20},{13,21},{14,22},{15,23}} | collective-permute-start | bytes 6152 | tf_op jit(solution)/shard_map/ppermute | solution.py:745
  18.6 0.0 collective-permute-done.6.own_ref
  18.7 0.7 %collective-permute-start.7 = (f32[2,256]{1,0:T(2,128)S(1)}, f32[2,256]{1,0:T(2,128)S(1)}, u32[]{:S(2)}, u32[]{:S(2)}) collective-permute-start(f32[2,256]{1,0:T(2,128)S(1)} %get-tuple-element.53), channel_id=1, source_target_pairs={{9,16},{10,17},{11,18},{12,19},{13,20},{14,21},{15,22}} | collective-permute-start | bytes 6152 | tf_op jit(solution)/shard_map/ppermute | solution.py:745
  19.3 0.0 collective-permute-done.7.high_ref
  19.3 0.0 collective-permute-done.8.refs_4_
  19.3 0.5 shard_map.53
  19.8 0.0 collective-permute-done.10.refs_1_
  19.8 0.0 collective-permute-done.11.refs_2_
  19.9 7.0 %collective-permute-done.9.refs_0_ = f32[544,128]{1,0:T(8,128)S(1)} collective-permute-done((f32[544,128]{1,0:T(8,128)S(1)}, f32[544,128]{1,0:T(8,128)S(1)}, u32[]{:S(2)}, u32[]{:S(2)}) %collective-permute-start.9) | collective-permute-done | bytes 278560 | tf_op jit(solution)/shard_map/ppermute | solution.py:735
  26.8 28.4 %all_to_all.5.got_ref = f32[32,8,128]{2,1,0:T(8,128)S(1)} all-to-all(f32[32,8,128]{2,1,0:T(8,128)S(1)} %get-tuple-element.61), channel_id=1, replica_groups=mesh['section'=4,'pix'=8] {'section','pix'}, dimensions={0} | all-to-all | bytes 262144 | tf_op jit(solution)/shard_map/all_to_all | solution.py:783
  55.3 3.0 %finish.1 = (f32[50,2,256]{2,1,0:T(2,128)}, f32[2,1,256]{2,1,0:T(1,128)}) custom-call(s32[8,128]{1,0:T(8,128)S(1)} %broadcast_in_dim.3.pixel_ref.refs_0_, s32[15,256]{1,0:T(8,128)S(1)} %get-tuple-element.36.idx_ref, f32[32,8,128]{2,1,0:T(8,128)S(1)} %all_to_all.5.got_ref, f32[2,50,256]{2,1,0:T(8,128)S(1)} %get-tuple-element.62.vec0_ref, ...), custom_call_target="tpu_custom_call" | custom-call | tf_op jit(solution)/shard_map/finish/pallas_call | solution.py:784
  (4 shorter events, 0.1 us)
Async XLA Ops:
  0.6 1.9 %collective-permute-start = (f32[50,2,256]{2,1,0:T(2,128)}, f32[50,2,256]{2,1,0:T(2,128)S(1)}, u32[]{:S(2)}, u32[]{:S(2)}) collective-permute-start(f32[50,2,256]{2,1,0:T(2,128)} %bitcast.4), channel_id=1, source_target_pairs={{0,1},{2,3},{4,5},{6,7},{1,0},{3,2},{5,4},{7,6},{8,9},{10,11},{12,... | collective-permute-start | bytes 307208 | tf_op jit(solution)/shard_map/ppermute | solution.py:683
  1.2 3.4 %collective-permute-start.1 = (f32[50,2,256]{2,1,0:T(2,128)}, f32[50,2,256]{2,1,0:T(2,128)S(1)}, u32[]{:S(2)}, u32[]{:S(2)}) collective-permute-start(f32[50,2,256]{2,1,0:T(2,128)} %bitcast.5), channel_id=1, source_target_pairs={{1,2},{3,4},{5,6},{2,1},{4,3},{6,5},{9,10},{11,12},{13,14},{10,9},... | collective-permute-start | bytes 307208 | tf_op jit(solution)/shard_map/ppermute | solution.py:683
  9.2 6.6 %collective-permute-start.2 = (f32[2,256]{1,0:T(2,128)S(1)}, f32[2,256]{1,0:T(2,128)S(1)}, u32[]{:S(2)}, u32[]{:S(2)}) collective-permute-start(f32[2,256]{1,0:T(2,128)S(1)} %get-tuple-element.40), channel_id=1, source_target_pairs={{0,9},{1,10},{2,11},{3,12},{4,13},{5,14},{6,15}} | collective-permute-start | bytes 6152 | tf_op jit(solution)/shard_map/ppermute | solution.py:745
  11.9 4.7 %collective-permute-start.3 = (f32[2,256]{1,0:T(2,128)S(1)}, f32[2,256]{1,0:T(2,128)S(1)}, u32[]{:S(2)}, u32[]{:S(2)}) collective-permute-start(f32[2,256]{1,0:T(2,128)S(1)} %get-tuple-element.40), channel_id=1, source_target_pairs={{0,8},{1,9},{2,10},{3,11},{4,12},{5,13},{6,14},{7,15}} | collective-permute-start | bytes 6152 | tf_op jit(solution)/shard_map/ppermute | solution.py:745
  13.2 6.7 %collective-permute-start.10 = (f32[544,128]{1,0:T(8,128)S(1)}, f32[544,128]{1,0:T(8,128)S(1)}, u32[]{:S(2)}, u32[]{:S(2)}) collective-permute-start(f32[544,128]{1,0:T(8,128)S(1)} %get-tuple-element.67.refs_3_), channel_id=1, source_target_pairs={{24,8},{25,9},{26,10},{27,11},{28,12},{29,13},{30,14},{31,15}} | collective-permute-start | bytes 835592 | tf_op jit(solution)/shard_map/ppermute | solution.py:735
  13.8 6.0 %collective-permute-start.11 = (f32[544,128]{1,0:T(8,128)S(1)}, f32[544,128]{1,0:T(8,128)S(1)}, u32[]{:S(2)}, u32[]{:S(2)}) collective-permute-start(f32[544,128]{1,0:T(8,128)S(1)} %get-tuple-element.67.refs_3_), channel_id=1, source_target_pairs={{24,16},{25,17},{26,18},{27,19},{28,20},{29,21},{30,22},{31,23}} | collective-permute-start | bytes 835592 | tf_op jit(solution)/shard_map/ppermute | solution.py:735
  14.5 12.3 %collective-permute-start.9 = (f32[544,128]{1,0:T(8,128)S(1)}, f32[544,128]{1,0:T(8,128)S(1)}, u32[]{:S(2)}, u32[]{:S(2)}) collective-permute-start(f32[544,128]{1,0:T(8,128)S(1)} %get-tuple-element.67.refs_3_), channel_id=1, source_target_pairs={{24,0},{25,1},{26,2},{27,3},{28,4},{29,5},{30,6},{31,7}} | collective-permute-start | bytes 835592 | tf_op jit(solution)/shard_map/ppermute | solution.py:735
  15.9 1.4 %collective-permute-start.4 = (f32[2,256]{1,0:T(2,128)S(1)}, f32[2,256]{1,0:T(2,128)S(1)}, u32[]{:S(2)}, u32[]{:S(2)}) collective-permute-start(f32[2,256]{1,0:T(2,128)S(1)} %get-tuple-element.40), channel_id=1, source_target_pairs={{1,8},{2,9},{3,10},{4,11},{5,12},{6,13},{7,14}} | collective-permute-start | bytes 6152 | tf_op jit(solution)/shard_map/ppermute | solution.py:745
  16.6 2.7 %collective-permute-start.8 = (f32[16,128]{1,0:T(8,128)S(1)}, f32[16,128]{1,0:T(8,128)S(1)}, u32[]{:S(2)}, u32[]{:S(2)}) collective-permute-start(f32[16,128]{1,0:T(8,128)S(1)} %tile.1.refs_3_), channel_id=1, source_target_pairs={{24,25},{25,24},{26,27},{27,26},{28,29},{29,28},{30,31},{31,30}} | collective-permute-start | bytes 24584 | tf_op jit(solution)/shard_map/ppermute | solution.py:780
  17.3 0.7 %collective-permute-start.5 = (f32[2,256]{1,0:T(2,128)S(1)}, f32[2,256]{1,0:T(2,128)S(1)}, u32[]{:S(2)}, u32[]{:S(2)}) collective-permute-start(f32[2,256]{1,0:T(2,128)S(1)} %get-tuple-element.53), channel_id=1, source_target_pairs={{8,17},{9,18},{10,19},{11,20},{12,21},{13,22},{14,23}} | collective-permute-start | bytes 6152 | tf_op jit(solution)/shard_map/ppermute | solution.py:745
  18.0 0.7 %collective-permute-start.6 = (f32[2,256]{1,0:T(2,128)S(1)}, f32[2,256]{1,0:T(2,128)S(1)}, u32[]{:S(2)}, u32[]{:S(2)}) collective-permute-start(f32[2,256]{1,0:T(2,128)S(1)} %get-tuple-element.53), channel_id=1, source_target_pairs={{8,16},{9,17},{10,18},{11,19},{12,20},{13,21},{14,22},{15,23}} | collective-permute-start | bytes 6152 | tf_op jit(solution)/shard_map/ppermute | solution.py:745
  18.7 0.7 %collective-permute-start.7 = (f32[2,256]{1,0:T(2,128)S(1)}, f32[2,256]{1,0:T(2,128)S(1)}, u32[]{:S(2)}, u32[]{:S(2)}) collective-permute-start(f32[2,256]{1,0:T(2,128)S(1)} %get-tuple-element.53), channel_id=1, source_target_pairs={{9,16},{10,17},{11,18},{12,19},{13,20},{14,21},{15,22}} | collective-permute-start | bytes 6152 | tf_op jit(solution)/shard_map/ppermute | solution.py:745
